TPU v7x, 256 devices: a whole 4x4x8 slice. The times are simulated.
256 devices in a mesh: dom: 256 (over z, x, y, core).
Axes of the slice: x: 4, y: 4, z: 8, core: 2. Of those that a mesh axis runs over, the one named last changes fastest.
Arguments:
- entities: float32 [262144, 200], P('dom'), may hold values from -3 to 3
- entity_state: float32 [262144], P('dom'), may hold values from 1e-05 to 0.1
- relations: float32 [1345, 200], replicated, may hold values from -3 to 3
- relation_state: float32 [1345], replicated, may hold values from 1 to 100
- edges: int32 [2, 3, 131072], P(None, None, 'dom'), may hold values from 0 to 1344, as said below
- negatives: int32 [2, 1024, 1000], P(None, 'dom'), may hold values from 0 to 1023
- counts: int32 [2, 256], P(None, 'dom'), may hold values from 1 to 512, as said below
Outputs:
- entities_after: float32 [262144, 200], P('dom')
- entity_state_after: float32 [262144], P('dom')
- relations_after: float32 [1345, 200], replicated
- relation_state_after: float32 [1345], replicated
Inputs may be any that keep to these rules, and one draw needn't show every extreme that they name: `edges`: rows 0 and 2 are local entity ids below 1024; row 1 holds relation ids below 1345. `negatives`: local ids in the partner's partition. `counts`: in every round some bucket is full.
All inputs are finite; a program needn't handle non-finite values.
Results may differ from a plain program's by a relative error of at most 0.0003.
Values sent between devices are 32-bit elements; how exact they have to be, the bound alone decides.
No kernel may reach another device: no remote copies, remote signals or barrier semaphores. Data moves between devices by JAX's collectives and lax.ppermute only.
A program may use at most 64 MiB of HBM per device.

v0:
```python
import jax
import jax.numpy as jnp
from jax import lax
from jax.experimental import pallas as pl
from jax.experimental.pallas import tpu as pltpu
from jax.sharding import Mesh
from jax.sharding import PartitionSpec as P

Z, X, Y, C = "z", "x", "y", "c"
DOM = (Z, X, Y, C)
F32 = jnp.float32
BF16 = jnp.bfloat16
RATE = 0.2

ROWS = 1024
DIM = 200
HALF = DIM // 2
REL = 1345
RELP = 1408
NEG = 1000
BLOCK = 128
STEP = 256
EDGES = 512
LOAD = 216
ID_ROW = 200
HIST_ROW = 208
FLAT = 2304
SIDE = FLAT // 2

VMEM = pl.BlockSpec(memory_space=pltpu.VMEM)
SMEM = pl.BlockSpec(memory_space=pltpu.SMEM)


def shape(*dims, dtype=F32):
    return jax.ShapeDtypeStruct(dims, dtype)


def params():
    return pltpu.CompilerParams(vmem_limit_bytes=48 * 1024 * 1024)


def halves(value):
    high = value.astype(BF16)
    return high, (value - high.astype(F32)).astype(BF16)


def dot(a, b, dims=((1,), (0,))):
    return lax.dot_general(a, b, (dims, ((), ())), preferred_element_type=F32)


NT = ((1,), (1,))


def dot3(a, b, dims=((1,), (0,))):
    return dot(a[0], b[0], dims) + (dot(a[1], b[0], dims) + dot(a[0], b[1], dims))


def one_hot(ids, count):
    places = lax.broadcasted_iota(jnp.int32, (count, ids.shape[1]), 0)
    return jnp.where(places == ids, 1.0, 0.0).astype(BF16)


def histogram(ids):
    upper = lax.broadcasted_iota(jnp.int32, (8, NEG), 0)
    lower = lax.broadcasted_iota(jnp.int32, (128, NEG), 0)
    high = jnp.where(upper == (ids >> 7), 1.0, 0.0).astype(BF16)
    low = jnp.where(lower == (ids & 127), 1.0, 0.0).astype(BF16)
    return dot(high, low, NT)


def live_sources(edges_ref, count, which):
    places = lax.broadcasted_iota(jnp.int32, (1, EDGES), 1)
    return jnp.where(places < count, edges_ref[which, 0:1, :], -1)


def write_payload(out_refs, parts, edges_ref, negatives_ref, count, which):
    source = live_sources(edges_ref, count, which)
    pick = one_hot(source, ROWS)
    high, low = parts
    rows = dot(high, pick) + dot(low, pick)
    wide = EDGES // len(out_refs)
    for number, ref in enumerate(out_refs):
        span = slice(number * wide, (number + 1) * wide)
        ref[0:DIM, :] = rows[:, span]
        ref[ID_ROW : ID_ROW + 1, :] = edges_ref[which, 1:2, span].astype(F32)
        ref[ID_ROW + 1 : ID_ROW + 2, :] = edges_ref[which, 2:3, span].astype(F32)
        ref[ID_ROW + 2 : HIST_ROW, :] = jnp.zeros((HIST_ROW - ID_ROW - 2, wide), F32)
        for block in range(wide // BLOCK):
            k = number * (wide // BLOCK) + block
            ref[HIST_ROW:LOAD, block * BLOCK : (block + 1) * BLOCK] = histogram(
                negatives_ref[which, k : k + 1, :]
            )


def prepare(counts_ref, table_ref, edges_ref, negatives_ref, high_out, low_out, first, second):
    parts = halves(table_ref[...])
    high_out[...], low_out[...] = parts
    write_payload((first, second), parts, edges_ref, negatives_ref, counts_ref[0, 0], 0)


def pad_relations(rel_ref, state_ref, rel_out, state_out, high_out, low_out):
    rel_out[:, 10 * 128 : RELP] = jnp.zeros((DIM, RELP - 10 * 128), F32)
    rel_out[:, 0:REL] = rel_ref[...]
    high_out[...], low_out[...] = halves(rel_out[...])
    state_out[...] = jnp.ones((1, RELP), F32)
    state_out[:, 0:REL] = state_ref[...]


def multiply(a_re, a_im, b_re, b_im, conjugate, out, lanes):
    if conjugate:
        out[0:HALF, lanes] = a_re * b_re + a_im * b_im
        out[HALF:DIM, lanes] = a_im * b_re - a_re * b_im
    else:
        out[0:HALF, lanes] = a_re * b_re - a_im * b_im
        out[HALF:DIM, lanes] = a_re * b_im + a_im * b_re


def weights(scores, times, target, first_lane):
    small = jnp.exp(-jnp.abs(scores))
    large = 1.0 / (1.0 + small)
    small = small * large
    up = scores >= 0.0
    plus = jnp.where(up, large, small)
    minus = jnp.where(up, small, large)
    lanes = lax.broadcasted_iota(jnp.int32, (1, 128), 1) + first_lane
    return plus * times - jnp.where(lanes == target, minus, 0.0)


def edge_terms(load_ref, table_parts, rel_parts, work, sg_out, first, carried):
    w_ref, q_ref, score_ref, high_ref, low_ref, back_ref, rg_ref = work
    wide = load_ref.shape[1]
    pick = one_hot(load_ref[ID_ROW : ID_ROW + 1, :].astype(jnp.int32), RELP)
    w_ref[...] = dot(rel_parts[0], pick) + dot(rel_parts[1], pick)
    s_re, s_im = load_ref[0:HALF, :], load_ref[HALF:DIM, :]
    w_re, w_im = w_ref[0:HALF, :], w_ref[HALF:DIM, :]
    multiply(s_re, s_im, w_re, w_im, False, q_ref, slice(None))
    product = q_ref[...]
    product_parts = halves(product)
    target = load_ref[ID_ROW : ID_ROW + 8, :].T[:, 1:2].astype(jnp.int32)
    turned = halves(product.T)
    for start in range(0, wide, STEP):
        edges = slice(start, start + STEP)
        score_ref[edges, :] = dot3((turned[0][edges], turned[1][edges]), table_parts)
    table_grad = None
    for start in range(0, wide, STEP):
        for block in range(start, start + STEP, BLOCK):
            edges = slice(block, block + BLOCK)
            for tile in range(ROWS // 128):
                lanes = slice(tile * 128, (tile + 1) * 128)
                times = load_ref[HIST_ROW + tile : HIST_ROW + tile + 1, edges] * (1.0 / NEG)
                value = weights(score_ref[edges, lanes], times, target[edges], tile * 128)
                high_ref[edges, lanes], low_ref[edges, lanes] = halves(value)
        edges = slice(start, start + STEP)
        weight_parts = high_ref[edges, :], low_ref[edges, :]
        back_ref[:, edges] = dot3(table_parts, weight_parts, NT)
        part = dot3((product_parts[0][:, edges], product_parts[1][:, edges]), weight_parts)
        table_grad = part if table_grad is None else table_grad + part
    if carried is not None:
        table_grad = table_grad + carried[0][...]
    up_re, up_im = back_ref[0:HALF, :], back_ref[HALF:DIM, :]
    multiply(up_re, up_im, s_re, s_im, True, rg_ref, slice(None))
    multiply(up_re, up_im, w_re, w_im, True, sg_out, slice(first, first + wide))
    rg_high, rg_low = halves(rg_ref[...])
    grad = dot(rg_high, pick, NT) + dot(rg_low, pick, NT)
    return table_grad, grad if carried is None else grad + carried[1][...]


def split_flat(core, grad, flat, send_out, keep_out):
    for tile in range(RELP // 128):
        flat[tile * DIM : (tile + 1) * DIM, :] = grad[:, tile * 128 : (tile + 1) * 128]
    flat[RELP // 128 * DIM : FLAT, :] = jnp.zeros((FLAT - RELP // 128 * DIM, 128), F32)
    keep_out[...] = flat[pl.ds(pl.multiple_of(core * SIDE, SIDE), SIDE), :]
    send_out[...] = flat[pl.ds(pl.multiple_of((1 - core) * SIDE, SIDE), SIDE), :]


def join_flat(core, mine_ref, other_ref, flat):
    flat[pl.ds(pl.multiple_of(core * SIDE, SIDE), SIDE), :] = mine_ref[...]
    flat[pl.ds(pl.multiple_of((1 - core) * SIDE, SIDE), SIDE), :] = other_ref[...]


def adagrad(table, state, grad):
    state = state + jnp.sum(grad * grad, axis=0, keepdims=True) * (1.0 / DIM)
    return table - grad * (RATE / jnp.sqrt(state)), state


def first_piece(
    load_ref, high_ref, low_ref, rel_high, rel_low, sg_out, table_grad, rel_grad, *work
):
    table_parts, rel_parts = (high_ref[...], low_ref[...]), (rel_high[...], rel_low[...])
    table_grad[...], rel_grad[...] = edge_terms(
        load_ref, table_parts, rel_parts, work, sg_out, 0, None
    )


def second_piece(
    core_ref,
    load_ref,
    high_ref,
    low_ref,
    rel_high,
    rel_low,
    sg_ref,
    g_ref,
    h_ref,
    sg_out,
    table_grad,
    send,
    keep,
    *work,
):
    table_parts, rel_parts = (high_ref[...], low_ref[...]), (rel_high[...], rel_low[...])
    first = sg_ref.shape[1]
    sg_out[:, 0:first] = sg_ref[...]
    table_grad[...], grad = edge_terms(
        load_ref, table_parts, rel_parts, work[:-1], sg_out, first, (g_ref, h_ref)
    )
    split_flat(core_ref[0], grad, work[-1], send, keep)


def step_relations(core, mine_ref, other_ref, rel_ref, state_ref, flat, rel_out, state_out):
    join_flat(core, mine_ref, other_ref, flat)
    for tile in range(RELP // 128):
        lanes = slice(tile * 128, (tile + 1) * 128)
        rel_out[:, lanes], state_out[:, lanes] = adagrad(
            rel_ref[:, lanes], state_ref[:, lanes], flat[tile * DIM : (tile + 1) * DIM, :]
        )


def second_round(
    core_ref,
    mine_ref,
    other_ref,
    rel_ref,
    state_ref,
    load_ref,
    high_ref,
    low_ref,
    sg_out,
    table_grad,
    send,
    keep,
    rel_out,
    state_out,
    *work,
):
    core, flat = core_ref[0], work[-1]
    step_relations(core, mine_ref, other_ref, rel_ref, state_ref, flat, rel_out, state_out)
    table_grad[...], grad = edge_terms(
        load_ref,
        (high_ref[...], low_ref[...]),
        halves(rel_out[...]),
        work[:-1],
        sg_out,
        0,
        None,
    )
    split_flat(core, grad, flat, send, keep)


def step_entities(table_ref, state_ref, grad_ref, back_ref, edges_ref, count, which):
    pick = one_hot(live_sources(edges_ref, count, which), ROWS)
    high, low = halves(back_ref[...])
    grad = grad_ref[...] + (dot(high, pick, NT) + dot(low, pick, NT))
    return adagrad(table_ref[...], state_ref[...], grad)


def between(
    counts_ref,
    table_ref,
    state_ref,
    grad_ref,
    back_ref,
    edges_ref,
    negatives_ref,
    table_out,
    state_out,
    high_out,
    low_out,
    load,
):
    table, state_out[...] = step_entities(
        table_ref, state_ref, grad_ref, back_ref, edges_ref, counts_ref[0, 0], 0
    )
    table_out[...] = table
    parts = halves(table)
    high_out[...], low_out[...] = parts
    write_payload((load,), parts, edges_ref, negatives_ref, counts_ref[1, 0], 1)


def last_entities(
    counts_ref, table_ref, state_ref, grad_ref, back_ref, edges_ref, table_out, state_out
):
    table_out[...], state_out[...] = step_entities(
        table_ref, state_ref, grad_ref, back_ref, edges_ref, counts_ref[1, 0], 1
    )


def last_relations(
    core_ref, mine_ref, other_ref, rel_ref, state_ref, rel_out, state_out, flat, rel, state
):
    step_relations(core_ref[0], mine_ref, other_ref, rel_ref, state_ref, flat, rel, state)
    rel_out[...] = rel[:, 0:REL]
    state_out[...] = state[:, 0:REL]


def work_shapes(wide):
    return [
        pltpu.VMEM((DIM, wide), F32),
        pltpu.VMEM((DIM, wide), F32),
        pltpu.VMEM((wide, ROWS), F32),
        pltpu.VMEM((wide, ROWS), BF16),
        pltpu.VMEM((wide, ROWS), BF16),
        pltpu.VMEM((DIM, wide), F32),
        pltpu.VMEM((DIM, wide), F32),
    ]


def call(body, ins, outs, operands, scratch=(), flops=0):
    specs = [SMEM if kind else VMEM for kind in ins]
    return pl.pallas_call(
        body,
        out_shape=outs,
        in_specs=specs,
        out_specs=[VMEM] * len(outs),
        scratch_shapes=list(scratch),
        compiler_params=params(),
        cost_estimate=pl.CostEstimate(flops=flops, bytes_accessed=0, transcendentals=0),
    )(*operands)


def across(value, axis, apart):
    count = lax.axis_size(axis)
    return lax.ppermute(value, axis, [(i, i ^ apart) for i in range(count)])


def total(send, keep):
    part = (keep + across(send, C, 1)).reshape(16, SIDE // 16, 128)
    part = lax.all_to_all(part, (X, Y), 0, 0, tiled=True).sum(axis=0)
    part = jnp.broadcast_to(part[None], (8, *part.shape))
    part = lax.all_to_all(part, Z, 0, 0, tiled=True).sum(axis=0)
    part = jnp.broadcast_to(part[None], (16, *part.shape))
    part = lax.all_to_all(part, (X, Y), 0, 0, tiled=True)
    mine = part.reshape(SIDE, 128)
    return mine, across(mine, C, 1)


def body(entities, entity_state, relations, relation_state, edges, negatives, counts):
    core = lax.axis_index(C).astype(jnp.int32).reshape(1)
    table, rel = entities.T, relations.T
    state = entity_state.reshape(1, ROWS)
    piece = shape(LOAD, EDGES // 2)
    narrow = shape(DIM, ROWS, dtype=BF16)
    high, low, first, second = call(
        prepare,
        (1, 0, 0, 0),
        [narrow, narrow, piece, piece],
        (counts, table, edges, negatives),
    )
    first = across(first, Z, 4)
    second = across(second, Z, 4)
    wide_rel = shape(DIM, RELP, dtype=BF16)
    rel, rel_state, rel_high, rel_low = call(
        pad_relations,
        (0, 0),
        [shape(DIM, RELP), shape(1, RELP), wide_rel, wide_rel],
        (rel, relation_state.reshape(1, REL)),
    )
    back, grad, rel_grad = call(
        first_piece,
        (0, 0, 0, 0, 0),
        [shape(DIM, EDGES // 2), shape(DIM, ROWS), shape(DIM, RELP)],
        (first, high, low, rel_high, rel_low),
        work_shapes(EDGES // 2),
    )
    back, grad, send, keep = call(
        second_piece,
        (1, 0, 0, 0, 0, 0, 0, 0, 0),
        [shape(DIM, EDGES), shape(DIM, ROWS), shape(SIDE, 128), shape(SIDE, 128)],
        (core, second, high, low, rel_high, rel_low, back, grad, rel_grad),
        work_shapes(EDGES // 2) + [pltpu.VMEM((FLAT, 128), F32)],
    )
    back = across(back, Z, 4)
    mine, other = total(send, keep)
    table, state, high, low, load = call(
        between,
        (1, 0, 0, 0, 0, 0, 0),
        [shape(DIM, ROWS), shape(1, ROWS), narrow, narrow, shape(LOAD, EDGES)],
        (counts, table, state, grad, back, edges, negatives),
    )
    load = across(load, C, 1)
    back, grad, send, keep, rel, rel_state = call(
        second_round,
        (1, 0, 0, 0, 0, 0, 0, 0),
        [
            shape(DIM, EDGES),
            shape(DIM, ROWS),
            shape(SIDE, 128),
            shape(SIDE, 128),
            shape(DIM, RELP),
            shape(1, RELP),
        ],
        (core, mine, other, rel, rel_state, load, high, low),
        work_shapes(EDGES) + [pltpu.VMEM((FLAT, 128), F32)],
    )
    back = across(back, C, 1)
    mine, other = total(send, keep)
    table, state = call(
        last_entities,
        (1, 0, 0, 0, 0, 0),
        [shape(DIM, ROWS), shape(1, ROWS)],
        (counts, table, state, grad, back, edges),
    )
    rel, rel_state = call(
        last_relations,
        (1, 0, 0, 0, 0),
        [shape(DIM, REL), shape(1, REL)],
        (core, mine, other, rel, rel_state),
        [pltpu.VMEM((FLAT, 128), F32), pltpu.VMEM((DIM, RELP), F32), pltpu.VMEM((1, RELP), F32)],
    )
    return table.T, state.reshape(ROWS), rel.T, rel_state.reshape(REL)


def solution(mesh):
    finer = Mesh(mesh.devices.reshape(8, 4, 4, 2), DOM)
    return jax.shard_map(
        body,
        mesh=finer,
        in_specs=(
            P(DOM, None),
            P(DOM),
            P(),
            P(),
            P(None, None, DOM),
            P(None, DOM, None),
            P(None, DOM),
        ),
        out_specs=(P(DOM, None), P(DOM), P(), P()),
        check_vma=False,
    )
```

profile of v0, /device:TPU:1, one launch (start us, length us, event | category | flops | bytes accessed | tf_op | source)
XLA Modules:
  0.0 176.4 jit_solution(4337345811035663823)
XLA Ops:
  0.6 0.7 copy.21.counts_ref
  1.4 0.7 copy.18.edges_ref
  2.1 0.0 copy-start
  2.1 1.1 copy-done
  3.2 0.0 copy-start.7
  3.2 0.8 copy-done.7
  4.0 1.6 shard_map.102
  5.6 7.7 %collective-permute-start.1 = (f32[216,256]{1,0:T(8,128)S(1)}, f32[216,256]{1,0:T(8,128)S(1)}, u32[]{:S(2)}, u32[]{:S(2)}) collective-permute-start(f32[216,256]{1,0:T(8,128)S(1)} %get-tuple-element.39), channel_id=1, source_target_pairs={{0,128},{32,160},{64,192},{96,224},{128,0},{160,32},{192,64},{224,... | collective-permute-start | bytes 663560 | tf_op jit(solution)/shard_map/ppermute | solution.py:333
  13.4 0.1 collective-permute-start
  13.4 0.7 reshape.41.state_ref
  14.1 0.0 copy-start.2
  14.1 1.2 copy-done.2
  15.4 0.4 shard_map.103
  15.8 0.0 copy-start.3
  15.8 1.0 copy-done.3
  16.8 1.2 collective-permute-done.1.load_ref
  18.0 3.6 %shard_map.104 = (f32[200,256]{1,0:T(8,128)S(1)}, f32[200,1024]{1,0:T(8,128)S(1)}, f32[200,1408]{1,0:T(8,128)S(1)}) custom-call(f32[216,256]{1,0:T(8,128)S(1)} %collective-permute-done.1.load_ref, bf16[200,1024]{1,0:T(8,128)(2,1)S(1)} %get-tuple-element.35.high_ref, bf16[200,1024]{1,0:T(8,128)(2,1)S(1)} %get-tuple-element.36.low_ref, ...), custom_call_target="tpu_custom_call" | custom-call | tf_op jit(solution)/shard_map/pallas_call | solution.py:320
  21.7 0.0 copy-start.4
  21.7 1.0 copy-done.4
  22.7 1.4 collective-permute-done.load_ref
  24.1 5.0 %shard_map.105 = (f32[200,512]{1,0:T(8,128)S(1)}, f32[200,1024]{1,0:T(8,128)S(1)}, f32[1152,128]{1,0:T(8,128)S(1)}, f32[1152,128]{1,0:T(8,128)S(1)}) custom-call(s32[1]{0:T(128)} %bitcast.2.core_ref, f32[216,256]{1,0:T(8,128)S(1)} %collective-permute-done.load_ref, bf16[200,1024]{1,0:T(8,128)(2,1)S(1)} %get-tuple-element.35.high_ref, ...), custom_call_target="tpu_custom_call" | custom-call | tf_op jit(solution)/shard_map/pallas_call | solution.py:320
  29.1 2.8 %collective-permute-start.3 = (f32[1152,128]{1,0:T(8,128)S(1)}, f32[1152,128]{1,0:T(8,128)S(1)}, u32[]{:S(2)}, u32[]{:S(2)}) collective-permute-start(f32[1152,128]{1,0:T(8,128)S(1)} %get-tuple-element.48), channel_id=1, source_target_pairs={{0,1},{1,0},{2,3},{3,2},{4,5},{5,4},{6,7},{7,6},{8,9},{9,8},{10,11... | collective-permute-start | bytes 1769480 | tf_op jit(solution)/shard_map/ppermute | solution.py:333
  31.8 1.6 collective-permute-done.3
  33.5 0.1 add.6
  33.5 18.1 %all_to_all.30 = f32[16,72,128]{2,1,0:T(8,128)S(1)} all-to-all(f32[16,72,128]{2,1,0:T(8,128)S(1)} %bitcast.19), channel_id=1, replica_groups=mesh['z'=8,'x'=4,'y'=4,'c'=2] {'x','y'}, dimensions={0} | all-to-all | bytes 1179648 | tf_op jit(solution)/shard_map/all_to_all | solution.py:338
  51.6 23.4 %all_to_all.31 = f32[8,72,128]{2,1,0:T(8,128)S(1)} all-to-all(f32[8,72,128]{2,1,0:T(8,128)S(1)} %broadcast_in_dim.8), channel_id=1, replica_groups=mesh['z'=8,'x'=4,'y'=4,'c'=2] {'z'}, dimensions={0} | all-to-all | bytes 589824 | tf_op jit(solution)/shard_map/all_to_all | solution.py:340
  75.1 0.0 copy-start.1
  75.1 0.0 copy-start.8
  75.1 0.0 copy-start.9
  75.1 0.9 broadcast_in_dim.9
  75.9 3.8 %all-to-all-start.2 = ((f32[16,72,128]{2,1,0:T(8,128)}), f32[16,72,128]{2,1,0:T(8,128)S(1)}, u32[]{:S(2)}, u32[]{:S(2)}) async-start(f32[16,72,128]{2,1,0:T(8,128)} %broadcast_in_dim.9), calls=%async_computation.2 | async-start | bytes 1179648 | tf_op jit(solution)/shard_map/all_to_all | solution.py:342
  79.7 2.1 %collective-permute-start.2 = (f32[200,512]{1,0:T(8,128)S(1)}, f32[200,512]{1,0:T(8,128)S(1)}, u32[]{:S(2)}, u32[]{:S(2)}) collective-permute-start(f32[200,512]{1,0:T(8,128)S(1)} %get-tuple-element.44), channel_id=1, source_target_pairs={{0,128},{32,160},{64,192},{96,224},{128,0},{160,32},{192,64},{224,... | collective-permute-start | bytes 1228808 | tf_op jit(solution)/shard_map/ppermute | solution.py:333
  81.9 7.2 %all-to-all-done.2 = f32[16,72,128]{2,1,0:T(8,128)S(1)} async-done(((f32[16,72,128]{2,1,0:T(8,128)}), f32[16,72,128]{2,1,0:T(8,128)S(1)}, u32[]{:S(2)}, u32[]{:S(2)}) %all-to-all-start.2) | async-done | bytes 589856 | tf_op jit(solution)/shard_map/all_to_all | solution.py:342
  89.1 4.6 %collective-permute-start.4 = (f32[1152,128]{1,0:T(8,128)S(1)}, f32[1152,128]{1,0:T(8,128)S(1)}, u32[]{:S(2)}, u32[]{:S(2)}) collective-permute-start(f32[1152,128]{1,0:T(8,128)S(1)} %bitcast.13), channel_id=1, source_target_pairs={{0,1},{1,0},{2,3},{3,2},{4,5},{5,4},{6,7},{7,6},{8,9},{9,8},{10,11... | collective-permute-start | bytes 1769480 | tf_op jit(solution)/shard_map/ppermute | solution.py:333
  93.6 4.1 %collective-permute-done.2.back_ref = f32[200,512]{1,0:T(8,128)S(1)} collective-permute-done((f32[200,512]{1,0:T(8,128)S(1)}, f32[200,512]{1,0:T(8,128)S(1)}, u32[]{:S(2)}, u32[]{:S(2)}) %collective-permute-start.2) | collective-permute-done | bytes 409632 | tf_op jit(solution)/shard_map/ppermute | solution.py:333
  97.8 0.0 copy-start.5
  97.8 0.7 copy-done.5
  98.5 0.0 copy-done.1
  98.5 0.0 copy-done.8
  98.5 0.0 copy-done.9
  98.5 1.0 copy-done.6
  99.5 2.5 %shard_map.106 = (f32[200,1024]{1,0:T(8,128)S(1)}, f32[1,1024]{1,0:T(1,128)S(1)}, bf16[200,1024]{1,0:T(8,128)(2,1)S(1)}, bf16[200,1024]{1,0:T(8,128)(2,1)S(1)}, f32[216,512]{1,0:T(8,128)S(1)}) custom-call(s32[2,1]{1,0:T(2,128)S(1)} %copy.21.counts_ref, f32[200,1024]{1,0:T(8,128)S(1)} %bitcast.12, f32[1,1024]{1,0:T(1,128)S(1)} %bitcast.18, ...), custom_call_target="tpu_custom_call" | custom-call | tf_op jit(solution)/shard_map/pallas_call | solution.py:320
  102.1 5.8 %collective-permute-start.5 = (f32[216,512]{1,0:T(8,128)S(1)}, f32[216,512]{1,0:T(8,128)S(1)}, u32[]{:S(2)}, u32[]{:S(2)}) collective-permute-start(f32[216,512]{1,0:T(8,128)S(1)} %get-tuple-element.51), channel_id=1, source_target_pairs={{0,1},{1,0},{2,3},{3,2},{4,5},{5,4},{6,7},{7,6},{8,9},{9,8},{10,11... | collective-permute-start | bytes 1327112 | tf_op jit(solution)/shard_map/ppermute | solution.py:333
  107.8 1.4 collective-permute-done.5.load_ref
  109.2 0.0 collective-permute-done.4.other_ref
  109.2 7.6 %shard_map.107 = (f32[200,512]{1,0:T(8,128)S(1)}, f32[200,1024]{1,0:T(8,128)S(1)}, f32[1152,128]{1,0:T(8,128)S(1)}, f32[1152,128]{1,0:T(8,128)S(1)}, f32[200,1408]{1,0:T(8,128)S(1)}, /*index=5*/f32[1,1408]{1,0:T(1,128)S(1)}) custom-call(s32[1]{0:T(128)} %bitcast.2.core_ref, f32[1152,128]{1,0:T(8,128)S(1)} %bitcast.14, ...), custom_call_target="tpu_custom_call" | custom-call | tf_op jit(solution)/shard_map/pallas_call | solution.py:320
  116.8 0.0 copy-start.10
  116.8 0.5 collective-permute-start.7
  117.3 1.6 collective-permute-done.7
  118.9 0.1 add.7
  119.0 0.0 copy-done.10
  119.0 18.0 %all_to_all.32 = f32[16,72,128]{2,1,0:T(8,128)} all-to-all(f32[16,72,128]{2,1,0:T(8,128)S(1)} %bitcast.20), channel_id=1, replica_groups=mesh['z'=8,'x'=4,'y'=4,'c'=2] {'x','y'}, dimensions={0} | all-to-all | bytes 1179648 | tf_op jit(solution)/shard_map/all_to_all | solution.py:338
  137.0 1.1 reduce_sum.38
  138.1 13.8 %all_to_all.33 = f32[8,72,128]{2,1,0:T(8,128)S(1)} all-to-all(f32[8,72,128]{2,1,0:T(8,128)S(1)} %broadcast_in_dim.10), channel_id=1, replica_groups=mesh['z'=8,'x'=4,'y'=4,'c'=2] {'z'}, dimensions={0} | all-to-all | bytes 589824 | tf_op jit(solution)/shard_map/all_to_all | solution.py:340
  152.0 0.0 copy-start.11
  152.0 13.1 %all_to_all.34 = f32[16,72,128]{2,1,0:T(8,128)S(1)} all-to-all(f32[16,72,128]{2,1,0:T(8,128)S(1)} %broadcast_in_dim.11), channel_id=1, replica_groups=mesh['z'=8,'x'=4,'y'=4,'c'=2] {'x','y'}, dimensions={0} | all-to-all | bytes 1179648 | tf_op jit(solution)/shard_map/all_to_all | solution.py:342
  165.1 4.6 %collective-permute-start.8 = (f32[1152,128]{1,0:T(8,128)S(1)}, f32[1152,128]{1,0:T(8,128)S(1)}, u32[]{:S(2)}, u32[]{:S(2)}) collective-permute-start(f32[1152,128]{1,0:T(8,128)S(1)} %bitcast.15), channel_id=1, source_target_pairs={{0,1},{1,0},{2,3},{3,2},{4,5},{5,4},{6,7},{7,6},{8,9},{9,8},{10,11... | collective-permute-start | bytes 1769480 | tf_op jit(solution)/shard_map/ppermute | solution.py:333
  169.7 0.0 copy-done.11
  169.7 0.0 collective-permute-start.6
  169.7 2.2 %collective-permute-done.6.back_ref = f32[200,512]{1,0:T(8,128)S(1)} collective-permute-done((f32[200,512]{1,0:T(8,128)S(1)}, f32[200,512]{1,0:T(8,128)S(1)}, u32[]{:S(2)}, u32[]{:S(2)}) %collective-permute-start.6) | collective-permute-done | bytes 409632 | tf_op jit(solution)/shard_map/ppermute | solution.py:333
  171.9 2.5 %shard_map.108 = (f32[200,1024]{1,0:T(8,128)}, f32[1,1024]{1,0:T(1,128)}) custom-call(s32[2,1]{1,0:T(2,128)S(1)} %copy.21.counts_ref, f32[200,1024]{1,0:T(8,128)S(1)} %get-tuple-element.45.table_ref, f32[1,1024]{1,0:T(1,128)S(1)} %get-tuple-element.46.state_ref, f32[200,1024]{1,0:T(8,128)S(1)} %get-tuple-element.54.grad_ref, ...), custom_call_target="tpu_custom_call" | custom-call | tf_op jit(solution)/shard_map/pallas_call | solution.py:320
  174.5 0.0 collective-permute-done.8.other_ref
  174.5 1.3 shard_map.109
  175.8 0.6 reduce
  (7 shorter events, 0.2 us)
Async XLA Ops:
  2.1 1.1 copy-start
  3.2 0.8 copy-start.7
  5.6 12.4 %collective-permute-start.1 = (f32[216,256]{1,0:T(8,128)S(1)}, f32[216,256]{1,0:T(8,128)S(1)}, u32[]{:S(2)}, u32[]{:S(2)}) collective-permute-start(f32[216,256]{1,0:T(8,128)S(1)} %get-tuple-element.39), channel_id=1, source_target_pairs={{0,128},{32,160},{64,192},{96,224},{128,0},{160,32},{192,64},{224,... | collective-permute-start | bytes 663560 | tf_op jit(solution)/shard_map/ppermute | solution.py:333
  13.4 10.7 %collective-permute-start = (f32[216,256]{1,0:T(8,128)S(1)}, f32[216,256]{1,0:T(8,128)S(1)}, u32[]{:S(2)}, u32[]{:S(2)}) collective-permute-start(f32[216,256]{1,0:T(8,128)S(1)} %get-tuple-element.34), channel_id=1, source_target_pairs={{0,128},{32,160},{64,192},{96,224},{128,0},{160,32},{192,64},{224,... | collective-permute-start | bytes 663560 | tf_op jit(solution)/shard_map/ppermute | solution.py:333
  14.1 1.3 copy-start.2
  15.8 1.0 copy-start.3
  21.7 1.0 copy-start.4
  29.1 4.4 %collective-permute-start.3 = (f32[1152,128]{1,0:T(8,128)S(1)}, f32[1152,128]{1,0:T(8,128)S(1)}, u32[]{:S(2)}, u32[]{:S(2)}) collective-permute-start(f32[1152,128]{1,0:T(8,128)S(1)} %get-tuple-element.48), channel_id=1, source_target_pairs={{0,1},{1,0},{2,3},{3,2},{4,5},{5,4},{6,7},{7,6},{8,9},{9,8},{10,11... | collective-permute-start | bytes 1769480 | tf_op jit(solution)/shard_map/ppermute | solution.py:333
  75.1 23.5 %copy-start.1 = (f32[1024,200]{0,1:T(8,128)S(1)}, f32[1024,200]{0,1:T(8,128)}, u32[]{:S(2)}) copy-start(f32[1024,200]{0,1:T(8,128)} %param.7) | copy-start | bytes 2457604
  75.1 23.5 %copy-start.8 = (s32[2,4,1000]{2,1,0:T(4,128)S(1)}, s32[2,4,1000]{2,1,0:T(4,128)}, u32[]{:S(2)}) copy-start(s32[2,4,1000]{2,1,0:T(4,128)} %negatives_ref.3) | copy-start | bytes 96004
  75.1 23.5 %copy-start.9 = (f32[1024]{0:T(1024)S(1)}, f32[1024]{0:T(1024)}, u32[]{:S(2)}) copy-start(f32[1024]{0:T(1024)} %param.8) | copy-start | bytes 12292
  75.9 13.2 %all-to-all-start.2 = ((f32[16,72,128]{2,1,0:T(8,128)}), f32[16,72,128]{2,1,0:T(8,128)S(1)}, u32[]{:S(2)}, u32[]{:S(2)}) async-start(f32[16,72,128]{2,1,0:T(8,128)} %broadcast_in_dim.9), calls=%async_computation.2 | async-start | bytes 1179648 | tf_op jit(solution)/shard_map/all_to_all | solution.py:342
  79.7 18.1 %collective-permute-start.2 = (f32[200,512]{1,0:T(8,128)S(1)}, f32[200,512]{1,0:T(8,128)S(1)}, u32[]{:S(2)}, u32[]{:S(2)}) collective-permute-start(f32[200,512]{1,0:T(8,128)S(1)} %get-tuple-element.44), channel_id=1, source_target_pairs={{0,128},{32,160},{64,192},{96,224},{128,0},{160,32},{192,64},{224,... | collective-permute-start | bytes 1228808 | tf_op jit(solution)/shard_map/ppermute | solution.py:333
  89.1 20.2 %collective-permute-start.4 = (f32[1152,128]{1,0:T(8,128)S(1)}, f32[1152,128]{1,0:T(8,128)S(1)}, u32[]{:S(2)}, u32[]{:S(2)}) collective-permute-start(f32[1152,128]{1,0:T(8,128)S(1)} %bitcast.13), channel_id=1, source_target_pairs={{0,1},{1,0},{2,3},{3,2},{4,5},{5,4},{6,7},{7,6},{8,9},{9,8},{10,11... | collective-permute-start | bytes 1769480 | tf_op jit(solution)/shard_map/ppermute | solution.py:333
  97.8 0.8 copy-start.5
  98.5 1.0 copy-start.6
  102.1 7.2 %collective-permute-start.5 = (f32[216,512]{1,0:T(8,128)S(1)}, f32[216,512]{1,0:T(8,128)S(1)}, u32[]{:S(2)}, u32[]{:S(2)}) collective-permute-start(f32[216,512]{1,0:T(8,128)S(1)} %get-tuple-element.51), channel_id=1, source_target_pairs={{0,1},{1,0},{2,3},{3,2},{4,5},{5,4},{6,7},{7,6},{8,9},{9,8},{10,11... | collective-permute-start | bytes 1327112 | tf_op jit(solution)/shard_map/ppermute | solution.py:333
  116.8 2.2 %copy-start.10 = (f32[200,512]{1,0:T(8,128)}, f32[200,512]{1,0:T(8,128)S(1)}, u32[]{:S(2)}) copy-start(f32[200,512]{1,0:T(8,128)S(1)} %get-tuple-element.55) | copy-start | bytes 1228804
  116.8 2.1 %collective-permute-start.7 = (f32[1152,128]{1,0:T(8,128)S(1)}, f32[1152,128]{1,0:T(8,128)S(1)}, u32[]{:S(2)}, u32[]{:S(2)}) collective-permute-start(f32[1152,128]{1,0:T(8,128)S(1)} %get-tuple-element.59), channel_id=1, source_target_pairs={{0,1},{1,0},{2,3},{3,2},{4,5},{5,4},{6,7},{7,6},{8,9},{9,8},{10,11... | collective-permute-start | bytes 1769480 | tf_op jit(solution)/shard_map/ppermute | solution.py:333
  152.0 17.7 %copy-start.11 = (f32[200,512]{1,0:T(8,128)S(1)}, f32[200,512]{1,0:T(8,128)}, u32[]{:S(2)}) copy-start(f32[200,512]{1,0:T(8,128)} %copy-done.10) | copy-start | bytes 1228804
  165.1 9.4 %collective-permute-start.8 = (f32[1152,128]{1,0:T(8,128)S(1)}, f32[1152,128]{1,0:T(8,128)S(1)}, u32[]{:S(2)}, u32[]{:S(2)}) collective-permute-start(f32[1152,128]{1,0:T(8,128)S(1)} %bitcast.15), channel_id=1, source_target_pairs={{0,1},{1,0},{2,3},{3,2},{4,5},{5,4},{6,7},{7,6},{8,9},{9,8},{10,11... | collective-permute-start | bytes 1769480 | tf_op jit(solution)/shard_map/ppermute | solution.py:333
  169.7 2.2 %collective-permute-start.6 = (f32[200,512]{1,0:T(8,128)S(1)}, f32[200,512]{1,0:T(8,128)S(1)}, u32[]{:S(2)}, u32[]{:S(2)}) collective-permute-start(f32[200,512]{1,0:T(8,128)S(1)} %copy-done.11), channel_id=1, source_target_pairs={{0,1},{1,0},{2,3},{3,2},{4,5},{5,4},{6,7},{7,6},{8,9},{9,8},{10,11... | collective-permute-start | bytes 1228808 | tf_op jit(solution)/shard_map/ppermute | solution.py:333
where the time goes:
time: 177 us; the launch traced here: 176 us
  blocking collectives  86.4 us (49%)
  starting transfers between devices  31.9 us (18%)
  Pallas kernels  24.6 us (14%)
  waiting for transfers between devices  20.9 us (12%)
  local copies, waits for them, and re-layouts  10 us (6%)
  other arithmetic  1.92 us (1%)
    all_to_all x2, blocking collectives, total(): part = lax.all_to_all(part, Z, 0, 0, tiled=True).sum(axis=0)  37.2 us
    all_to_all x2, blocking collectives, total(): part = lax.all_to_all(part, (X, Y), 0, 0, tiled=True).sum(axis=0)  36.1 us
    ppermute x9, starting transfers between devices, across(): return lax.ppermute(value, axis, [(i, i ^ apart) for i in range(count)])  28.1 us
    pallas_call x8, Pallas kernels, call(): pl.pallas_call(body, out_shape=outs, in_specs=specs, out_specs=[VMEM] * l...  24.6 us
    ppermute x9, waiting for transfers between devices, across(): return lax.ppermute(value, axis, [(i, i ^ apart) for i in range(count)])  13.7 us
    all_to_all x1, blocking collectives, total(): part = lax.all_to_all(part, (X, Y), 0, 0, tiled=True)  13.1 us
    unnamed x26, local copies, waits for them, and re-layouts  8.37 us
    all_to_all x1, waiting for transfers between devices, total(): part = lax.all_to_all(part, (X, Y), 0, 0, tiled=True)  7.22 us
  transfers between devices with their start and end apart: 10, of which 8 were waited for; matrix products, arithmetic and copies ran while one was open for 0% of the time, Pallas kernels for 5%

commit v1 on v0

v1 whole, which is shorter than its diff:
```python
import jax
import jax.numpy as jnp
from jax import lax
from jax.experimental import pallas as pl
from jax.experimental.pallas import tpu as pltpu
from jax.sharding import Mesh
from jax.sharding import PartitionSpec as P

Z, X, Y, C = "z", "x", "y", "c"
DOM = (Z, X, Y, C)
F32 = jnp.float32
BF16 = jnp.bfloat16
RATE = 0.2

ROWS = 1024
DIM = 200
HALF = DIM // 2
REL = 1345
RELP = 1408
NEG = 1000
BLOCK = 128
STEP = 256
EARLY = 384
EDGES = 512
LOAD = 216
ID_ROW = 200
HIST_ROW = 208
FLAT = 2304
SIDE = FLAT // 2

VMEM = pl.BlockSpec(memory_space=pltpu.VMEM)
SMEM = pl.BlockSpec(memory_space=pltpu.SMEM)
HBM = pl.BlockSpec(memory_space=pltpu.HBM)


def shape(*dims, dtype=F32):
    return jax.ShapeDtypeStruct(dims, dtype)


def params(grant):
    return pltpu.CompilerParams(vmem_limit_bytes=grant)


def halves(value):
    high = value.astype(BF16)
    return high, (value - high.astype(F32)).astype(BF16)


def dot(a, b, dims=((1,), (0,))):
    return lax.dot_general(a, b, (dims, ((), ())), preferred_element_type=F32)


NT = ((1,), (1,))


def dot3(a, b, dims=((1,), (0,))):
    return dot(a[0], b[0], dims) + (dot(a[1], b[0], dims) + dot(a[0], b[1], dims))


def one_hot(ids, count):
    places = lax.broadcasted_iota(jnp.int32, (count, ids.shape[1]), 0)
    return jnp.where(places == ids, 1.0, 0.0).astype(BF16)


def histogram(ids):
    upper = lax.broadcasted_iota(jnp.int32, (8, NEG), 0)
    lower = lax.broadcasted_iota(jnp.int32, (128, NEG), 0)
    high = jnp.where(upper == (ids >> 7), 1.0, 0.0).astype(BF16)
    low = jnp.where(lower == (ids & 127), 1.0, 0.0).astype(BF16)
    return dot(high, low, NT)


def live_sources(edges_ref, count, which):
    places = lax.broadcasted_iota(jnp.int32, (1, EDGES), 1)
    return jnp.where(places < count, edges_ref[0, which : which + 1, :], -1)


def fetch(sem, *pairs):
    copies = [pltpu.make_async_copy(a, b, sem.at[i]) for i, (a, b) in enumerate(pairs)]
    for copy in copies:
        copy.start()
    return copies


def write_payload(out_refs, parts, edges_ref, negatives_ref, count, which):
    source = live_sources(edges_ref, count, which)
    pick = one_hot(source, ROWS)
    high, low = parts
    rows = dot(high, pick) + dot(low, pick)
    first = 0
    for ref in out_refs:
        wide = ref.shape[1]
        span = slice(first, first + wide)
        ref[0:DIM, :] = rows[:, span]
        ref[ID_ROW : ID_ROW + 1, :] = edges_ref[1, which : which + 1, span].astype(F32)
        ref[ID_ROW + 1 : ID_ROW + 2, :] = edges_ref[2, which : which + 1, span].astype(F32)
        ref[ID_ROW + 2 : HIST_ROW, :] = jnp.zeros((HIST_ROW - ID_ROW - 2, wide), F32)
        for block in range(wide // BLOCK):
            k = first // BLOCK + block
            ref[HIST_ROW:LOAD, block * BLOCK : (block + 1) * BLOCK] = histogram(
                negatives_ref[which, k : k + 1, :]
            )
        first += wide


def prepare(
    counts_ref,
    table_hbm,
    edges_hbm,
    negatives_hbm,
    high_out,
    low_out,
    first_out,
    second_out,
    table_ref,
    edges_ref,
    negatives_ref,
    high_ref,
    low_ref,
    first_ref,
    second_ref,
    sem,
):
    copies = fetch(
        sem, (edges_hbm, edges_ref), (table_hbm, table_ref), (negatives_hbm, negatives_ref)
    )
    for copy in copies:
        copy.wait()
    parts = halves(table_ref[...])
    high_ref[...], low_ref[...] = parts
    copies = fetch(sem, (high_ref, high_out), (low_ref, low_out))
    pieces = (first_ref, second_ref)
    write_payload(pieces, parts, edges_ref, negatives_ref, counts_ref[0, 0], 0)
    copies += fetch(sem.at[2:4], (first_ref, first_out), (second_ref, second_out))
    for copy in copies:
        copy.wait()


def pad_relations(rel_ref, state_ref, rel_out, state_out, high_out, low_out):
    rel_out[:, 10 * 128 : RELP] = jnp.zeros((DIM, RELP - 10 * 128), F32)
    rel_out[:, 0:REL] = rel_ref[...]
    high_out[...], low_out[...] = halves(rel_out[...])
    state_out[...] = jnp.ones((1, RELP), F32)
    state_out[:, 0:REL] = state_ref[...]


def multiply(a_re, a_im, b_re, b_im, conjugate, out, lanes):
    if conjugate:
        out[0:HALF, lanes] = a_re * b_re + a_im * b_im
        out[HALF:DIM, lanes] = a_im * b_re - a_re * b_im
    else:
        out[0:HALF, lanes] = a_re * b_re - a_im * b_im
        out[HALF:DIM, lanes] = a_re * b_im + a_im * b_re


def weights(scores, times, target, first_lane):
    small = jnp.exp(-jnp.abs(scores))
    large = 1.0 / (1.0 + small)
    small = small * large
    up = scores >= 0.0
    plus = jnp.where(up, large, small)
    minus = jnp.where(up, small, large)
    lanes = lax.broadcasted_iota(jnp.int32, (1, 128), 1) + first_lane
    return plus * times - jnp.where(lanes == target, minus, 0.0)


def edge_terms(load_ref, table_parts, rel_parts, work, sg_out, rg_ref, first):
    w_ref, q_ref, score_ref, high_ref, low_ref, back_ref = work
    wide = load_ref.shape[1]
    pick = one_hot(load_ref[ID_ROW : ID_ROW + 1, :].astype(jnp.int32), RELP)
    w_ref[...] = dot(rel_parts[0], pick) + dot(rel_parts[1], pick)
    s_re, s_im = load_ref[0:HALF, :], load_ref[HALF:DIM, :]
    w_re, w_im = w_ref[0:HALF, :], w_ref[HALF:DIM, :]
    multiply(s_re, s_im, w_re, w_im, False, q_ref, slice(None))
    product = q_ref[...]
    product_parts = halves(product)
    target = load_ref[ID_ROW : ID_ROW + 8, :].T[:, 1:2].astype(jnp.int32)
    turned = halves(product.T)
    spans = [slice(start, min(start + STEP, wide)) for start in range(0, wide, STEP)]
    for edges in spans:
        score_ref[edges, :] = dot3((turned[0][edges], turned[1][edges]), table_parts)
    table_grad = None
    for span in spans:
        for block in range(span.start, span.stop, BLOCK):
            edges = slice(block, block + BLOCK)
            for tile in range(ROWS // 128):
                lanes = slice(tile * 128, (tile + 1) * 128)
                times = load_ref[HIST_ROW + tile : HIST_ROW + tile + 1, edges] * (1.0 / NEG)
                value = weights(score_ref[edges, lanes], times, target[edges], tile * 128)
                high_ref[edges, lanes], low_ref[edges, lanes] = halves(value)
        weight_parts = high_ref[span, :], low_ref[span, :]
        back_ref[:, span] = dot3(table_parts, weight_parts, NT)
        part = dot3((product_parts[0][:, span], product_parts[1][:, span]), weight_parts)
        table_grad = part if table_grad is None else table_grad + part
    up_re, up_im = back_ref[0:HALF, :], back_ref[HALF:DIM, :]
    lanes = slice(first, first + wide)
    multiply(up_re, up_im, s_re, s_im, True, rg_ref, lanes)
    multiply(up_re, up_im, w_re, w_im, True, sg_out, lanes)
    return table_grad, pick


def relation_grad(rg_ref, pick):
    high, low = halves(rg_ref[...])
    return dot(high, pick, NT) + dot(low, pick, NT)


def split_flat(core, grad, flat, send_out, keep_out):
    for tile in range(RELP // 128):
        flat[tile * DIM : (tile + 1) * DIM, :] = grad[:, tile * 128 : (tile + 1) * 128]
    flat[RELP // 128 * DIM : FLAT, :] = jnp.zeros((FLAT - RELP // 128 * DIM, 128), F32)
    keep_out[...] = flat[pl.ds(pl.multiple_of(core * SIDE, SIDE), SIDE), :]
    send_out[...] = flat[pl.ds(pl.multiple_of((1 - core) * SIDE, SIDE), SIDE), :]


def join_flat(core, mine_ref, other_ref, flat):
    flat[pl.ds(pl.multiple_of(core * SIDE, SIDE), SIDE), :] = mine_ref[...]
    flat[pl.ds(pl.multiple_of((1 - core) * SIDE, SIDE), SIDE), :] = other_ref[...]


def adagrad(table, state, grad):
    state = state + jnp.sum(grad * grad, axis=0, keepdims=True) * (1.0 / DIM)
    return table - grad * (RATE / jnp.sqrt(state)), state


def first_piece(
    load_ref, high_ref, low_ref, rel_high, rel_low, sg_out, rg_out, table_grad, *work
):
    table_parts, rel_parts = (high_ref[...], low_ref[...]), (rel_high[...], rel_low[...])
    table_grad[...], _ = edge_terms(load_ref, table_parts, rel_parts, work, sg_out, rg_out, 0)


def second_piece(
    core_ref,
    early_ref,
    load_ref,
    high_ref,
    low_ref,
    rel_high,
    rel_low,
    sg_ref,
    rg_ref,
    g_ref,
    sg_out,
    table_grad,
    send,
    keep,
    *work,
):
    work, rg, flat = work[:-2], work[-2], work[-1]
    table_parts, rel_parts = (high_ref[...], low_ref[...]), (rel_high[...], rel_low[...])
    first = EARLY
    sg_out[:, 0:first] = sg_ref[...]
    rg[:, 0:first] = rg_ref[...]
    grad, pick = edge_terms(load_ref, table_parts, rel_parts, work, sg_out, rg, first)
    table_grad[...] = grad + g_ref[...]
    early = one_hot(early_ref[ID_ROW : ID_ROW + 1, :].astype(jnp.int32), RELP)
    pick = jnp.concatenate([early, pick], axis=1)
    split_flat(core_ref[0], relation_grad(rg, pick), flat, send, keep)


def step_relations(core, mine_ref, other_ref, rel_ref, state_ref, flat, rel_out, state_out):
    join_flat(core, mine_ref, other_ref, flat)
    for tile in range(RELP // 128):
        lanes = slice(tile * 128, (tile + 1) * 128)
        rel_out[:, lanes], state_out[:, lanes] = adagrad(
            rel_ref[:, lanes], state_ref[:, lanes], flat[tile * DIM : (tile + 1) * DIM, :]
        )


def second_round(
    core_ref,
    mine_ref,
    other_ref,
    rel_ref,
    state_ref,
    load_ref,
    high_ref,
    low_ref,
    sg_out,
    table_grad,
    send,
    keep,
    rel_out,
    state_out,
    *work,
):
    work, rg, flat = work[:-2], work[-2], work[-1]
    core = core_ref[0]
    step_relations(core, mine_ref, other_ref, rel_ref, state_ref, flat, rel_out, state_out)
    table_grad[...], pick = edge_terms(
        load_ref, (high_ref[...], low_ref[...]), halves(rel_out[...]), work, sg_out, rg, 0
    )
    split_flat(core, relation_grad(rg, pick), flat, send, keep)


def step_entities(table_ref, state_ref, grad_ref, back_ref, edges_ref, count, which):
    pick = one_hot(live_sources(edges_ref, count, which), ROWS)
    high, low = halves(back_ref[...])
    grad = grad_ref[...] + (dot(high, pick, NT) + dot(low, pick, NT))
    return adagrad(table_ref[...], state_ref[...], grad)


def between(
    counts_ref,
    table_hbm,
    state_ref,
    grad_hbm,
    back_hbm,
    edges_hbm,
    negatives_hbm,
    table_out,
    state_out,
    high_out,
    low_out,
    load,
    table_ref,
    grad_ref,
    back_ref,
    edges_ref,
    negatives_ref,
    high_ref,
    low_ref,
    sem,
):
    copies = fetch(
        sem,
        (edges_hbm, edges_ref),
        (back_hbm, back_ref),
        (grad_hbm, grad_ref),
        (table_hbm, table_ref),
        (negatives_hbm, negatives_ref),
    )
    for copy in copies:
        copy.wait()
    table, state_out[...] = step_entities(
        table_ref, state_ref, grad_ref, back_ref, edges_ref, counts_ref[0, 0], 0
    )
    table_ref[...] = table
    parts = halves(table)
    high_ref[...], low_ref[...] = parts
    copies = fetch(sem, (table_ref, table_out), (high_ref, high_out), (low_ref, low_out))
    write_payload((load,), parts, edges_ref, negatives_ref, counts_ref[0, 1], 1)
    for copy in copies:
        copy.wait()


def last_entities(
    counts_ref,
    table_hbm,
    state_ref,
    grad_hbm,
    back_hbm,
    edges_hbm,
    table_out,
    state_out,
    table_ref,
    grad_ref,
    back_ref,
    edges_ref,
    sem,
):
    copies = fetch(
        sem,
        (edges_hbm, edges_ref),
        (back_hbm, back_ref),
        (grad_hbm, grad_ref),
        (table_hbm, table_ref),
    )
    for copy in copies:
        copy.wait()
    table, state_out[...] = step_entities(
        table_ref, state_ref, grad_ref, back_ref, edges_ref, counts_ref[0, 1], 1
    )
    table_ref[...] = table
    (copy,) = fetch(sem, (table_ref, table_out))
    copy.wait()


def last_relations(
    core_ref, mine_ref, other_ref, rel_ref, state_ref, rel_out, state_out, flat, rel, state
):
    step_relations(core_ref[0], mine_ref, other_ref, rel_ref, state_ref, flat, rel, state)
    rel_out[...] = rel[:, 0:REL]
    state_out[...] = state[:, 0:REL]


def work_shapes(wide):
    return [
        pltpu.VMEM((DIM, wide), F32),
        pltpu.VMEM((DIM, wide), F32),
        pltpu.VMEM((wide, ROWS), F32),
        pltpu.VMEM((wide, ROWS), BF16),
        pltpu.VMEM((wide, ROWS), BF16),
        pltpu.VMEM((DIM, wide), F32),
    ]


SPECS = {"s": SMEM, "v": VMEM, "h": HBM}


def call(body, ins, outs, operands, scratch=(), copies=0, grant=48 << 20):
    scratch = list(scratch) + ([pltpu.SemaphoreType.DMA((copies,))] if copies else [])
    return pl.pallas_call(
        body,
        out_shape=[out for _, out in outs],
        in_specs=[SPECS[kind] for kind in ins],
        out_specs=[SPECS[kind] for kind, _ in outs],
        scratch_shapes=scratch,
        compiler_params=params(grant),
    )(*operands)


def across(value, axis, apart):
    count = lax.axis_size(axis)
    return lax.ppermute(value, axis, [(i, i ^ apart) for i in range(count)])


def total(send, keep):
    part = (keep + across(send, C, 1)).reshape(16, SIDE // 16, 128)
    part = lax.all_to_all(part, (X, Y), 0, 0, tiled=True).sum(axis=0)
    part = jnp.broadcast_to(part[None], (8, *part.shape))
    part = lax.all_to_all(part, Z, 0, 0, tiled=True).sum(axis=0)
    part = jnp.broadcast_to(part[None], (16, *part.shape))
    part = lax.all_to_all(part, (X, Y), 0, 0, tiled=True)
    mine = part.reshape(SIDE, 128)
    return mine, across(mine, C, 1)


def body(entities, entity_state, relations, relation_state, edges, negatives, counts):
    core = lax.axis_index(C).astype(jnp.int32).reshape(1)
    table, rel, counts = entities.T, relations.T, counts.T
    edges = edges.transpose(1, 0, 2)
    state = entity_state.reshape(1, ROWS)
    late = EDGES - EARLY
    grown = shape(DIM, ROWS)
    narrow = shape(DIM, ROWS, dtype=BF16)
    wide_rel = shape(DIM, RELP, dtype=BF16)
    vmem = pltpu.VMEM
    table_mem, narrow_mem = vmem((DIM, ROWS), F32), vmem((DIM, ROWS), BF16)
    flat_mem, back_mem = vmem((FLAT, 128), F32), vmem((DIM, EDGES), F32)
    edge_mem, negative_mem = vmem((3, 2, EDGES), jnp.int32), vmem(negatives.shape, jnp.int32)
    high, low, first, second = call(
        prepare,
        "shhh",
        [("h", narrow), ("h", narrow), ("h", shape(LOAD, EARLY)), ("h", shape(LOAD, late))],
        (counts, table, edges, negatives),
        [table_mem, edge_mem, negative_mem, narrow_mem, narrow_mem]
        + [vmem((LOAD, EARLY), F32), vmem((LOAD, late), F32)],
        4,
        63 << 20,
    )
    first = across(first, Z, 4)
    second = across(second, Z, 4)
    rel, rel_state, rel_high, rel_low = call(
        pad_relations,
        "vv",
        [("v", shape(DIM, RELP)), ("v", shape(1, RELP)), ("v", wide_rel), ("v", wide_rel)],
        (rel, relation_state.reshape(1, REL)),
    )
    piece = ("v", shape(DIM, EARLY))
    back, rel_terms, grad = call(
        first_piece,
        "vvvvv",
        [piece, piece, ("v", grown)],
        (first, high, low, rel_high, rel_low),
        work_shapes(EARLY),
    )
    half = ("v", shape(SIDE, 128))
    back, grad, send, keep = call(
        second_piece,
        "svvvvvvvvv",
        [("v", shape(DIM, EDGES)), ("v", grown), half, half],
        (core, first, second, high, low, rel_high, rel_low, back, rel_terms, grad),
        work_shapes(late) + [back_mem, flat_mem],
    )
    back = across(back, Z, 4)
    mine, other = total(send, keep)
    table, state, high, low, load = call(
        between,
        "shvhhhh",
        [
            ("h", grown),
            ("v", shape(1, ROWS)),
            ("h", narrow),
            ("h", narrow),
            ("v", shape(LOAD, EDGES)),
        ],
        (counts, table, state, grad, back, edges, negatives),
        [table_mem, table_mem, back_mem, edge_mem, negative_mem, narrow_mem, narrow_mem],
        5,
        63 << 20,
    )
    load = across(load, C, 1)
    back, grad, send, keep, rel, rel_state = call(
        second_round,
        "svvvvvvv",
        [
            ("v", shape(DIM, EDGES)),
            ("v", grown),
            half,
            half,
            ("v", shape(DIM, RELP)),
            ("v", shape(1, RELP)),
        ],
        (core, mine, other, rel, rel_state, load, high, low),
        work_shapes(EDGES) + [back_mem, flat_mem],
    )
    back = across(back, C, 1)
    mine, other = total(send, keep)
    table, state = call(
        last_entities,
        "shvhhh",
        [("h", grown), ("v", shape(1, ROWS))],
        (counts, table, state, grad, back, edges),
        [table_mem, table_mem, back_mem, edge_mem],
        4,
        63 << 20,
    )
    rel, rel_state = call(
        last_relations,
        "svvvv",
        [("v", shape(DIM, REL)), ("v", shape(1, REL))],
        (core, mine, other, rel, rel_state),
        [flat_mem, vmem((DIM, RELP), F32), vmem((1, RELP), F32)],
    )
    return table.T, state.reshape(ROWS), rel.T, rel_state.reshape(REL)


def solution(mesh):
    finer = Mesh(mesh.devices.reshape(8, 4, 4, 2), DOM)
    return jax.shard_map(
        body,
        mesh=finer,
        in_specs=(
            P(DOM, None),
            P(DOM),
            P(),
            P(),
            P(None, None, DOM),
            P(None, DOM, None),
            P(None, DOM),
        ),
        out_specs=(P(DOM, None), P(DOM), P(), P()),
        check_vma=False,
    )
```

time: 177 us -> 191 us (1.079)
  Pallas kernels: 24.6 us -> 33.5 us
  waiting for transfers between devices: 20.9 us -> 24.2 us
    pallas_call x8, Pallas kernels: 24.6 us -> 33.5 us  [call(): pl.pallas_call(body, out_shape=[out for _, out in outs], in_specs=[SPECS[...]
    ppermute x9, waiting for transfers between devices: 13.7 us -> 16.9 us  [across(): return lax.ppermute(value, axis, [(i, i ^ apart) for i in range(count)])]
  transfers between devices with their start and end apart: 10 -> 10, of which waited for: 8 -> 7; matrix products, arithmetic and copies ran while one was open for 0% -> 0% of each run, Pallas kernels for 5% -> 8%
where the time goes in v1:
time: 191 us; the launch traced here: 190 us
  blocking collectives  87 us (46%)
  Pallas kernels  33.5 us (18%)
  starting transfers between devices  32.2 us (17%)
  waiting for transfers between devices  24.2 us (13%)
  local copies, waits for them, and re-layouts  11.3 us (6%)
    all_to_all x2, blocking collectives, total(): part = lax.all_to_all(part, Z, 0, 0, tiled=True).sum(axis=0)  38.1 us
    all_to_all x2, blocking collectives, total(): part = lax.all_to_all(part, (X, Y), 0, 0, tiled=True).sum(axis=0)  36 us
    pallas_call x8, Pallas kernels, call(): pl.pallas_call(body, out_shape=[out for _, out in outs], in_specs=[SPECS[...  33.5 us
    ppermute x9, starting transfers between devices, across(): return lax.ppermute(value, axis, [(i, i ^ apart) for i in range(count)])  28.4 us
    ppermute x9, waiting for transfers between devices, across(): return lax.ppermute(value, axis, [(i, i ^ apart) for i in range(count)])  16.9 us
    all_to_all x1, blocking collectives, total(): part = lax.all_to_all(part, (X, Y), 0, 0, tiled=True)  12.9 us
    unnamed x26, local copies, waits for them, and re-layouts  9.7 us
    all_to_all x1, waiting for transfers between devices, total(): part = lax.all_to_all(part, (X, Y), 0, 0, tiled=True)  7.23 us
  transfers between devices with their start and end apart: 10, of which 7 were waited for; matrix products, arithmetic and copies ran while one was open for 0% of the time, Pallas kernels for 8%

profile of v1, /device:TPU:1, one launch (start us, length us, event | category | flops | bytes accessed | tf_op | source)
XLA Modules:
  0.0 189.8 jit_solution(17208435140849290269)
XLA Ops:
  0.6 3.7 %shard_map.102 = (bf16[200,1024]{1,0:T(8,128)(2,1)}, bf16[200,1024]{1,0:T(8,128)(2,1)}, f32[216,384]{1,0:T(8,128)}, f32[216,128]{1,0:T(8,128)}) custom-call(s32[1,2]{1,0:T(1,128)} %bitcast.25, f32[200,1024]{1,0:T(8,128)} %bitcast.18, s32[3,2,512]{2,1,0:T(2,128)} %bitcast.22, s32[2,4,1000]{2,1,0:T(4,128)} %negatives_hbm.3), custom_call_target="tpu_custom_call" | custom-call | tf_op jit(solution)/shard_map/pallas_call | solution.py:403
  4.4 0.0 copy-start
  4.4 0.0 copy-start.1
  4.4 7.8 %collective-permute-start = (f32[216,384]{1,0:T(8,128)}, f32[216,384]{1,0:T(8,128)S(1)}, u32[]{:S(2)}, u32[]{:S(2)}) collective-permute-start(f32[216,384]{1,0:T(8,128)} %get-tuple-element.34), channel_id=1, source_target_pairs={{0,128},{32,160},{64,192},{96,224},{128,0},{160,32},{192,64},{224,... | collective-permute-start | bytes 995336 | tf_op jit(solution)/shard_map/ppermute | solution.py:415
  12.2 0.1 collective-permute-start.1
  12.3 0.7 reshape.41.state_ref
  13.0 0.0 copy-start.2
  13.0 1.2 copy-done.2
  14.3 0.4 shard_map.103
  14.7 0.0 copy-start.3
  14.7 5.8 %collective-permute-done.load_ref.early_ref = f32[216,384]{1,0:T(8,128)S(1)} collective-permute-done((f32[216,384]{1,0:T(8,128)}, f32[216,384]{1,0:T(8,128)S(1)}, u32[]{:S(2)}, u32[]{:S(2)}) %collective-permute-start) | collective-permute-done | bytes 331808 | tf_op jit(solution)/shard_map/ppermute | solution.py:415
  20.5 0.0 copy-done
  20.5 0.0 copy-done.1
  20.5 4.7 %shard_map.104 = (f32[200,384]{1,0:T(8,128)S(1)}, f32[200,384]{1,0:T(8,128)S(1)}, f32[200,1024]{1,0:T(8,128)S(1)}) custom-call(f32[216,384]{1,0:T(8,128)S(1)} %collective-permute-done.load_ref.early_ref, bf16[200,1024]{1,0:T(8,128)(2,1)S(1)} %copy-done, bf16[200,1024]{1,0:T(8,128)(2,1)S(1)} %copy-done.1, bf16[200,1408]{1,0:T(8,128)(2,1)S(1)} %get-tuple-element.38.rel_high, ...), custom_call_target="tpu_custom_call" | custom-call | tf_op jit(solution)/shard_map/pallas_call | solution.py:403
  25.1 0.0 copy-done.3
  25.1 0.0 copy-start.8
  25.1 0.9 copy-done.8
  26.0 0.0 collective-permute-done.1.load_ref
  26.0 4.2 %shard_map.105 = (f32[200,512]{1,0:T(8,128)S(1)}, f32[200,1024]{1,0:T(8,128)S(1)}, f32[1152,128]{1,0:T(8,128)S(1)}, f32[1152,128]{1,0:T(8,128)S(1)}) custom-call(s32[1]{0:T(128)} %bitcast.3.core_ref, f32[216,384]{1,0:T(8,128)S(1)} %collective-permute-done.load_ref.early_ref, f32[216,128]{1,0:T(8,128)S(1)} %collective-permute-done.1.load_ref, ...), custom_call_target="tpu_custom_call" | custom-call | tf_op jit(solution)/shard_map/pallas_call | solution.py:403
  30.2 0.0 copy-start.6
  30.2 0.9 copy-done.6
  31.1 3.0 %collective-permute-start.3 = (f32[1152,128]{1,0:T(8,128)S(1)}, f32[1152,128]{1,0:T(8,128)S(1)}, u32[]{:S(2)}, u32[]{:S(2)}) collective-permute-start(f32[1152,128]{1,0:T(8,128)S(1)} %get-tuple-element.48), channel_id=1, source_target_pairs={{0,1},{1,0},{2,3},{3,2},{4,5},{5,4},{6,7},{7,6},{8,9},{9,8},{10,11... | collective-permute-start | bytes 1769480 | tf_op jit(solution)/shard_map/ppermute | solution.py:415
  34.1 1.6 collective-permute-done.3
  35.8 0.1 add.6
  35.8 17.7 %all_to_all.30 = f32[16,72,128]{2,1,0:T(8,128)S(1)} all-to-all(f32[16,72,128]{2,1,0:T(8,128)S(1)} %bitcast.20), channel_id=1, replica_groups=mesh['z'=8,'x'=4,'y'=4,'c'=2] {'x','y'}, dimensions={0} | all-to-all | bytes 1179648 | tf_op jit(solution)/shard_map/all_to_all | solution.py:420
  53.6 24.4 %all_to_all.31 = f32[8,72,128]{2,1,0:T(8,128)S(1)} all-to-all(f32[8,72,128]{2,1,0:T(8,128)S(1)} %broadcast_in_dim.8), channel_id=1, replica_groups=mesh['z'=8,'x'=4,'y'=4,'c'=2] {'z'}, dimensions={0} | all-to-all | bytes 589824 | tf_op jit(solution)/shard_map/all_to_all | solution.py:422
  78.1 0.9 broadcast_in_dim.9
  79.0 3.8 %all-to-all-start.2 = ((f32[16,72,128]{2,1,0:T(8,128)}), f32[16,72,128]{2,1,0:T(8,128)S(1)}, u32[]{:S(2)}, u32[]{:S(2)}) async-start(f32[16,72,128]{2,1,0:T(8,128)} %broadcast_in_dim.9), calls=%async_computation.2 | async-start | bytes 1179648 | tf_op jit(solution)/shard_map/all_to_all | solution.py:424
  82.7 2.1 %collective-permute-start.2 = (f32[200,512]{1,0:T(8,128)S(1)}, f32[200,512]{1,0:T(8,128)S(1)}, u32[]{:S(2)}, u32[]{:S(2)}) collective-permute-start(f32[200,512]{1,0:T(8,128)S(1)} %get-tuple-element.44), channel_id=1, source_target_pairs={{0,128},{32,160},{64,192},{96,224},{128,0},{160,32},{192,64},{224,... | collective-permute-start | bytes 1228808 | tf_op jit(solution)/shard_map/ppermute | solution.py:415
  84.9 7.2 %all-to-all-done.2 = f32[16,72,128]{2,1,0:T(8,128)S(1)} async-done(((f32[16,72,128]{2,1,0:T(8,128)}), f32[16,72,128]{2,1,0:T(8,128)S(1)}, u32[]{:S(2)}, u32[]{:S(2)}) %all-to-all-start.2) | async-done | bytes 589856 | tf_op jit(solution)/shard_map/all_to_all | solution.py:424
  92.1 4.6 %collective-permute-start.4 = (f32[1152,128]{1,0:T(8,128)S(1)}, f32[1152,128]{1,0:T(8,128)}, u32[]{:S(2)}, u32[]{:S(2)}) collective-permute-start(f32[1152,128]{1,0:T(8,128)S(1)} %bitcast.13), channel_id=1, source_target_pairs={{0,1},{1,0},{2,3},{3,2},{4,5},{5,4},{6,7},{7,6},{8,9},{9,8},{10,11... | collective-permute-start | bytes 1769480 | tf_op jit(solution)/shard_map/ppermute | solution.py:415
  96.7 4.0 %collective-permute-done.2.back_hbm = f32[200,512]{1,0:T(8,128)S(1)} collective-permute-done((f32[200,512]{1,0:T(8,128)S(1)}, f32[200,512]{1,0:T(8,128)S(1)}, u32[]{:S(2)}, u32[]{:S(2)}) %collective-permute-start.2) | collective-permute-done | bytes 409632 | tf_op jit(solution)/shard_map/ppermute | solution.py:415
  100.7 0.0 copy-start.11
  100.7 0.7 copy-done.11
  101.4 5.6 %shard_map.106 = (f32[200,1024]{1,0:T(8,128)}, f32[1,1024]{1,0:T(1,128)}, bf16[200,1024]{1,0:T(8,128)(2,1)}, bf16[200,1024]{1,0:T(8,128)(2,1)}, f32[216,512]{1,0:T(8,128)}) custom-call(s32[1,2]{1,0:T(1,128)} %bitcast.26, f32[200,1024]{1,0:T(8,128)} %bitcast.19, f32[1,1024]{1,0:T(1,128)} %bitcast.28, f32[200,1024]{1,0:T(8,128)} %copy-done.6, ...), custom_call_target="tpu_custom_call" | custom-call | tf_op jit(solution)/shard_map/pallas_call | solution.py:403
  107.0 5.8 %collective-permute-start.5 = (f32[216,512]{1,0:T(8,128)}, f32[216,512]{1,0:T(8,128)S(1)}, u32[]{:S(2)}, u32[]{:S(2)}) collective-permute-start(f32[216,512]{1,0:T(8,128)} %get-tuple-element.51), channel_id=1, source_target_pairs={{0,1},{1,0},{2,3},{3,2},{4,5},{5,4},{6,7},{7,6},{8,9},{9,8},{10,11... | collective-permute-start | bytes 1327112 | tf_op jit(solution)/shard_map/ppermute | solution.py:415
  112.8 1.6 collective-permute-done.5.load_ref
  114.5 0.0 collective-permute-done.4.other_ref
  114.5 0.0 copy-start.9
  114.5 1.0 copy-done.9
  115.5 0.0 copy-start.10
  115.5 1.0 copy-done.10
  116.5 7.8 %shard_map.107 = (f32[200,512]{1,0:T(8,128)S(1)}, f32[200,1024]{1,0:T(8,128)S(1)}, f32[1152,128]{1,0:T(8,128)S(1)}, f32[1152,128]{1,0:T(8,128)S(1)}, f32[200,1408]{1,0:T(8,128)S(1)}, /*index=5*/f32[1,1408]{1,0:T(1,128)S(1)}) custom-call(s32[1]{0:T(128)} %bitcast.3.core_ref, f32[1152,128]{1,0:T(8,128)S(1)} %bitcast.14, ...), custom_call_target="tpu_custom_call" | custom-call | tf_op jit(solution)/shard_map/pallas_call | solution.py:403
  124.2 0.0 copy-start.4
  124.2 1.0 copy-done.4
  125.2 0.0 copy-start.7
  125.2 0.9 copy-done.7
  126.1 0.4 collective-permute-start.7
  126.5 1.6 collective-permute-done.7
  128.2 0.1 add.7
  128.2 18.2 %all_to_all.32 = f32[16,72,128]{2,1,0:T(8,128)S(1)} all-to-all(f32[16,72,128]{2,1,0:T(8,128)S(1)} %bitcast.21), channel_id=1, replica_groups=mesh['z'=8,'x'=4,'y'=4,'c'=2] {'x','y'}, dimensions={0} | all-to-all | bytes 1179648 | tf_op jit(solution)/shard_map/all_to_all | solution.py:420
  146.5 13.7 %all_to_all.33 = f32[8,72,128]{2,1,0:T(8,128)S(1)} all-to-all(f32[8,72,128]{2,1,0:T(8,128)S(1)} %broadcast_in_dim.10), channel_id=1, replica_groups=mesh['z'=8,'x'=4,'y'=4,'c'=2] {'z'}, dimensions={0} | all-to-all | bytes 589824 | tf_op jit(solution)/shard_map/all_to_all | solution.py:422
  160.2 12.9 %all_to_all.34 = f32[16,72,128]{2,1,0:T(8,128)S(1)} all-to-all(f32[16,72,128]{2,1,0:T(8,128)S(1)} %broadcast_in_dim.11), channel_id=1, replica_groups=mesh['z'=8,'x'=4,'y'=4,'c'=2] {'x','y'}, dimensions={0} | all-to-all | bytes 1179648 | tf_op jit(solution)/shard_map/all_to_all | solution.py:424
  173.2 4.6 %collective-permute-start.8 = (f32[1152,128]{1,0:T(8,128)S(1)}, f32[1152,128]{1,0:T(8,128)}, u32[]{:S(2)}, u32[]{:S(2)}) collective-permute-start(f32[1152,128]{1,0:T(8,128)S(1)} %bitcast.15), channel_id=1, source_target_pairs={{0,1},{1,0},{2,3},{3,2},{4,5},{5,4},{6,7},{7,6},{8,9},{9,8},{10,11... | collective-permute-start | bytes 1769480 | tf_op jit(solution)/shard_map/ppermute | solution.py:415
  177.8 0.0 collective-permute-start.6
  177.8 2.2 %collective-permute-done.6.back_hbm = f32[200,512]{1,0:T(8,128)S(1)} collective-permute-done((f32[200,512]{1,0:T(8,128)S(1)}, f32[200,512]{1,0:T(8,128)S(1)}, u32[]{:S(2)}, u32[]{:S(2)}) %collective-permute-start.6) | collective-permute-done | bytes 409632 | tf_op jit(solution)/shard_map/ppermute | solution.py:415
  180.0 0.0 copy-start.12
  180.0 0.8 copy-done.12
  180.7 4.8 %shard_map.108 = (f32[200,1024]{1,0:T(8,128)}, f32[1,1024]{1,0:T(1,128)}) custom-call(s32[1,2]{1,0:T(1,128)} %bitcast.27, f32[200,1024]{1,0:T(8,128)} %get-tuple-element.45.table_hbm, f32[1,1024]{1,0:T(1,128)} %get-tuple-element.46.state_ref, f32[200,1024]{1,0:T(8,128)} %copy-done.7, f32[200,512]{1,0:T(8,128)} %copy-done.12, s32[3,2,512]{2,1,0:T(2,128)} %bitcast.24), custom_call_target="tpu_custom_call" | custom-call | tf_op jit(solution)/shard_map/pallas_call | solution.py:403
  185.6 0.0 collective-permute-done.8.other_ref
  185.6 0.0 copy-start.5
  185.6 1.2 copy-done.5
  186.8 2.4 %shard_map.109 = (f32[200,1345]{1,0:T(8,128)}, f32[1,1345]{1,0:T(1,128)S(1)}) custom-call(s32[1]{0:T(128)} %bitcast.3.core_ref, f32[1152,128]{1,0:T(8,128)S(1)} %bitcast.16, f32[1152,128]{1,0:T(8,128)} %collective-permute-done.8.other_ref, f32[200,1408]{1,0:T(8,128)S(1)} %copy-done.5, f32[1,1408]{1,0:T(1,128)S(1)} %get-tuple-element.61.state_ref), custom_call_target="tpu_custom_call" | custom-call | tf_op jit(solution)/shard_map/pallas_call | solution.py:403
  189.2 0.6 reduce
  (7 shorter events, 0.2 us)
Async XLA Ops:
  4.4 16.1 %copy-start = (bf16[200,1024]{1,0:T(8,128)(2,1)S(1)}, bf16[200,1024]{1,0:T(8,128)(2,1)}, u32[]{:S(2)}) copy-start(bf16[200,1024]{1,0:T(8,128)(2,1)} %get-tuple-element.36.high_ref) | copy-start | bytes 1228804
  4.4 16.1 %copy-start.1 = (bf16[200,1024]{1,0:T(8,128)(2,1)S(1)}, bf16[200,1024]{1,0:T(8,128)(2,1)}, u32[]{:S(2)}) copy-start(bf16[200,1024]{1,0:T(8,128)(2,1)} %get-tuple-element.37.low_ref) | copy-start | bytes 1228804
  4.4 16.1 %collective-permute-start = (f32[216,384]{1,0:T(8,128)}, f32[216,384]{1,0:T(8,128)S(1)}, u32[]{:S(2)}, u32[]{:S(2)}) collective-permute-start(f32[216,384]{1,0:T(8,128)} %get-tuple-element.34), channel_id=1, source_target_pairs={{0,128},{32,160},{64,192},{96,224},{128,0},{160,32},{192,64},{224,... | collective-permute-start | bytes 995336 | tf_op jit(solution)/shard_map/ppermute | solution.py:415
  12.2 13.8 %collective-permute-start.1 = (f32[216,128]{1,0:T(8,128)}, f32[216,128]{1,0:T(8,128)S(1)}, u32[]{:S(2)}, u32[]{:S(2)}) collective-permute-start(f32[216,128]{1,0:T(8,128)} %get-tuple-element.35), channel_id=1, source_target_pairs={{0,128},{32,160},{64,192},{96,224},{128,0},{160,32},{192,64},{224,... | collective-permute-start | bytes 331784 | tf_op jit(solution)/shard_map/ppermute | solution.py:415
  13.0 1.3 copy-start.2
  14.7 10.5 %copy-start.3 = (f32[200,1408]{1,0:T(8,128)}, f32[200,1408]{1,0:T(8,128)S(1)}, u32[]{:S(2)}) copy-start(f32[200,1408]{1,0:T(8,128)S(1)} %get-tuple-element.49.rel_ref) | copy-start | bytes 3379204
  25.1 0.9 copy-start.8
  30.2 0.9 copy-start.6
  31.1 4.7 %collective-permute-start.3 = (f32[1152,128]{1,0:T(8,128)S(1)}, f32[1152,128]{1,0:T(8,128)S(1)}, u32[]{:S(2)}, u32[]{:S(2)}) collective-permute-start(f32[1152,128]{1,0:T(8,128)S(1)} %get-tuple-element.48), channel_id=1, source_target_pairs={{0,1},{1,0},{2,3},{3,2},{4,5},{5,4},{6,7},{7,6},{8,9},{9,8},{10,11... | collective-permute-start | bytes 1769480 | tf_op jit(solution)/shard_map/ppermute | solution.py:415
  79.0 13.2 %all-to-all-start.2 = ((f32[16,72,128]{2,1,0:T(8,128)}), f32[16,72,128]{2,1,0:T(8,128)S(1)}, u32[]{:S(2)}, u32[]{:S(2)}) async-start(f32[16,72,128]{2,1,0:T(8,128)} %broadcast_in_dim.9), calls=%async_computation.2 | async-start | bytes 1179648 | tf_op jit(solution)/shard_map/all_to_all | solution.py:424
  82.7 18.0 %collective-permute-start.2 = (f32[200,512]{1,0:T(8,128)S(1)}, f32[200,512]{1,0:T(8,128)S(1)}, u32[]{:S(2)}, u32[]{:S(2)}) collective-permute-start(f32[200,512]{1,0:T(8,128)S(1)} %get-tuple-element.44), channel_id=1, source_target_pairs={{0,128},{32,160},{64,192},{96,224},{128,0},{160,32},{192,64},{224,... | collective-permute-start | bytes 1228808 | tf_op jit(solution)/shard_map/ppermute | solution.py:415
  92.1 22.3 %collective-permute-start.4 = (f32[1152,128]{1,0:T(8,128)S(1)}, f32[1152,128]{1,0:T(8,128)}, u32[]{:S(2)}, u32[]{:S(2)}) collective-permute-start(f32[1152,128]{1,0:T(8,128)S(1)} %bitcast.13), channel_id=1, source_target_pairs={{0,1},{1,0},{2,3},{3,2},{4,5},{5,4},{6,7},{7,6},{8,9},{9,8},{10,11... | collective-permute-start | bytes 1769480 | tf_op jit(solution)/shard_map/ppermute | solution.py:415
  100.7 0.7 copy-start.11
  107.0 7.4 %collective-permute-start.5 = (f32[216,512]{1,0:T(8,128)}, f32[216,512]{1,0:T(8,128)S(1)}, u32[]{:S(2)}, u32[]{:S(2)}) collective-permute-start(f32[216,512]{1,0:T(8,128)} %get-tuple-element.51), channel_id=1, source_target_pairs={{0,1},{1,0},{2,3},{3,2},{4,5},{5,4},{6,7},{7,6},{8,9},{9,8},{10,11... | collective-permute-start | bytes 1327112 | tf_op jit(solution)/shard_map/ppermute | solution.py:415
  114.5 1.0 copy-start.9
  115.5 1.0 copy-start.10
  124.2 1.0 copy-start.4
  125.2 0.9 copy-start.7
  126.1 2.0 %collective-permute-start.7 = (f32[1152,128]{1,0:T(8,128)S(1)}, f32[1152,128]{1,0:T(8,128)S(1)}, u32[]{:S(2)}, u32[]{:S(2)}) collective-permute-start(f32[1152,128]{1,0:T(8,128)S(1)} %get-tuple-element.59), channel_id=1, source_target_pairs={{0,1},{1,0},{2,3},{3,2},{4,5},{5,4},{6,7},{7,6},{8,9},{9,8},{10,11... | collective-permute-start | bytes 1769480 | tf_op jit(solution)/shard_map/ppermute | solution.py:415
  173.2 12.4 %collective-permute-start.8 = (f32[1152,128]{1,0:T(8,128)S(1)}, f32[1152,128]{1,0:T(8,128)}, u32[]{:S(2)}, u32[]{:S(2)}) collective-permute-start(f32[1152,128]{1,0:T(8,128)S(1)} %bitcast.15), channel_id=1, source_target_pairs={{0,1},{1,0},{2,3},{3,2},{4,5},{5,4},{6,7},{7,6},{8,9},{9,8},{10,11... | collective-permute-start | bytes 1769480 | tf_op jit(solution)/shard_map/ppermute | solution.py:415
  177.8 2.2 %collective-permute-start.6 = (f32[200,512]{1,0:T(8,128)S(1)}, f32[200,512]{1,0:T(8,128)S(1)}, u32[]{:S(2)}, u32[]{:S(2)}) collective-permute-start(f32[200,512]{1,0:T(8,128)S(1)} %get-tuple-element.55), channel_id=1, source_target_pairs={{0,1},{1,0},{2,3},{3,2},{4,5},{5,4},{6,7},{7,6},{8,9},{9,8},{10,11... | collective-permute-start | bytes 1228808 | tf_op jit(solution)/shard_map/ppermute | solution.py:415
  180.0 0.8 copy-start.12
  185.6 1.3 copy-start.5

commit v2 on v1

v2 whole, which is shorter than its diff:
```python
import jax
import jax.numpy as jnp
from jax import lax
from jax.experimental import pallas as pl
from jax.experimental.pallas import tpu as pltpu
from jax.sharding import Mesh
from jax.sharding import PartitionSpec as P

Z, X, Y, C = "z", "x", "y", "c"
DOM = (Z, X, Y, C)
F32 = jnp.float32
BF16 = jnp.bfloat16
RATE = 0.2

ROWS = 1024
DIM = 200
HALF = DIM // 2
REL = 1345
RELP = 1536
NEG = 1000
BLOCK = 128
STEP = 256
EARLY = 256
STORE = 18
GRAD, RELATION, TABLE = 0, 1, 2
EDGES = 512
LOAD = 216
ID_ROW = 200
HIST_ROW = 208
FLAT = 2304
SIDE = FLAT // 2
TILES = 11

VMEM = pl.BlockSpec(memory_space=pltpu.VMEM)
SMEM = pl.BlockSpec(memory_space=pltpu.SMEM)
HBM = pl.BlockSpec(memory_space=pltpu.HBM)


def shape(*dims, dtype=F32):
    return jax.ShapeDtypeStruct(dims, dtype)


def params(grant):
    return pltpu.CompilerParams(vmem_limit_bytes=grant)


def halves(value):
    high = value.astype(BF16)
    return high, (value - high.astype(F32)).astype(BF16)


def dot(a, b, dims=((1,), (0,))):
    return lax.dot_general(a, b, (dims, ((), ())), preferred_element_type=F32)


NT = ((1,), (1,))


def dot3(a, b, dims=((1,), (0,))):
    return dot(a[0], b[0], dims) + (dot(a[1], b[0], dims) + dot(a[0], b[1], dims))


def one_hot(ids, count, first=0):
    places = lax.broadcasted_iota(jnp.int32, (count, ids.shape[1]), 0)
    return jnp.where(places == ids - first, 1.0, 0.0).astype(BF16)


def steps(count, size, step):
    def visit(index, carry):
        step(pl.multiple_of(index * size, size))
        return carry

    lax.fori_loop(0, count // size, visit, 0)


def histogram(ids):
    upper = lax.broadcasted_iota(jnp.int32, (8, NEG), 0)
    lower = lax.broadcasted_iota(jnp.int32, (128, NEG), 0)
    high = jnp.where(upper == (ids >> 7), 1.0, 0.0).astype(BF16)
    low = jnp.where(lower == (ids & 127), 1.0, 0.0).astype(BF16)
    return dot(high, low, NT)


def live_sources(edges_ref, count, which):
    places = lax.broadcasted_iota(jnp.int32, (1, EDGES), 1)
    return jnp.where(places < count, edges_ref[0, which : which + 1, :], -1)


def fetch(sem, *pairs):
    copies = [pltpu.make_async_copy(a, b, sem.at[i]) for i, (a, b) in enumerate(pairs)]
    for copy in copies:
        copy.start()
    return copies


def write_payload(out_refs, parts, edges_ref, negatives_ref, count, which):
    source = live_sources(edges_ref, count, which)
    pick = one_hot(source, ROWS)
    high, low = parts
    rows = dot(high, pick) + dot(low, pick)
    first = 0
    for ref in out_refs:
        wide = ref.shape[1]
        span = slice(first, first + wide)
        ref[0:DIM, :] = rows[:, span]
        ref[ID_ROW : ID_ROW + 1, :] = edges_ref[1, which : which + 1, span].astype(F32)
        ref[ID_ROW + 1 : ID_ROW + 2, :] = edges_ref[2, which : which + 1, span].astype(F32)
        ref[ID_ROW + 2 : HIST_ROW, :] = jnp.zeros((HIST_ROW - ID_ROW - 2, wide), F32)
        for block in range(wide // BLOCK):
            k = first // BLOCK + block
            ref[HIST_ROW:LOAD, block * BLOCK : (block + 1) * BLOCK] = histogram(
                negatives_ref[which, k : k + 1, :]
            )
        first += wide


def prepare(
    counts_ref,
    table_hbm,
    edges_hbm,
    negatives_hbm,
    high_out,
    low_out,
    first_out,
    second_out,
    table_ref,
    edges_ref,
    negatives_ref,
    high_ref,
    low_ref,
    first_ref,
    second_ref,
    sem,
):
    copies = fetch(
        sem, (edges_hbm, edges_ref), (table_hbm, table_ref), (negatives_hbm, negatives_ref)
    )
    for copy in copies:
        copy.wait()
    parts = halves(table_ref[...])
    high_ref[...], low_ref[...] = parts
    copies = fetch(sem, (high_ref, high_out), (low_ref, low_out))
    pieces = (first_ref, second_ref)
    write_payload(pieces, parts, edges_ref, negatives_ref, counts_ref[0, 0], 0)
    copies += fetch(sem.at[2:4], (first_ref, first_out), (second_ref, second_out))
    for copy in copies:
        copy.wait()


def pad_relations(rel_ref, state_ref, rel_out, state_out, high_out, low_out, rel, sem):
    rel[:, 10 * 128 : RELP] = jnp.zeros((DIM, RELP - 10 * 128), F32)
    rel[:, 0:REL] = rel_ref[...]
    (copy,) = fetch(sem, (rel, rel_out.at[RELATION]))
    high_out[...], low_out[...] = halves(rel[...])
    state_out[...] = jnp.ones((1, RELP), F32)
    state_out[:, 0:REL] = state_ref[...]
    copy.wait()


def multiply(a_re, a_im, b_re, b_im, conjugate, out, lanes):
    if conjugate:
        out[0:HALF, lanes] = a_re * b_re + a_im * b_im
        out[HALF:DIM, lanes] = a_im * b_re - a_re * b_im
    else:
        out[0:HALF, lanes] = a_re * b_re - a_im * b_im
        out[HALF:DIM, lanes] = a_re * b_im + a_im * b_re


def weights(scores, times, target, first_lane):
    small = jnp.exp(-jnp.abs(scores))
    large = 1.0 / (1.0 + small)
    small = small * large
    up = scores >= 0.0
    plus = jnp.where(up, large, small)
    minus = jnp.where(up, small, large)
    lanes = lax.broadcasted_iota(jnp.int32, (1, 128), 1) + first_lane
    return plus * times - jnp.where(lanes == target, minus, 0.0)


def edge_terms(load_ref, high_ref, low_ref, rel_parts, work, grad_ref, sg_out, rg_ref, first, put):
    w_ref, q_ref, qh_ref, ql_ref, score_ref, wh_ref, wl_ref, back_ref, target_ref = work
    wide = load_ref.shape[1]
    ids = load_ref[ID_ROW : ID_ROW + 1, :].astype(jnp.int32)
    w_ref[...] = jnp.zeros((DIM, wide), F32)

    def gather(start):
        pick = one_hot(ids, STEP, start)
        high, low = rel_parts(start)
        w_ref[...] += dot(high, pick) + dot(low, pick)

    steps(RELP, STEP, gather)
    s_re, s_im = load_ref[0:HALF, :], load_ref[HALF:DIM, :]
    w_re, w_im = w_ref[0:HALF, :], w_ref[HALF:DIM, :]
    multiply(s_re, s_im, w_re, w_im, False, q_ref, slice(None))
    product = q_ref[...]
    qh_ref[...], ql_ref[...] = halves(product)
    target = load_ref[ID_ROW : ID_ROW + 8, :].T[:, 1:2].astype(jnp.int32)
    target_ref[...] = jnp.broadcast_to(target, (wide, BLOCK))
    turned = halves(product.T)

    def score(start):
        lanes = pl.ds(start, STEP)
        score_ref[:, lanes] = dot3(turned, (high_ref[:, lanes], low_ref[:, lanes]))

    steps(ROWS, STEP, score)

    def weigh(start):
        edges = pl.ds(start, BLOCK)
        for tile in range(ROWS // BLOCK):
            lanes = slice(tile * BLOCK, (tile + 1) * BLOCK)
            times = load_ref[HIST_ROW + tile : HIST_ROW + tile + 1, edges] * (1.0 / NEG)
            value = weights(score_ref[edges, lanes], times, target_ref[edges, :], tile * BLOCK)
            wh_ref[edges, lanes], wl_ref[edges, lanes] = halves(value)

    steps(wide, BLOCK, weigh)

    def backward(start):
        edges = pl.ds(start, STEP)
        parts = wh_ref[edges, :], wl_ref[edges, :]
        back_ref[:, edges] = dot3((high_ref[...], low_ref[...]), parts, NT)

    steps(wide, STEP, backward)

    def table(start):
        lanes = pl.ds(start, STEP)
        parts = wh_ref[:, lanes], wl_ref[:, lanes]
        grad_ref[:, lanes] = dot3((qh_ref[...], ql_ref[...]), parts)

    steps(ROWS, STEP, table)
    copies = put()
    up_re, up_im = back_ref[0:HALF, :], back_ref[HALF:DIM, :]
    lanes = slice(first, first + wide)
    multiply(up_re, up_im, s_re, s_im, True, rg_ref, lanes)
    multiply(up_re, up_im, w_re, w_im, True, sg_out, lanes)
    return copies


def relation_grad(core, rg_ref, ids, flat, send_out, keep_out):
    high, low = halves(rg_ref[...])

    def scatter(start):
        pick = one_hot(ids, STEP, start)
        grad = dot(high, pick, NT) + dot(low, pick, NT)
        row = pl.multiple_of(start // BLOCK * DIM, 8)
        flat[pl.ds(row, DIM), :] = grad[:, 0:BLOCK]
        flat[pl.ds(row + DIM, DIM), :] = grad[:, BLOCK:STEP]

    steps(RELP, STEP, scatter)
    keep_out[...] = flat[pl.ds(pl.multiple_of(core * SIDE, SIDE), SIDE), :]
    send_out[...] = flat[pl.ds(pl.multiple_of((1 - core) * SIDE, SIDE), SIDE), :]


def join_flat(core, mine_ref, other_ref, flat):
    flat[pl.ds(pl.multiple_of(core * SIDE, SIDE), SIDE), :] = mine_ref[...]
    flat[pl.ds(pl.multiple_of((1 - core) * SIDE, SIDE), SIDE), :] = other_ref[...]


def adagrad(table, state, grad):
    state = state + jnp.sum(grad * grad, axis=0, keepdims=True) * (1.0 / DIM)
    return table - grad * (RATE / jnp.sqrt(state)), state


def parts_of(high_ref, low_ref):
    def parts(start):
        return high_ref[:, pl.ds(start, STEP)], low_ref[:, pl.ds(start, STEP)]

    return parts


def entities_of(store, plane):
    return store.at[plane, :, 0:ROWS]


def first_piece(
    load_ref, high_ref, low_ref, rel_high, rel_low, _, sg_out, rg_out, store, *work
):
    work, grad_ref, sem = work[:-2], work[-2], work[-1]

    def put():
        return fetch(sem, (grad_ref, entities_of(store, GRAD)))

    parts = parts_of(rel_high, rel_low)
    copies = edge_terms(load_ref, high_ref, low_ref, parts, work, grad_ref, sg_out, rg_out, 0, put)
    for copy in copies:
        copy.wait()


def second_piece(
    core_ref,
    early_ref,
    load_ref,
    high_ref,
    low_ref,
    rel_high,
    rel_low,
    sg_ref,
    rg_ref,
    _,
    sg_out,
    send,
    keep,
    store,
    *work,
):
    work, rg, flat, grad_ref, g_ref, sem = work[:-5], *work[-5:]
    (g_copy,) = fetch(sem, (entities_of(store, GRAD), g_ref))

    def put():
        g_copy.wait()
        grad_ref[...] += g_ref[...]
        return fetch(sem, (grad_ref, entities_of(store, GRAD)))

    parts = parts_of(rel_high, rel_low)
    sg_out[:, 0:EARLY] = sg_ref[...]
    rg[:, 0:EARLY] = rg_ref[...]
    copies = edge_terms(
        load_ref, high_ref, low_ref, parts, work, grad_ref, sg_out, rg, EARLY, put
    )
    row = slice(ID_ROW, ID_ROW + 1)
    ids = jnp.concatenate([early_ref[row, :], load_ref[row, :]], axis=1).astype(jnp.int32)
    relation_grad(core_ref[0], rg, ids, flat, send, keep)
    for copy in copies:
        copy.wait()


def step_relations(core, mine_ref, other_ref, rel_ref, state_ref, flat, rel_out, state_out):
    join_flat(core, mine_ref, other_ref, flat)

    def step(start):
        lanes = pl.ds(start, BLOCK)
        row = pl.multiple_of(start // BLOCK * DIM, 8)
        rel_out[:, lanes], state_out[:, lanes] = adagrad(
            rel_ref[:, lanes], state_ref[:, lanes], flat[pl.ds(row, DIM), :]
        )

    steps(TILES * BLOCK, BLOCK, step)
    rest = slice(TILES * BLOCK, RELP)
    rel_out[:, rest] = jnp.zeros((DIM, RELP - TILES * BLOCK), F32)
    state_out[:, rest] = state_ref[:, rest]


def second_round(
    core_ref,
    mine_ref,
    other_ref,
    state_ref,
    load_ref,
    _,
    sg_out,
    send,
    keep,
    state_out,
    store,
    *work,
):
    work, rg, flat, old_ref, rel_ref, high_ref, low_ref, grad_ref, sem = work[:-8], *work[-8:]
    rel_copy, table_copy = fetch(
        sem, (store.at[RELATION], old_ref), (entities_of(store, TABLE), grad_ref)
    )
    core = core_ref[0]
    rel_copy.wait()
    step_relations(core, mine_ref, other_ref, old_ref, state_ref, flat, rel_ref, state_out)
    (rel_copy,) = fetch(sem, (rel_ref, store.at[RELATION]))
    table_copy.wait()
    high_ref[...], low_ref[...] = halves(grad_ref[...])

    def parts(start):
        return halves(rel_ref[:, pl.ds(start, STEP)])

    def put():
        return fetch(sem.at[1:2], (grad_ref, entities_of(store, GRAD)))

    copies = edge_terms(load_ref, high_ref, low_ref, parts, work, grad_ref, sg_out, rg, 0, put)
    ids = load_ref[ID_ROW : ID_ROW + 1, :].astype(jnp.int32)
    relation_grad(core, rg, ids, flat, send, keep)
    for copy in [rel_copy, *copies]:
        copy.wait()


def step_entities(table_ref, state_ref, grad_ref, back_ref, edges_ref, count, which):
    pick = one_hot(live_sources(edges_ref, count, which), ROWS)
    high, low = halves(back_ref[...])
    grad = grad_ref[...] + (dot(high, pick, NT) + dot(low, pick, NT))
    return adagrad(table_ref[...], state_ref[...], grad)


def between(
    counts_ref,
    table_hbm,
    state_ref,
    _,
    back_hbm,
    edges_hbm,
    negatives_hbm,
    state_out,
    store,
    load,
    table_ref,
    grad_ref,
    back_ref,
    edges_ref,
    negatives_ref,
    sem,
):
    copies = fetch(
        sem,
        (edges_hbm, edges_ref),
        (back_hbm, back_ref),
        (entities_of(store, GRAD), grad_ref),
        (table_hbm, table_ref),
        (negatives_hbm, negatives_ref),
    )
    for copy in copies:
        copy.wait()
    table, state_out[...] = step_entities(
        table_ref, state_ref, grad_ref, back_ref, edges_ref, counts_ref[0, 0], 0
    )
    table_ref[...] = table
    (copy,) = fetch(sem, (table_ref, entities_of(store, TABLE)))
    write_payload((load,), halves(table), edges_ref, negatives_ref, counts_ref[0, 1], 1)
    copy.wait()


def last_entities(
    counts_ref,
    state_ref,
    store,
    back_hbm,
    edges_hbm,
    table_out,
    state_out,
    table_ref,
    grad_ref,
    back_ref,
    edges_ref,
    sem,
):
    copies = fetch(
        sem,
        (edges_hbm, edges_ref),
        (back_hbm, back_ref),
        (entities_of(store, GRAD), grad_ref),
        (entities_of(store, TABLE), table_ref),
    )
    for copy in copies:
        copy.wait()
    table, state_out[...] = step_entities(
        table_ref, state_ref, grad_ref, back_ref, edges_ref, counts_ref[0, 1], 1
    )
    table_ref[...] = table
    (copy,) = fetch(sem, (table_ref, table_out))
    copy.wait()


def last_relations(
    core_ref,
    mine_ref,
    other_ref,
    store,
    state_ref,
    rel_out,
    state_out,
    flat,
    old_ref,
    rel,
    state,
    sem,
):
    (copy,) = fetch(sem, (store.at[RELATION], old_ref))
    copy.wait()
    step_relations(core_ref[0], mine_ref, other_ref, old_ref, state_ref, flat, rel, state)
    rel_out[...] = rel[:, 0:REL]
    state_out[...] = state[:, 0:REL]


def work_shapes(wide):
    return [
        pltpu.VMEM((DIM, wide), F32),
        pltpu.VMEM((DIM, wide), F32),
        pltpu.VMEM((DIM, wide), BF16),
        pltpu.VMEM((DIM, wide), BF16),
        pltpu.VMEM((wide, ROWS), F32),
        pltpu.VMEM((wide, ROWS), BF16),
        pltpu.VMEM((wide, ROWS), BF16),
        pltpu.VMEM((DIM, wide), F32),
        pltpu.VMEM((wide, BLOCK), jnp.int32),
    ]


SPECS = {"s": SMEM, "v": VMEM, "h": HBM}


def call(body, ins, outs, operands, scratch=(), copies=0, grant=48 << 20, alias=None):
    scratch = list(scratch) + ([pltpu.SemaphoreType.DMA((copies,))] if copies else [])
    return pl.pallas_call(
        body,
        out_shape=[out for _, out in outs],
        in_specs=[SPECS[kind] for kind in ins],
        out_specs=[SPECS[kind] for kind, _ in outs],
        scratch_shapes=scratch,
        input_output_aliases=alias or {},
        compiler_params=params(grant),
    )(*operands)


def across(value, axis, apart):
    count = lax.axis_size(axis)
    return lax.ppermute(value, axis, [(i, i ^ apart) for i in range(count)])


def total(send, keep):
    part = (keep + across(send, C, 1)).reshape(16, SIDE // 16, 128)
    part = lax.all_to_all(part, (X, Y), 0, 0, tiled=True).sum(axis=0)
    part = jnp.broadcast_to(part[None], (8, *part.shape))
    part = lax.all_to_all(part, Z, 0, 0, tiled=True).sum(axis=0)
    part = jnp.broadcast_to(part[None], (16, *part.shape))
    part = lax.all_to_all(part, (X, Y), 0, 0, tiled=True)
    mine = part.reshape(SIDE, 128)
    return mine, across(mine, C, 1)


def body(entities, entity_state, relations, relation_state, edges, negatives, counts):
    core = lax.axis_index(C).astype(jnp.int32).reshape(1)
    table, rel, counts = entities.T, relations.T, counts.T
    edges = edges.transpose(1, 0, 2)
    state = entity_state.reshape(1, ROWS)
    late = EDGES - EARLY
    grown = shape(DIM, ROWS)
    narrow = shape(DIM, ROWS, dtype=BF16)
    wide_rel = shape(DIM, RELP, dtype=BF16)
    vmem = pltpu.VMEM
    table_mem, narrow_mem = vmem((DIM, ROWS), F32), vmem((DIM, ROWS), BF16)
    flat_mem = vmem((RELP // BLOCK * DIM, 128), F32)
    back_mem, rel_mem = vmem((DIM, EDGES), F32), vmem((DIM, RELP), F32)
    edge_mem, negative_mem = vmem((3, 2, EDGES), jnp.int32), vmem(negatives.shape, jnp.int32)
    high, low, first, second = call(
        prepare,
        "shhh",
        [("h", narrow), ("h", narrow), ("h", shape(LOAD, EARLY)), ("h", shape(LOAD, late))],
        (counts, table, edges, negatives),
        [table_mem, edge_mem, negative_mem, narrow_mem, narrow_mem]
        + [vmem((LOAD, EARLY), F32), vmem((LOAD, late), F32)],
        4,
        63 << 20,
    )
    first = across(first, Z, 4)
    second = across(second, Z, 4)
    store_out = ("h", shape(STORE, DIM, RELP))
    store, rel_state, rel_high, rel_low = call(
        pad_relations,
        "vv",
        [store_out, ("v", shape(1, RELP)), ("v", wide_rel), ("v", wide_rel)],
        (rel, relation_state.reshape(1, REL)),
        [rel_mem],
        1,
    )
    piece = ("v", shape(DIM, EARLY))
    back, rel_terms, store = call(
        first_piece,
        "vvvvvh",
        [piece, piece, store_out],
        (first, high, low, rel_high, rel_low, store),
        work_shapes(EARLY) + [table_mem],
        1,
        alias={5: 2},
    )
    half = ("v", shape(SIDE, 128))
    back, send, keep, store = call(
        second_piece,
        "svvvvvvvvh",
        [("v", shape(DIM, EDGES)), half, half, store_out],
        (core, first, second, high, low, rel_high, rel_low, back, rel_terms, store),
        work_shapes(late) + [back_mem, flat_mem, table_mem, table_mem],
        1,
        alias={9: 3},
    )
    back = across(back, Z, 4)
    mine, other = total(send, keep)
    state, store, load = call(
        between,
        "shvhhhh",
        [("v", shape(1, ROWS)), store_out, ("v", shape(LOAD, EDGES))],
        (counts, table, state, store, back, edges, negatives),
        [table_mem, table_mem, back_mem, edge_mem, negative_mem],
        5,
        63 << 20,
        {3: 1},
    )
    load = across(load, C, 1)
    back, send, keep, rel_state, store = call(
        second_round,
        "svvvvh",
        [("v", shape(DIM, EDGES)), half, half, ("v", shape(1, RELP)), store_out],
        (core, mine, other, rel_state, load, store),
        work_shapes(EDGES)
        + [back_mem, flat_mem, rel_mem, rel_mem, narrow_mem, narrow_mem, table_mem],
        2,
        alias={5: 4},
    )
    back = across(back, C, 1)
    mine, other = total(send, keep)
    table, state = call(
        last_entities,
        "svhhh",
        [("h", grown), ("v", shape(1, ROWS))],
        (counts, state, store, back, edges),
        [table_mem, table_mem, back_mem, edge_mem],
        4,
        63 << 20,
    )
    rel, rel_state = call(
        last_relations,
        "svvhv",
        [("v", shape(DIM, REL)), ("v", shape(1, REL))],
        (core, mine, other, store, rel_state),
        [flat_mem, rel_mem, rel_mem, vmem((1, RELP), F32)],
        1,
    )
    return table.T, state.reshape(ROWS), rel.T, rel_state.reshape(REL)


def solution(mesh):
    finer = Mesh(mesh.devices.reshape(8, 4, 4, 2), DOM)
    return jax.shard_map(
        body,
        mesh=finer,
        in_specs=(
            P(DOM, None),
            P(DOM),
            P(),
            P(),
            P(None, None, DOM),
            P(None, DOM, None),
            P(None, DOM),
        ),
        out_specs=(P(DOM, None), P(DOM), P(), P()),
        check_vma=False,
    )
```

time: 191 us -> 195 us (1.021)
  Pallas kernels: 33.5 us -> 46.3 us
  local copies, waits for them, and re-layouts: 11.3 us -> 6.39 us
  waiting for transfers between devices: 24.2 us -> 20.2 us
    pallas_call x8, Pallas kernels: 33.5 us -> 46.3 us  [call(): pl.pallas_call(body, out_shape=[out for _, out in outs], in_specs=[SPECS[...]
    unnamed x26 -> x10, local copies, waits for them, and re-layouts: 9.7 us -> 4.75 us
    ppermute x9, waiting for transfers between devices: 16.9 us -> 12.9 us  [across(): return lax.ppermute(value, axis, [(i, i ^ apart) for i in range(count)])]
  transfers between devices with their start and end apart: 10 -> 10, of which waited for: 7 -> 7; matrix products, arithmetic and copies ran while one was open for 0% -> 0% of each run, Pallas kernels for 8% -> 9%
where the time goes in v2:
time: 195 us; the launch traced here: 194 us
  blocking collectives  87 us (45%)
  Pallas kernels  46.3 us (24%)
  starting transfers between devices  32.8 us (17%)
  waiting for transfers between devices  20.2 us (10%)
  local copies, waits for them, and re-layouts  6.39 us (3%)
    pallas_call x8, Pallas kernels, call(): pl.pallas_call(body, out_shape=[out for _, out in outs], in_specs=[SPECS[...  46.3 us
    all_to_all x2, blocking collectives, total(): part = lax.all_to_all(part, Z, 0, 0, tiled=True).sum(axis=0)  38.1 us
    all_to_all x2, blocking collectives, total(): part = lax.all_to_all(part, (X, Y), 0, 0, tiled=True).sum(axis=0)  36 us
    ppermute x9, starting transfers between devices, across(): return lax.ppermute(value, axis, [(i, i ^ apart) for i in range(count)])  29 us
    ppermute x9, waiting for transfers between devices, across(): return lax.ppermute(value, axis, [(i, i ^ apart) for i in range(count)])  12.9 us
    all_to_all x1, blocking collectives, total(): part = lax.all_to_all(part, (X, Y), 0, 0, tiled=True)  12.9 us
    all_to_all x1, waiting for transfers between devices, total(): part = lax.all_to_all(part, (X, Y), 0, 0, tiled=True)  7.22 us
    unnamed x10, local copies, waits for them, and re-layouts  4.75 us
  transfers between devices with their start and end apart: 10, of which 7 were waited for; matrix products, arithmetic and copies ran while one was open for 0% of the time, Pallas kernels for 9%

profile of v2, /device:TPU:1, one launch (start us, length us, event | category | flops | bytes accessed | tf_op | source)
XLA Modules:
  0.0 194.3 jit_solution(1055405691937829073)
XLA Ops:
  0.6 3.7 %shard_map.102 = (bf16[200,1024]{1,0:T(8,128)(2,1)}, bf16[200,1024]{1,0:T(8,128)(2,1)}, f32[216,256]{1,0:T(8,128)}, f32[216,256]{1,0:T(8,128)}) custom-call(s32[1,2]{1,0:T(1,128)} %bitcast.25, f32[200,1024]{1,0:T(8,128)} %bitcast.18, s32[3,2,512]{2,1,0:T(2,128)} %bitcast.22, s32[2,4,1000]{2,1,0:T(4,128)} %negatives_hbm.3), custom_call_target="tpu_custom_call" | custom-call | tf_op jit(solution)/shard_map/pallas_call | solution.py:495
  4.3 7.8 %collective-permute-start = (f32[216,256]{1,0:T(8,128)}, f32[216,256]{1,0:T(8,128)S(1)}, u32[]{:S(2)}, u32[]{:S(2)}) collective-permute-start(f32[216,256]{1,0:T(8,128)} %get-tuple-element.31), channel_id=1, source_target_pairs={{0,128},{32,160},{64,192},{96,224},{128,0},{160,32},{192,64},{224,... | collective-permute-start | bytes 663560 | tf_op jit(solution)/shard_map/ppermute | solution.py:508
  12.1 0.1 collective-permute-start.1
  12.2 0.7 reshape.41.state_ref
  12.9 0.0 copy-start.2
  12.9 1.2 copy-done.2
  14.2 1.1 shard_map.103
  15.3 1.7 collective-permute-done.load_ref.early_ref
  17.0 0.0 copy-start
  17.0 1.0 copy-done
  18.0 0.0 copy-start.1
  18.0 1.0 copy-done.1
  19.0 6.1 %shard_map.104 = (f32[200,256]{1,0:T(8,128)S(1)}, f32[200,256]{1,0:T(8,128)S(1)}, f32[18,200,1536]{2,1,0:T(8,128)}) custom-call(f32[216,256]{1,0:T(8,128)S(1)} %collective-permute-done.load_ref.early_ref, bf16[200,1024]{1,0:T(8,128)(2,1)S(1)} %copy-done, bf16[200,1024]{1,0:T(8,128)(2,1)S(1)} %copy-done.1, ...), custom_call_target="tpu_custom_call", output_to_operand_aliasing={{2}: (5, {})} | custom-call | tf_op jit(solution)/shard_map/pallas_call | solution.py:495
  25.1 0.0 collective-permute-done.1.load_ref
  25.1 7.5 %shard_map.105 = (f32[200,512]{1,0:T(8,128)S(1)}, f32[1152,128]{1,0:T(8,128)S(1)}, f32[1152,128]{1,0:T(8,128)S(1)}, f32[18,200,1536]{2,1,0:T(8,128)}) custom-call(s32[1]{0:T(128)} %bitcast.3.core_ref, f32[216,256]{1,0:T(8,128)S(1)} %collective-permute-done.load_ref.early_ref, ...), custom_call_target="tpu_custom_call", output_to_operand_aliasing={{3}: (9, {})} | custom-call | tf_op jit(solution)/shard_map/pallas_call | solution.py:495
  32.7 3.3 %collective-permute-start.3 = (f32[1152,128]{1,0:T(8,128)S(1)}, f32[1152,128]{1,0:T(8,128)S(1)}, u32[]{:S(2)}, u32[]{:S(2)}) collective-permute-start(f32[1152,128]{1,0:T(8,128)S(1)} %get-tuple-element.45), channel_id=1, source_target_pairs={{0,1},{1,0},{2,3},{3,2},{4,5},{5,4},{6,7},{7,6},{8,9},{9,8},{10,11... | collective-permute-start | bytes 1769480 | tf_op jit(solution)/shard_map/ppermute | solution.py:508
  36.0 1.6 collective-permute-done.3
  37.6 0.1 add.6
  37.7 18.1 %all_to_all.30 = f32[16,72,128]{2,1,0:T(8,128)S(1)} all-to-all(f32[16,72,128]{2,1,0:T(8,128)S(1)} %bitcast.20), channel_id=1, replica_groups=mesh['z'=8,'x'=4,'y'=4,'c'=2] {'x','y'}, dimensions={0} | all-to-all | bytes 1179648 | tf_op jit(solution)/shard_map/all_to_all | solution.py:513
  55.8 24.2 %all_to_all.31 = f32[8,72,128]{2,1,0:T(8,128)S(1)} all-to-all(f32[8,72,128]{2,1,0:T(8,128)S(1)} %broadcast_in_dim.8), channel_id=1, replica_groups=mesh['z'=8,'x'=4,'y'=4,'c'=2] {'z'}, dimensions={0} | all-to-all | bytes 589824 | tf_op jit(solution)/shard_map/all_to_all | solution.py:515
  80.1 0.9 broadcast_in_dim.9
  80.9 3.8 %all-to-all-start.2 = ((f32[16,72,128]{2,1,0:T(8,128)}), f32[16,72,128]{2,1,0:T(8,128)S(1)}, u32[]{:S(2)}, u32[]{:S(2)}) async-start(f32[16,72,128]{2,1,0:T(8,128)} %broadcast_in_dim.9), calls=%async_computation.2 | async-start | bytes 1179648 | tf_op jit(solution)/shard_map/all_to_all | solution.py:517
  84.7 2.1 %collective-permute-start.2 = (f32[200,512]{1,0:T(8,128)S(1)}, f32[200,512]{1,0:T(8,128)S(1)}, u32[]{:S(2)}, u32[]{:S(2)}) collective-permute-start(f32[200,512]{1,0:T(8,128)S(1)} %get-tuple-element.42), channel_id=1, source_target_pairs={{0,128},{32,160},{64,192},{96,224},{128,0},{160,32},{192,64},{224,... | collective-permute-start | bytes 1228808 | tf_op jit(solution)/shard_map/ppermute | solution.py:508
  86.8 7.2 %all-to-all-done.2 = f32[16,72,128]{2,1,0:T(8,128)S(1)} async-done(((f32[16,72,128]{2,1,0:T(8,128)}), f32[16,72,128]{2,1,0:T(8,128)S(1)}, u32[]{:S(2)}, u32[]{:S(2)}) %all-to-all-start.2) | async-done | bytes 589856 | tf_op jit(solution)/shard_map/all_to_all | solution.py:517
  94.1 4.6 %collective-permute-start.4 = (f32[1152,128]{1,0:T(8,128)S(1)}, f32[1152,128]{1,0:T(8,128)}, u32[]{:S(2)}, u32[]{:S(2)}) collective-permute-start(f32[1152,128]{1,0:T(8,128)S(1)} %bitcast.15), channel_id=1, source_target_pairs={{0,1},{1,0},{2,3},{3,2},{4,5},{5,4},{6,7},{7,6},{8,9},{9,8},{10,11... | collective-permute-start | bytes 1769480 | tf_op jit(solution)/shard_map/ppermute | solution.py:508
  98.6 4.1 %collective-permute-done.2.back_hbm = f32[200,512]{1,0:T(8,128)S(1)} collective-permute-done((f32[200,512]{1,0:T(8,128)S(1)}, f32[200,512]{1,0:T(8,128)S(1)}, u32[]{:S(2)}, u32[]{:S(2)}) %collective-permute-start.2) | collective-permute-done | bytes 409632 | tf_op jit(solution)/shard_map/ppermute | solution.py:508
  102.8 0.0 copy-start.3
  102.8 0.7 copy-done.3
  103.5 5.3 %shard_map.106 = (f32[1,1024]{1,0:T(1,128)}, f32[18,200,1536]{2,1,0:T(8,128)}, f32[216,512]{1,0:T(8,128)}) custom-call(s32[1,2]{1,0:T(1,128)} %bitcast.26, f32[200,1024]{1,0:T(8,128)} %bitcast.19, f32[1,1024]{1,0:T(1,128)} %bitcast.28, f32[18,200,1536]{2,1,0:T(8,128)} %get-tuple-element.41._, f32[200,512]{1,0:T(8,128)} %copy-done.3, ...), custom_call_target="tpu_custom_call", output_to_operand_aliasing={{1}: (3, {})} | custom-call | tf_op jit(solution)/shard_map/pallas_call | solution.py:495
  108.8 6.0 %collective-permute-start.5 = (f32[216,512]{1,0:T(8,128)}, f32[216,512]{1,0:T(8,128)S(1)}, u32[]{:S(2)}, u32[]{:S(2)}) collective-permute-start(f32[216,512]{1,0:T(8,128)} %get-tuple-element.47), channel_id=1, source_target_pairs={{0,1},{1,0},{2,3},{3,2},{4,5},{5,4},{6,7},{7,6},{8,9},{9,8},{10,11... | collective-permute-start | bytes 1327112 | tf_op jit(solution)/shard_map/ppermute | solution.py:508
  114.9 1.6 collective-permute-done.5.load_ref
  116.5 0.0 collective-permute-done.4.other_ref
  116.5 13.6 %shard_map.107 = (f32[200,512]{1,0:T(8,128)S(1)}, f32[1152,128]{1,0:T(8,128)S(1)}, f32[1152,128]{1,0:T(8,128)S(1)}, f32[1,1536]{1,0:T(1,128)S(1)}, f32[18,200,1536]{2,1,0:T(8,128)}) custom-call(s32[1]{0:T(128)} %bitcast.3.core_ref, f32[1152,128]{1,0:T(8,128)S(1)} %bitcast.16, ...), custom_call_target="tpu_custom_call", output_to_operand_aliasing={{4}: (5, {})} | custom-call | tf_op jit(solution)/shard_map/pallas_call | solution.py:495
  130.0 0.5 collective-permute-start.7
  130.5 1.6 collective-permute-done.7
  132.1 0.1 add.7
  132.2 17.9 %all_to_all.32 = f32[16,72,128]{2,1,0:T(8,128)S(1)} all-to-all(f32[16,72,128]{2,1,0:T(8,128)S(1)} %bitcast.21), channel_id=1, replica_groups=mesh['z'=8,'x'=4,'y'=4,'c'=2] {'x','y'}, dimensions={0} | all-to-all | bytes 1179648 | tf_op jit(solution)/shard_map/all_to_all | solution.py:513
  150.2 13.8 %all_to_all.33 = f32[8,72,128]{2,1,0:T(8,128)S(1)} all-to-all(f32[8,72,128]{2,1,0:T(8,128)S(1)} %broadcast_in_dim.10), channel_id=1, replica_groups=mesh['z'=8,'x'=4,'y'=4,'c'=2] {'z'}, dimensions={0} | all-to-all | bytes 589824 | tf_op jit(solution)/shard_map/all_to_all | solution.py:515
  164.1 12.9 %all_to_all.34 = f32[16,72,128]{2,1,0:T(8,128)S(1)} all-to-all(f32[16,72,128]{2,1,0:T(8,128)S(1)} %broadcast_in_dim.11), channel_id=1, replica_groups=mesh['z'=8,'x'=4,'y'=4,'c'=2] {'x','y'}, dimensions={0} | all-to-all | bytes 1179648 | tf_op jit(solution)/shard_map/all_to_all | solution.py:517
  177.0 4.6 %collective-permute-start.8 = (f32[1152,128]{1,0:T(8,128)S(1)}, f32[1152,128]{1,0:T(8,128)}, u32[]{:S(2)}, u32[]{:S(2)}) collective-permute-start(f32[1152,128]{1,0:T(8,128)S(1)} %bitcast.13), channel_id=1, source_target_pairs={{0,1},{1,0},{2,3},{3,2},{4,5},{5,4},{6,7},{7,6},{8,9},{9,8},{10,11... | collective-permute-start | bytes 1769480 | tf_op jit(solution)/shard_map/ppermute | solution.py:508
  181.6 0.0 collective-permute-start.6
  181.6 2.2 %collective-permute-done.6.back_hbm = f32[200,512]{1,0:T(8,128)S(1)} collective-permute-done((f32[200,512]{1,0:T(8,128)S(1)}, f32[200,512]{1,0:T(8,128)S(1)}, u32[]{:S(2)}, u32[]{:S(2)}) %collective-permute-start.6) | collective-permute-done | bytes 409632 | tf_op jit(solution)/shard_map/ppermute | solution.py:508
  183.8 0.0 copy-start.4
  183.8 0.7 copy-done.4
  184.6 4.8 %shard_map.108 = (f32[200,1024]{1,0:T(8,128)}, f32[1,1024]{1,0:T(1,128)}) custom-call(s32[1,2]{1,0:T(1,128)} %bitcast.27, f32[1,1024]{1,0:T(1,128)} %get-tuple-element.43.state_ref, f32[18,200,1536]{2,1,0:T(8,128)} %get-tuple-element.49.store, f32[200,512]{1,0:T(8,128)} %copy-done.4, s32[3,2,512]{2,1,0:T(2,128)} %bitcast.24), custom_call_target="tpu_custom_call" | custom-call | tf_op jit(solution)/shard_map/pallas_call | solution.py:495
  189.4 0.0 collective-permute-done.8.other_ref
  189.4 4.2 %shard_map.109 = (f32[200,1345]{1,0:T(8,128)}, f32[1,1345]{1,0:T(1,128)S(1)}) custom-call(s32[1]{0:T(128)} %bitcast.3.core_ref, f32[1152,128]{1,0:T(8,128)S(1)} %bitcast.14, f32[1152,128]{1,0:T(8,128)} %collective-permute-done.8.other_ref, f32[18,200,1536]{2,1,0:T(8,128)} %get-tuple-element.49.store, f32[1,1536]{1,0:T(1,128)S(1)} %get-tuple-element.55.state_ref), custom_call_target="tpu_custom_call" | custom-call | tf_op jit(solution)/shard_map/pallas_call | solution.py:495
  193.7 0.6 reduce
  (7 shorter events, 0.2 us)
Async XLA Ops:
  4.3 12.7 %collective-permute-start = (f32[216,256]{1,0:T(8,128)}, f32[216,256]{1,0:T(8,128)S(1)}, u32[]{:S(2)}, u32[]{:S(2)}) collective-permute-start(f32[216,256]{1,0:T(8,128)} %get-tuple-element.31), channel_id=1, source_target_pairs={{0,128},{32,160},{64,192},{96,224},{128,0},{160,32},{192,64},{224,... | collective-permute-start | bytes 663560 | tf_op jit(solution)/shard_map/ppermute | solution.py:508
  12.1 13.0 %collective-permute-start.1 = (f32[216,256]{1,0:T(8,128)}, f32[216,256]{1,0:T(8,128)S(1)}, u32[]{:S(2)}, u32[]{:S(2)}) collective-permute-start(f32[216,256]{1,0:T(8,128)} %get-tuple-element.32), channel_id=1, source_target_pairs={{0,128},{32,160},{64,192},{96,224},{128,0},{160,32},{192,64},{224,... | collective-permute-start | bytes 663560 | tf_op jit(solution)/shard_map/ppermute | solution.py:508
  12.9 1.3 copy-start.2
  17.0 1.0 copy-start
  18.0 1.0 copy-start.1
  32.7 5.0 %collective-permute-start.3 = (f32[1152,128]{1,0:T(8,128)S(1)}, f32[1152,128]{1,0:T(8,128)S(1)}, u32[]{:S(2)}, u32[]{:S(2)}) collective-permute-start(f32[1152,128]{1,0:T(8,128)S(1)} %get-tuple-element.45), channel_id=1, source_target_pairs={{0,1},{1,0},{2,3},{3,2},{4,5},{5,4},{6,7},{7,6},{8,9},{9,8},{10,11... | collective-permute-start | bytes 1769480 | tf_op jit(solution)/shard_map/ppermute | solution.py:508
  80.9 13.2 %all-to-all-start.2 = ((f32[16,72,128]{2,1,0:T(8,128)}), f32[16,72,128]{2,1,0:T(8,128)S(1)}, u32[]{:S(2)}, u32[]{:S(2)}) async-start(f32[16,72,128]{2,1,0:T(8,128)} %broadcast_in_dim.9), calls=%async_computation.2 | async-start | bytes 1179648 | tf_op jit(solution)/shard_map/all_to_all | solution.py:517
  84.7 18.1 %collective-permute-start.2 = (f32[200,512]{1,0:T(8,128)S(1)}, f32[200,512]{1,0:T(8,128)S(1)}, u32[]{:S(2)}, u32[]{:S(2)}) collective-permute-start(f32[200,512]{1,0:T(8,128)S(1)} %get-tuple-element.42), channel_id=1, source_target_pairs={{0,128},{32,160},{64,192},{96,224},{128,0},{160,32},{192,64},{224,... | collective-permute-start | bytes 1228808 | tf_op jit(solution)/shard_map/ppermute | solution.py:508
  94.1 22.4 %collective-permute-start.4 = (f32[1152,128]{1,0:T(8,128)S(1)}, f32[1152,128]{1,0:T(8,128)}, u32[]{:S(2)}, u32[]{:S(2)}) collective-permute-start(f32[1152,128]{1,0:T(8,128)S(1)} %bitcast.15), channel_id=1, source_target_pairs={{0,1},{1,0},{2,3},{3,2},{4,5},{5,4},{6,7},{7,6},{8,9},{9,8},{10,11... | collective-permute-start | bytes 1769480 | tf_op jit(solution)/shard_map/ppermute | solution.py:508
  102.8 0.8 copy-start.3
  108.8 7.6 %collective-permute-start.5 = (f32[216,512]{1,0:T(8,128)}, f32[216,512]{1,0:T(8,128)S(1)}, u32[]{:S(2)}, u32[]{:S(2)}) collective-permute-start(f32[216,512]{1,0:T(8,128)} %get-tuple-element.47), channel_id=1, source_target_pairs={{0,1},{1,0},{2,3},{3,2},{4,5},{5,4},{6,7},{7,6},{8,9},{9,8},{10,11... | collective-permute-start | bytes 1327112 | tf_op jit(solution)/shard_map/ppermute | solution.py:508
  130.0 2.1 %collective-permute-start.7 = (f32[1152,128]{1,0:T(8,128)S(1)}, f32[1152,128]{1,0:T(8,128)S(1)}, u32[]{:S(2)}, u32[]{:S(2)}) collective-permute-start(f32[1152,128]{1,0:T(8,128)S(1)} %get-tuple-element.54), channel_id=1, source_target_pairs={{0,1},{1,0},{2,3},{3,2},{4,5},{5,4},{6,7},{7,6},{8,9},{9,8},{10,11... | collective-permute-start | bytes 1769480 | tf_op jit(solution)/shard_map/ppermute | solution.py:508
  177.0 12.4 %collective-permute-start.8 = (f32[1152,128]{1,0:T(8,128)S(1)}, f32[1152,128]{1,0:T(8,128)}, u32[]{:S(2)}, u32[]{:S(2)}) collective-permute-start(f32[1152,128]{1,0:T(8,128)S(1)} %bitcast.13), channel_id=1, source_target_pairs={{0,1},{1,0},{2,3},{3,2},{4,5},{5,4},{6,7},{7,6},{8,9},{9,8},{10,11... | collective-permute-start | bytes 1769480 | tf_op jit(solution)/shard_map/ppermute | solution.py:508
  181.6 2.2 %collective-permute-start.6 = (f32[200,512]{1,0:T(8,128)S(1)}, f32[200,512]{1,0:T(8,128)S(1)}, u32[]{:S(2)}, u32[]{:S(2)}) collective-permute-start(f32[200,512]{1,0:T(8,128)S(1)} %get-tuple-element.50), channel_id=1, source_target_pairs={{0,1},{1,0},{2,3},{3,2},{4,5},{5,4},{6,7},{7,6},{8,9},{9,8},{10,11... | collective-permute-start | bytes 1228808 | tf_op jit(solution)/shard_map/ppermute | solution.py:508
  183.8 0.8 copy-start.4

commit v3 on v2

--- a/solution.py
+++ b/solution.py
@@ -16,7 +16,7 @@
 DIM = 200
 HALF = DIM // 2
 REL = 1345
-RELP = 1536
+RELP = 1408
 NEG = 1000
 BLOCK = 128
 STEP = 256
@@ -29,7 +29,6 @@
 HIST_ROW = 208
 FLAT = 2304
 SIDE = FLAT // 2
-TILES = 11
 
 VMEM = pl.BlockSpec(memory_space=pltpu.VMEM)
 SMEM = pl.BlockSpec(memory_space=pltpu.SMEM)
@@ -60,17 +59,9 @@
     return dot(a[0], b[0], dims) + (dot(a[1], b[0], dims) + dot(a[0], b[1], dims))
 
 
-def one_hot(ids, count, first=0):
+def one_hot(ids, count):
     places = lax.broadcasted_iota(jnp.int32, (count, ids.shape[1]), 0)
-    return jnp.where(places == ids - first, 1.0, 0.0).astype(BF16)
-
-
-def steps(count, size, step):
-    def visit(index, carry):
-        step(pl.multiple_of(index * size, size))
-        return carry
-
-    lax.fori_loop(0, count // size, visit, 0)
+    return jnp.where(places == ids, 1.0, 0.0).astype(BF16)
 
 
 def histogram(ids):
@@ -119,15 +110,11 @@
     table_hbm,
     edges_hbm,
     negatives_hbm,
-    high_out,
-    low_out,
     first_out,
     second_out,
     table_ref,
     edges_ref,
     negatives_ref,
-    high_ref,
-    low_ref,
     first_ref,
     second_ref,
     sem,
@@ -137,21 +124,31 @@
     )
     for copy in copies:
         copy.wait()
+    pieces = (first_ref, second_ref)
     parts = halves(table_ref[...])
-    high_ref[...], low_ref[...] = parts
-    copies = fetch(sem, (high_ref, high_out), (low_ref, low_out))
-    pieces = (first_ref, second_ref)
     write_payload(pieces, parts, edges_ref, negatives_ref, counts_ref[0, 0], 0)
-    copies += fetch(sem.at[2:4], (first_ref, first_out), (second_ref, second_out))
-    for copy in copies:
-        copy.wait()
-
-
-def pad_relations(rel_ref, state_ref, rel_out, state_out, high_out, low_out, rel, sem):
+    for copy in fetch(sem, (first_ref, first_out), (second_ref, second_out)):
+        copy.wait()
+
+
+def settle(
+    table_ref,
+    rel_ref,
+    state_ref,
+    store,
+    state_out,
+    rel_high,
+    rel_low,
+    table_high,
+    table_low,
+    rel,
+    sem,
+):
     rel[:, 10 * 128 : RELP] = jnp.zeros((DIM, RELP - 10 * 128), F32)
     rel[:, 0:REL] = rel_ref[...]
-    (copy,) = fetch(sem, (rel, rel_out.at[RELATION]))
-    high_out[...], low_out[...] = halves(rel[...])
+    (copy,) = fetch(sem, (rel, store.at[RELATION]))
+    rel_high[...], rel_low[...] = halves(rel[...])
+    table_high[...], table_low[...] = halves(table_ref[...])
     state_out[...] = jnp.ones((1, RELP), F32)
     state_out[:, 0:REL] = state_ref[...]
     copy.wait()
@@ -177,75 +174,51 @@
     return plus * times - jnp.where(lanes == target, minus, 0.0)
 
 
-def edge_terms(load_ref, high_ref, low_ref, rel_parts, work, grad_ref, sg_out, rg_ref, first, put):
-    w_ref, q_ref, qh_ref, ql_ref, score_ref, wh_ref, wl_ref, back_ref, target_ref = work
+def edge_terms(load_ref, table_parts, rel_parts, work, sg_out, rg_ref, first, put):
+    w_ref, q_ref, score_ref, high_ref, low_ref, back_ref = work
     wide = load_ref.shape[1]
-    ids = load_ref[ID_ROW : ID_ROW + 1, :].astype(jnp.int32)
-    w_ref[...] = jnp.zeros((DIM, wide), F32)
-
-    def gather(start):
-        pick = one_hot(ids, STEP, start)
-        high, low = rel_parts(start)
-        w_ref[...] += dot(high, pick) + dot(low, pick)
-
-    steps(RELP, STEP, gather)
+    pick = one_hot(load_ref[ID_ROW : ID_ROW + 1, :].astype(jnp.int32), RELP)
+    w_ref[...] = dot(rel_parts[0], pick) + dot(rel_parts[1], pick)
     s_re, s_im = load_ref[0:HALF, :], load_ref[HALF:DIM, :]
     w_re, w_im = w_ref[0:HALF, :], w_ref[HALF:DIM, :]
     multiply(s_re, s_im, w_re, w_im, False, q_ref, slice(None))
     product = q_ref[...]
-    qh_ref[...], ql_ref[...] = halves(product)
+    product_parts = halves(product)
     target = load_ref[ID_ROW : ID_ROW + 8, :].T[:, 1:2].astype(jnp.int32)
-    target_ref[...] = jnp.broadcast_to(target, (wide, BLOCK))
     turned = halves(product.T)
-
-    def score(start):
-        lanes = pl.ds(start, STEP)
-        score_ref[:, lanes] = dot3(turned, (high_ref[:, lanes], low_ref[:, lanes]))
-
-    steps(ROWS, STEP, score)
-
-    def weigh(start):
-        edges = pl.ds(start, BLOCK)
-        for tile in range(ROWS // BLOCK):
-            lanes = slice(tile * BLOCK, (tile + 1) * BLOCK)
-            times = load_ref[HIST_ROW + tile : HIST_ROW + tile + 1, edges] * (1.0 / NEG)
-            value = weights(score_ref[edges, lanes], times, target_ref[edges, :], tile * BLOCK)
-            wh_ref[edges, lanes], wl_ref[edges, lanes] = halves(value)
-
-    steps(wide, BLOCK, weigh)
-
-    def backward(start):
-        edges = pl.ds(start, STEP)
-        parts = wh_ref[edges, :], wl_ref[edges, :]
-        back_ref[:, edges] = dot3((high_ref[...], low_ref[...]), parts, NT)
-
-    steps(wide, STEP, backward)
-
-    def table(start):
-        lanes = pl.ds(start, STEP)
-        parts = wh_ref[:, lanes], wl_ref[:, lanes]
-        grad_ref[:, lanes] = dot3((qh_ref[...], ql_ref[...]), parts)
-
-    steps(ROWS, STEP, table)
-    copies = put()
+    spans = [slice(start, min(start + STEP, wide)) for start in range(0, wide, STEP)]
+    for edges in spans:
+        score_ref[edges, :] = dot3((turned[0][edges], turned[1][edges]), table_parts)
+    table_grad = None
+    for span in spans:
+        for block in range(span.start, span.stop, BLOCK):
+            edges = slice(block, block + BLOCK)
+            for tile in range(ROWS // 128):
+                lanes = slice(tile * 128, (tile + 1) * 128)
+                times = load_ref[HIST_ROW + tile : HIST_ROW + tile + 1, edges] * (1.0 / NEG)
+                value = weights(score_ref[edges, lanes], times, target[edges], tile * 128)
+                high_ref[edges, lanes], low_ref[edges, lanes] = halves(value)
+        weight_parts = high_ref[span, :], low_ref[span, :]
+        back_ref[:, span] = dot3(table_parts, weight_parts, NT)
+        part = dot3((product_parts[0][:, span], product_parts[1][:, span]), weight_parts)
+        table_grad = part if table_grad is None else table_grad + part
+    copies = put(table_grad)
     up_re, up_im = back_ref[0:HALF, :], back_ref[HALF:DIM, :]
     lanes = slice(first, first + wide)
     multiply(up_re, up_im, s_re, s_im, True, rg_ref, lanes)
     multiply(up_re, up_im, w_re, w_im, True, sg_out, lanes)
-    return copies
-
-
-def relation_grad(core, rg_ref, ids, flat, send_out, keep_out):
+    return pick, copies
+
+
+def relation_grad(rg_ref, pick):
     high, low = halves(rg_ref[...])
-
-    def scatter(start):
-        pick = one_hot(ids, STEP, start)
-        grad = dot(high, pick, NT) + dot(low, pick, NT)
-        row = pl.multiple_of(start // BLOCK * DIM, 8)
-        flat[pl.ds(row, DIM), :] = grad[:, 0:BLOCK]
-        flat[pl.ds(row + DIM, DIM), :] = grad[:, BLOCK:STEP]
-
-    steps(RELP, STEP, scatter)
+    return dot(high, pick, NT) + dot(low, pick, NT)
+
+
+def split_flat(core, grad, flat, send_out, keep_out):
+    for tile in range(RELP // 128):
+        flat[tile * DIM : (tile + 1) * DIM, :] = grad[:, tile * 128 : (tile + 1) * 128]
+    flat[RELP // 128 * DIM : FLAT, :] = jnp.zeros((FLAT - RELP // 128 * DIM, 128), F32)
     keep_out[...] = flat[pl.ds(pl.multiple_of(core * SIDE, SIDE), SIDE), :]
     send_out[...] = flat[pl.ds(pl.multiple_of((1 - core) * SIDE, SIDE), SIDE), :]
 
@@ -260,13 +233,6 @@
     return table - grad * (RATE / jnp.sqrt(state)), state
 
 
-def parts_of(high_ref, low_ref):
-    def parts(start):
-        return high_ref[:, pl.ds(start, STEP)], low_ref[:, pl.ds(start, STEP)]
-
-    return parts
-
-
 def entities_of(store, plane):
     return store.at[plane, :, 0:ROWS]
 
@@ -276,11 +242,12 @@
 ):
     work, grad_ref, sem = work[:-2], work[-2], work[-1]
 
-    def put():
+    def put(value):
+        grad_ref[...] = value
         return fetch(sem, (grad_ref, entities_of(store, GRAD)))
 
-    parts = parts_of(rel_high, rel_low)
-    copies = edge_terms(load_ref, high_ref, low_ref, parts, work, grad_ref, sg_out, rg_out, 0, put)
+    table_parts, rel_parts = (high_ref[...], low_ref[...]), (rel_high[...], rel_low[...])
+    _, copies = edge_terms(load_ref, table_parts, rel_parts, work, sg_out, rg_out, 0, put)
     for copy in copies:
         copy.wait()
 
@@ -305,38 +272,29 @@
     work, rg, flat, grad_ref, g_ref, sem = work[:-5], *work[-5:]
     (g_copy,) = fetch(sem, (entities_of(store, GRAD), g_ref))
 
-    def put():
+    def put(value):
         g_copy.wait()
-        grad_ref[...] += g_ref[...]
+        grad_ref[...] = value + g_ref[...]
         return fetch(sem, (grad_ref, entities_of(store, GRAD)))
 
-    parts = parts_of(rel_high, rel_low)
+    table_parts, rel_parts = (high_ref[...], low_ref[...]), (rel_high[...], rel_low[...])
     sg_out[:, 0:EARLY] = sg_ref[...]
     rg[:, 0:EARLY] = rg_ref[...]
-    copies = edge_terms(
-        load_ref, high_ref, low_ref, parts, work, grad_ref, sg_out, rg, EARLY, put
-    )
-    row = slice(ID_ROW, ID_ROW + 1)
-    ids = jnp.concatenate([early_ref[row, :], load_ref[row, :]], axis=1).astype(jnp.int32)
-    relation_grad(core_ref[0], rg, ids, flat, send, keep)
+    pick, copies = edge_terms(load_ref, table_parts, rel_parts, work, sg_out, rg, EARLY, put)
+    early = one_hot(early_ref[ID_ROW : ID_ROW + 1, :].astype(jnp.int32), RELP)
+    pick = jnp.concatenate([early, pick], axis=1)
+    split_flat(core_ref[0], relation_grad(rg, pick), flat, send, keep)
     for copy in copies:
         copy.wait()
 
 
 def step_relations(core, mine_ref, other_ref, rel_ref, state_ref, flat, rel_out, state_out):
     join_flat(core, mine_ref, other_ref, flat)
-
-    def step(start):
-        lanes = pl.ds(start, BLOCK)
-        row = pl.multiple_of(start // BLOCK * DIM, 8)
+    for tile in range(RELP // 128):
+        lanes = slice(tile * 128, (tile + 1) * 128)
         rel_out[:, lanes], state_out[:, lanes] = adagrad(
-            rel_ref[:, lanes], state_ref[:, lanes], flat[pl.ds(row, DIM), :]
+            rel_ref[:, lanes], state_ref[:, lanes], flat[tile * DIM : (tile + 1) * DIM, :]
         )
-
-    steps(TILES * BLOCK, BLOCK, step)
-    rest = slice(TILES * BLOCK, RELP)
-    rel_out[:, rest] = jnp.zeros((DIM, RELP - TILES * BLOCK), F32)
-    state_out[:, rest] = state_ref[:, rest]
 
 
 def second_round(
@@ -353,7 +311,7 @@
     store,
     *work,
 ):
-    work, rg, flat, old_ref, rel_ref, high_ref, low_ref, grad_ref, sem = work[:-8], *work[-8:]
+    work, rg, flat, old_ref, rel_ref, grad_ref, sem = work[:-6], *work[-6:]
     rel_copy, table_copy = fetch(
         sem, (store.at[RELATION], old_ref), (entities_of(store, TABLE), grad_ref)
     )
@@ -362,17 +320,15 @@
     step_relations(core, mine_ref, other_ref, old_ref, state_ref, flat, rel_ref, state_out)
     (rel_copy,) = fetch(sem, (rel_ref, store.at[RELATION]))
     table_copy.wait()
-    high_ref[...], low_ref[...] = halves(grad_ref[...])
-
-    def parts(start):
-        return halves(rel_ref[:, pl.ds(start, STEP)])
-
-    def put():
+    table_parts = halves(grad_ref[...])
+
+    def put(value):
+        grad_ref[...] = value
         return fetch(sem.at[1:2], (grad_ref, entities_of(store, GRAD)))
 
-    copies = edge_terms(load_ref, high_ref, low_ref, parts, work, grad_ref, sg_out, rg, 0, put)
-    ids = load_ref[ID_ROW : ID_ROW + 1, :].astype(jnp.int32)
-    relation_grad(core, rg, ids, flat, send, keep)
+    rel_parts = halves(rel_ref[...])
+    pick, copies = edge_terms(load_ref, table_parts, rel_parts, work, sg_out, rg, 0, put)
+    split_flat(core, relation_grad(rg, pick), flat, send, keep)
     for copy in [rel_copy, *copies]:
         copy.wait()
 
@@ -477,13 +433,10 @@
     return [
         pltpu.VMEM((DIM, wide), F32),
         pltpu.VMEM((DIM, wide), F32),
-        pltpu.VMEM((DIM, wide), BF16),
-        pltpu.VMEM((DIM, wide), BF16),
         pltpu.VMEM((wide, ROWS), F32),
         pltpu.VMEM((wide, ROWS), BF16),
         pltpu.VMEM((wide, ROWS), BF16),
         pltpu.VMEM((DIM, wide), F32),
-        pltpu.VMEM((wide, BLOCK), jnp.int32),
     ]
 
 
@@ -529,28 +482,27 @@
     narrow = shape(DIM, ROWS, dtype=BF16)
     wide_rel = shape(DIM, RELP, dtype=BF16)
     vmem = pltpu.VMEM
-    table_mem, narrow_mem = vmem((DIM, ROWS), F32), vmem((DIM, ROWS), BF16)
-    flat_mem = vmem((RELP // BLOCK * DIM, 128), F32)
+    table_mem = vmem((DIM, ROWS), F32)
+    flat_mem = vmem((FLAT, 128), F32)
     back_mem, rel_mem = vmem((DIM, EDGES), F32), vmem((DIM, RELP), F32)
     edge_mem, negative_mem = vmem((3, 2, EDGES), jnp.int32), vmem(negatives.shape, jnp.int32)
-    high, low, first, second = call(
+    first, second = call(
         prepare,
         "shhh",
-        [("h", narrow), ("h", narrow), ("h", shape(LOAD, EARLY)), ("h", shape(LOAD, late))],
+        [("h", shape(LOAD, EARLY)), ("h", shape(LOAD, late))],
         (counts, table, edges, negatives),
-        [table_mem, edge_mem, negative_mem, narrow_mem, narrow_mem]
-        + [vmem((LOAD, EARLY), F32), vmem((LOAD, late), F32)],
-        4,
+        [table_mem, edge_mem, negative_mem, vmem((LOAD, EARLY), F32), vmem((LOAD, late), F32)],
+        3,
         63 << 20,
     )
     first = across(first, Z, 4)
     second = across(second, Z, 4)
     store_out = ("h", shape(STORE, DIM, RELP))
-    store, rel_state, rel_high, rel_low = call(
-        pad_relations,
-        "vv",
-        [store_out, ("v", shape(1, RELP)), ("v", wide_rel), ("v", wide_rel)],
-        (rel, relation_state.reshape(1, REL)),
+    store, rel_state, rel_high, rel_low, high, low = call(
+        settle,
+        "vvv",
+        [store_out, ("v", shape(1, RELP))] + [("v", wide_rel)] * 2 + [("v", narrow)] * 2,
+        (table, rel, relation_state.reshape(1, REL)),
         [rel_mem],
         1,
     )
@@ -593,7 +545,7 @@
         [("v", shape(DIM, EDGES)), half, half, ("v", shape(1, RELP)), store_out],
         (core, mine, other, rel_state, load, store),
         work_shapes(EDGES)
-        + [back_mem, flat_mem, rel_mem, rel_mem, narrow_mem, narrow_mem, table_mem],
+        + [back_mem, flat_mem, rel_mem, rel_mem, table_mem],
         2,
         alias={5: 4},
     )

time: 195 us -> 184 us (0.944)
  Pallas kernels: 46.3 us -> 36.6 us
    pallas_call x8, Pallas kernels: 46.3 us -> 36.6 us  [call(): pl.pallas_call(body, out_shape=[out for _, out in outs], in_specs=[SPECS[...]
    unnamed x10 -> x8, local copies, waits for them, and re-layouts: 4.75 us -> 3.9 us
  transfers between devices with their start and end apart: 10 -> 10, of which waited for: 7 -> 8; matrix products, arithmetic and copies ran while one was open for 0% -> 0% of each run, Pallas kernels for 9% -> 8%
where the time goes in v3:
time: 184 us; the launch traced here: 183 us
  blocking collectives  85.8 us (47%)
  Pallas kernels  36.6 us (20%)
  starting transfers between devices  32 us (17%)
  waiting for transfers between devices  21.1 us (11%)
  local copies, waits for them, and re-layouts  5.53 us (3%)
    all_to_all x2, blocking collectives, total(): part = lax.all_to_all(part, Z, 0, 0, tiled=True).sum(axis=0)  36.9 us
    pallas_call x8, Pallas kernels, call(): pl.pallas_call(body, out_shape=[out for _, out in outs], in_specs=[SPECS[...  36.6 us
    all_to_all x2, blocking collectives, total(): part = lax.all_to_all(part, (X, Y), 0, 0, tiled=True).sum(axis=0)  36 us
    ppermute x9, starting transfers between devices, across(): return lax.ppermute(value, axis, [(i, i ^ apart) for i in range(count)])  28.3 us
    ppermute x9, waiting for transfers between devices, across(): return lax.ppermute(value, axis, [(i, i ^ apart) for i in range(count)])  13.9 us
    all_to_all x1, blocking collectives, total(): part = lax.all_to_all(part, (X, Y), 0, 0, tiled=True)  13 us
    all_to_all x1, waiting for transfers between devices, total(): part = lax.all_to_all(part, (X, Y), 0, 0, tiled=True)  7.22 us
    unnamed x8, local copies, waits for them, and re-layouts  3.9 us
  transfers between devices with their start and end apart: 10, of which 8 were waited for; matrix products, arithmetic and copies ran while one was open for 0% of the time, Pallas kernels for 8%

profile of v3, /device:TPU:1, one launch (start us, length us, event | category | flops | bytes accessed | tf_op | source)
XLA Modules:
  0.0 182.8 jit_solution(16537609216347628695)
XLA Ops:
  0.6 3.5 %shard_map.102 = (f32[216,256]{1,0:T(8,128)}, f32[216,256]{1,0:T(8,128)}) custom-call(s32[1,2]{1,0:T(1,128)} %bitcast.26, f32[200,1024]{1,0:T(8,128)} %bitcast.13, s32[3,2,512]{2,1,0:T(2,128)} %bitcast.23, s32[2,4,1000]{2,1,0:T(4,128)} %negatives_hbm.3), custom_call_target="tpu_custom_call" | custom-call | tf_op jit(solution)/shard_map/pallas_call | solution.py:448
  4.2 7.8 %collective-permute-start = (f32[216,256]{1,0:T(8,128)}, f32[216,256]{1,0:T(8,128)S(1)}, u32[]{:S(2)}, u32[]{:S(2)}) collective-permute-start(f32[216,256]{1,0:T(8,128)} %get-tuple-element.31), channel_id=1, source_target_pairs={{0,128},{32,160},{64,192},{96,224},{128,0},{160,32},{192,64},{224,... | collective-permute-start | bytes 663560 | tf_op jit(solution)/shard_map/ppermute | solution.py:461
  12.0 0.1 collective-permute-start.1
  12.1 0.7 reshape.41.state_ref
  12.8 0.0 copy-start
  12.8 1.1 copy-done
  13.9 0.0 copy-start.1
  13.9 1.2 copy-done.1
  15.2 1.1 shard_map.103
  16.3 0.6 collective-permute-done.load_ref.early_ref
  16.9 3.9 %shard_map.104 = (f32[200,256]{1,0:T(8,128)S(1)}, f32[200,256]{1,0:T(8,128)S(1)}, f32[18,200,1408]{2,1,0:T(8,128)}) custom-call(f32[216,256]{1,0:T(8,128)S(1)} %collective-permute-done.load_ref.early_ref, bf16[200,1024]{1,0:T(8,128)(2,1)S(1)} %get-tuple-element.33.high_ref, ...), custom_call_target="tpu_custom_call", output_to_operand_aliasing={{2}: (5, {})} | custom-call | tf_op jit(solution)/shard_map/pallas_call | solution.py:448
  20.8 2.1 %collective-permute-done.1.load_ref = f32[216,256]{1,0:T(8,128)S(1)} collective-permute-done((f32[216,256]{1,0:T(8,128)}, f32[216,256]{1,0:T(8,128)S(1)}, u32[]{:S(2)}, u32[]{:S(2)}) %collective-permute-start.1) | collective-permute-done | bytes 221216 | tf_op jit(solution)/shard_map/ppermute | solution.py:461
  22.9 5.6 %shard_map.105 = (f32[200,512]{1,0:T(8,128)S(1)}, f32[1152,128]{1,0:T(8,128)S(1)}, f32[1152,128]{1,0:T(8,128)S(1)}, f32[18,200,1408]{2,1,0:T(8,128)}) custom-call(s32[1]{0:T(128)} %bitcast.3.core_ref, f32[216,256]{1,0:T(8,128)S(1)} %collective-permute-done.load_ref.early_ref, ...), custom_call_target="tpu_custom_call", output_to_operand_aliasing={{3}: (9, {})} | custom-call | tf_op jit(solution)/shard_map/pallas_call | solution.py:448
  28.5 2.8 %collective-permute-start.3 = (f32[1152,128]{1,0:T(8,128)S(1)}, f32[1152,128]{1,0:T(8,128)S(1)}, u32[]{:S(2)}, u32[]{:S(2)}) collective-permute-start(f32[1152,128]{1,0:T(8,128)S(1)} %get-tuple-element.45), channel_id=1, source_target_pairs={{0,1},{1,0},{2,3},{3,2},{4,5},{5,4},{6,7},{7,6},{8,9},{9,8},{10,11... | collective-permute-start | bytes 1769480 | tf_op jit(solution)/shard_map/ppermute | solution.py:461
  31.3 1.6 collective-permute-done.3
  32.9 0.1 add.6
  33.0 18.1 %all_to_all.30 = f32[16,72,128]{2,1,0:T(8,128)S(1)} all-to-all(f32[16,72,128]{2,1,0:T(8,128)S(1)} %bitcast.21), channel_id=1, replica_groups=mesh['z'=8,'x'=4,'y'=4,'c'=2] {'x','y'}, dimensions={0} | all-to-all | bytes 1179648 | tf_op jit(solution)/shard_map/all_to_all | solution.py:466
  51.1 23.1 %all_to_all.31 = f32[8,72,128]{2,1,0:T(8,128)S(1)} all-to-all(f32[8,72,128]{2,1,0:T(8,128)S(1)} %broadcast_in_dim.8), channel_id=1, replica_groups=mesh['z'=8,'x'=4,'y'=4,'c'=2] {'z'}, dimensions={0} | all-to-all | bytes 589824 | tf_op jit(solution)/shard_map/all_to_all | solution.py:468
  74.2 0.9 broadcast_in_dim.9
  75.0 3.8 %all-to-all-start.2 = ((f32[16,72,128]{2,1,0:T(8,128)}), f32[16,72,128]{2,1,0:T(8,128)S(1)}, u32[]{:S(2)}, u32[]{:S(2)}) async-start(f32[16,72,128]{2,1,0:T(8,128)} %broadcast_in_dim.9), calls=%async_computation.2 | async-start | bytes 1179648 | tf_op jit(solution)/shard_map/all_to_all | solution.py:470
  78.8 2.1 %collective-permute-start.2 = (f32[200,512]{1,0:T(8,128)S(1)}, f32[200,512]{1,0:T(8,128)S(1)}, u32[]{:S(2)}, u32[]{:S(2)}) collective-permute-start(f32[200,512]{1,0:T(8,128)S(1)} %get-tuple-element.42), channel_id=1, source_target_pairs={{0,128},{32,160},{64,192},{96,224},{128,0},{160,32},{192,64},{224,... | collective-permute-start | bytes 1228808 | tf_op jit(solution)/shard_map/ppermute | solution.py:461
  81.0 7.2 %all-to-all-done.2 = f32[16,72,128]{2,1,0:T(8,128)S(1)} async-done(((f32[16,72,128]{2,1,0:T(8,128)}), f32[16,72,128]{2,1,0:T(8,128)S(1)}, u32[]{:S(2)}, u32[]{:S(2)}) %all-to-all-start.2) | async-done | bytes 589856 | tf_op jit(solution)/shard_map/all_to_all | solution.py:470
  88.2 4.6 %collective-permute-start.4 = (f32[1152,128]{1,0:T(8,128)S(1)}, f32[1152,128]{1,0:T(8,128)}, u32[]{:S(2)}, u32[]{:S(2)}) collective-permute-start(f32[1152,128]{1,0:T(8,128)S(1)} %bitcast.16), channel_id=1, source_target_pairs={{0,1},{1,0},{2,3},{3,2},{4,5},{5,4},{6,7},{7,6},{8,9},{9,8},{10,11... | collective-permute-start | bytes 1769480 | tf_op jit(solution)/shard_map/ppermute | solution.py:461
  92.8 4.1 %collective-permute-done.2.back_hbm = f32[200,512]{1,0:T(8,128)S(1)} collective-permute-done((f32[200,512]{1,0:T(8,128)S(1)}, f32[200,512]{1,0:T(8,128)S(1)}, u32[]{:S(2)}, u32[]{:S(2)}) %collective-permute-start.2) | collective-permute-done | bytes 409632 | tf_op jit(solution)/shard_map/ppermute | solution.py:461
  96.9 0.0 copy-start.2
  96.9 0.7 copy-done.2
  97.6 5.3 %shard_map.106 = (f32[1,1024]{1,0:T(1,128)}, f32[18,200,1408]{2,1,0:T(8,128)}, f32[216,512]{1,0:T(8,128)}) custom-call(s32[1,2]{1,0:T(1,128)} %bitcast.27, f32[200,1024]{1,0:T(8,128)} %bitcast.14, f32[1,1024]{1,0:T(1,128)} %bitcast.29, f32[18,200,1408]{2,1,0:T(8,128)} %get-tuple-element.41._, f32[200,512]{1,0:T(8,128)} %copy-done.2, ...), custom_call_target="tpu_custom_call", output_to_operand_aliasing={{1}: (3, {})} | custom-call | tf_op jit(solution)/shard_map/pallas_call | solution.py:448
  103.0 5.8 %collective-permute-start.5 = (f32[216,512]{1,0:T(8,128)}, f32[216,512]{1,0:T(8,128)S(1)}, u32[]{:S(2)}, u32[]{:S(2)}) collective-permute-start(f32[216,512]{1,0:T(8,128)} %get-tuple-element.47), channel_id=1, source_target_pairs={{0,1},{1,0},{2,3},{3,2},{4,5},{5,4},{6,7},{7,6},{8,9},{9,8},{10,11... | collective-permute-start | bytes 1327112 | tf_op jit(solution)/shard_map/ppermute | solution.py:461
  108.8 1.6 collective-permute-done.5.load_ref
  110.4 0.0 collective-permute-done.4.other_ref
  110.4 8.7 %shard_map.107 = (f32[200,512]{1,0:T(8,128)S(1)}, f32[1152,128]{1,0:T(8,128)S(1)}, f32[1152,128]{1,0:T(8,128)S(1)}, f32[1,1408]{1,0:T(1,128)S(1)}, f32[18,200,1408]{2,1,0:T(8,128)}) custom-call(s32[1]{0:T(128)} %bitcast.3.core_ref, f32[1152,128]{1,0:T(8,128)S(1)} %bitcast.17, ...), custom_call_target="tpu_custom_call", output_to_operand_aliasing={{4}: (5, {})} | custom-call | tf_op jit(solution)/shard_map/pallas_call | solution.py:448
  119.1 0.5 collective-permute-start.7
  119.6 1.6 collective-permute-done.7
  121.2 0.1 add.7
  121.3 17.9 %all_to_all.32 = f32[16,72,128]{2,1,0:T(8,128)S(1)} all-to-all(f32[16,72,128]{2,1,0:T(8,128)S(1)} %bitcast.22), channel_id=1, replica_groups=mesh['z'=8,'x'=4,'y'=4,'c'=2] {'x','y'}, dimensions={0} | all-to-all | bytes 1179648 | tf_op jit(solution)/shard_map/all_to_all | solution.py:466
  139.2 13.8 %all_to_all.33 = f32[8,72,128]{2,1,0:T(8,128)S(1)} all-to-all(f32[8,72,128]{2,1,0:T(8,128)S(1)} %broadcast_in_dim.10), channel_id=1, replica_groups=mesh['z'=8,'x'=4,'y'=4,'c'=2] {'z'}, dimensions={0} | all-to-all | bytes 589824 | tf_op jit(solution)/shard_map/all_to_all | solution.py:468
  153.1 13.0 %all_to_all.34 = f32[16,72,128]{2,1,0:T(8,128)S(1)} all-to-all(f32[16,72,128]{2,1,0:T(8,128)S(1)} %broadcast_in_dim.11), channel_id=1, replica_groups=mesh['z'=8,'x'=4,'y'=4,'c'=2] {'x','y'}, dimensions={0} | all-to-all | bytes 1179648 | tf_op jit(solution)/shard_map/all_to_all | solution.py:470
  166.1 4.6 %collective-permute-start.8 = (f32[1152,128]{1,0:T(8,128)S(1)}, f32[1152,128]{1,0:T(8,128)}, u32[]{:S(2)}, u32[]{:S(2)}) collective-permute-start(f32[1152,128]{1,0:T(8,128)S(1)} %bitcast.18), channel_id=1, source_target_pairs={{0,1},{1,0},{2,3},{3,2},{4,5},{5,4},{6,7},{7,6},{8,9},{9,8},{10,11... | collective-permute-start | bytes 1769480 | tf_op jit(solution)/shard_map/ppermute | solution.py:461
  170.7 0.0 collective-permute-start.6
  170.7 2.2 %collective-permute-done.6.back_hbm = f32[200,512]{1,0:T(8,128)S(1)} collective-permute-done((f32[200,512]{1,0:T(8,128)S(1)}, f32[200,512]{1,0:T(8,128)S(1)}, u32[]{:S(2)}, u32[]{:S(2)}) %collective-permute-start.6) | collective-permute-done | bytes 409632 | tf_op jit(solution)/shard_map/ppermute | solution.py:461
  172.9 0.0 copy-start.3
  172.9 0.7 copy-done.3
  173.7 4.8 %shard_map.108 = (f32[200,1024]{1,0:T(8,128)}, f32[1,1024]{1,0:T(1,128)}) custom-call(s32[1,2]{1,0:T(1,128)} %bitcast.28, f32[1,1024]{1,0:T(1,128)} %get-tuple-element.43.state_ref, f32[18,200,1408]{2,1,0:T(8,128)} %get-tuple-element.49.store, f32[200,512]{1,0:T(8,128)} %copy-done.3, s32[3,2,512]{2,1,0:T(2,128)} %bitcast.25), custom_call_target="tpu_custom_call" | custom-call | tf_op jit(solution)/shard_map/pallas_call | solution.py:448
  178.5 0.0 collective-permute-done.8.other_ref
  178.5 3.6 %shard_map.109 = (f32[200,1345]{1,0:T(8,128)}, f32[1,1345]{1,0:T(1,128)S(1)}) custom-call(s32[1]{0:T(128)} %bitcast.3.core_ref, f32[1152,128]{1,0:T(8,128)S(1)} %bitcast.19, f32[1152,128]{1,0:T(8,128)} %collective-permute-done.8.other_ref, f32[18,200,1408]{2,1,0:T(8,128)} %get-tuple-element.49.store, f32[1,1408]{1,0:T(1,128)S(1)} %get-tuple-element.55.state_ref), custom_call_target="tpu_custom_call" | custom-call | tf_op jit(solution)/shard_map/pallas_call | solution.py:448
  182.1 0.6 reduce
  (7 shorter events, 0.2 us)
Async XLA Ops:
  4.2 12.7 %collective-permute-start = (f32[216,256]{1,0:T(8,128)}, f32[216,256]{1,0:T(8,128)S(1)}, u32[]{:S(2)}, u32[]{:S(2)}) collective-permute-start(f32[216,256]{1,0:T(8,128)} %get-tuple-element.31), channel_id=1, source_target_pairs={{0,128},{32,160},{64,192},{96,224},{128,0},{160,32},{192,64},{224,... | collective-permute-start | bytes 663560 | tf_op jit(solution)/shard_map/ppermute | solution.py:461
  12.0 10.9 %collective-permute-start.1 = (f32[216,256]{1,0:T(8,128)}, f32[216,256]{1,0:T(8,128)S(1)}, u32[]{:S(2)}, u32[]{:S(2)}) collective-permute-start(f32[216,256]{1,0:T(8,128)} %get-tuple-element.32), channel_id=1, source_target_pairs={{0,128},{32,160},{64,192},{96,224},{128,0},{160,32},{192,64},{224,... | collective-permute-start | bytes 663560 | tf_op jit(solution)/shard_map/ppermute | solution.py:461
  12.8 1.1 copy-start
  13.9 1.3 copy-start.1
  28.5 4.4 %collective-permute-start.3 = (f32[1152,128]{1,0:T(8,128)S(1)}, f32[1152,128]{1,0:T(8,128)S(1)}, u32[]{:S(2)}, u32[]{:S(2)}) collective-permute-start(f32[1152,128]{1,0:T(8,128)S(1)} %get-tuple-element.45), channel_id=1, source_target_pairs={{0,1},{1,0},{2,3},{3,2},{4,5},{5,4},{6,7},{7,6},{8,9},{9,8},{10,11... | collective-permute-start | bytes 1769480 | tf_op jit(solution)/shard_map/ppermute | solution.py:461
  75.0 13.2 %all-to-all-start.2 = ((f32[16,72,128]{2,1,0:T(8,128)}), f32[16,72,128]{2,1,0:T(8,128)S(1)}, u32[]{:S(2)}, u32[]{:S(2)}) async-start(f32[16,72,128]{2,1,0:T(8,128)} %broadcast_in_dim.9), calls=%async_computation.2 | async-start | bytes 1179648 | tf_op jit(solution)/shard_map/all_to_all | solution.py:470
  78.8 18.1 %collective-permute-start.2 = (f32[200,512]{1,0:T(8,128)S(1)}, f32[200,512]{1,0:T(8,128)S(1)}, u32[]{:S(2)}, u32[]{:S(2)}) collective-permute-start(f32[200,512]{1,0:T(8,128)S(1)} %get-tuple-element.42), channel_id=1, source_target_pairs={{0,128},{32,160},{64,192},{96,224},{128,0},{160,32},{192,64},{224,... | collective-permute-start | bytes 1228808 | tf_op jit(solution)/shard_map/ppermute | solution.py:461
  88.2 22.2 %collective-permute-start.4 = (f32[1152,128]{1,0:T(8,128)S(1)}, f32[1152,128]{1,0:T(8,128)}, u32[]{:S(2)}, u32[]{:S(2)}) collective-permute-start(f32[1152,128]{1,0:T(8,128)S(1)} %bitcast.16), channel_id=1, source_target_pairs={{0,1},{1,0},{2,3},{3,2},{4,5},{5,4},{6,7},{7,6},{8,9},{9,8},{10,11... | collective-permute-start | bytes 1769480 | tf_op jit(solution)/shard_map/ppermute | solution.py:461
  96.9 0.8 copy-start.2
  103.0 7.5 %collective-permute-start.5 = (f32[216,512]{1,0:T(8,128)}, f32[216,512]{1,0:T(8,128)S(1)}, u32[]{:S(2)}, u32[]{:S(2)}) collective-permute-start(f32[216,512]{1,0:T(8,128)} %get-tuple-element.47), channel_id=1, source_target_pairs={{0,1},{1,0},{2,3},{3,2},{4,5},{5,4},{6,7},{7,6},{8,9},{9,8},{10,11... | collective-permute-start | bytes 1327112 | tf_op jit(solution)/shard_map/ppermute | solution.py:461
  119.1 2.1 %collective-permute-start.7 = (f32[1152,128]{1,0:T(8,128)S(1)}, f32[1152,128]{1,0:T(8,128)S(1)}, u32[]{:S(2)}, u32[]{:S(2)}) collective-permute-start(f32[1152,128]{1,0:T(8,128)S(1)} %get-tuple-element.54), channel_id=1, source_target_pairs={{0,1},{1,0},{2,3},{3,2},{4,5},{5,4},{6,7},{7,6},{8,9},{9,8},{10,11... | collective-permute-start | bytes 1769480 | tf_op jit(solution)/shard_map/ppermute | solution.py:461
  166.1 12.4 %collective-permute-start.8 = (f32[1152,128]{1,0:T(8,128)S(1)}, f32[1152,128]{1,0:T(8,128)}, u32[]{:S(2)}, u32[]{:S(2)}) collective-permute-start(f32[1152,128]{1,0:T(8,128)S(1)} %bitcast.18), channel_id=1, source_target_pairs={{0,1},{1,0},{2,3},{3,2},{4,5},{5,4},{6,7},{7,6},{8,9},{9,8},{10,11... | collective-permute-start | bytes 1769480 | tf_op jit(solution)/shard_map/ppermute | solution.py:461
  170.7 2.2 %collective-permute-start.6 = (f32[200,512]{1,0:T(8,128)S(1)}, f32[200,512]{1,0:T(8,128)S(1)}, u32[]{:S(2)}, u32[]{:S(2)}) collective-permute-start(f32[200,512]{1,0:T(8,128)S(1)} %get-tuple-element.50), channel_id=1, source_target_pairs={{0,1},{1,0},{2,3},{3,2},{4,5},{5,4},{6,7},{7,6},{8,9},{9,8},{10,11... | collective-permute-start | bytes 1228808 | tf_op jit(solution)/shard_map/ppermute | solution.py:461
  172.9 0.8 copy-start.3

commit v4 on v3

--- a/solution.py
+++ b/solution.py
@@ -15,6 +15,8 @@
 ROWS = 1024
 DIM = 200
 HALF = DIM // 2
+LOW = 208
+STACK = 2 * LOW
 REL = 1345
 RELP = 1408
 NEG = 1000
@@ -55,8 +57,17 @@
 NT = ((1,), (1,))
 
 
-def dot3(a, b, dims=((1,), (0,))):
-    return dot(a[0], b[0], dims) + (dot(a[1], b[0], dims) + dot(a[0], b[1], dims))
+def stack(ref, value):
+    high, low = halves(value)
+    gap = jnp.zeros((LOW - DIM, value.shape[1]), BF16)
+    ref[0:DIM, :], ref[DIM:LOW, :] = high, gap
+    ref[LOW : LOW + DIM, :], ref[LOW + DIM : STACK, :] = low, gap
+
+
+def stack_dot(parts, high, low=None, dims=((1,), (0,))):
+    both = dot(parts, high, dims)
+    total = both[0:DIM] + both[LOW : LOW + DIM]
+    return total if low is None else total + dot(parts[0:DIM], low, dims)
 
 
 def one_hot(ids, count):
@@ -84,16 +95,11 @@
     return copies
 
 
-def write_payload(out_refs, parts, edges_ref, negatives_ref, count, which):
-    source = live_sources(edges_ref, count, which)
-    pick = one_hot(source, ROWS)
-    high, low = parts
-    rows = dot(high, pick) + dot(low, pick)
+def write_lists(refs, edges_ref, negatives_ref, which):
     first = 0
-    for ref in out_refs:
+    for ref in refs:
         wide = ref.shape[1]
         span = slice(first, first + wide)
-        ref[0:DIM, :] = rows[:, span]
         ref[ID_ROW : ID_ROW + 1, :] = edges_ref[1, which : which + 1, span].astype(F32)
         ref[ID_ROW + 1 : ID_ROW + 2, :] = edges_ref[2, which : which + 1, span].astype(F32)
         ref[ID_ROW + 2 : HIST_ROW, :] = jnp.zeros((HIST_ROW - ID_ROW - 2, wide), F32)
@@ -103,6 +109,11 @@
                 negatives_ref[which, k : k + 1, :]
             )
         first += wide
+
+
+def source_rows(parts_ref, edges_ref, count, which, first, wide):
+    source = live_sources(edges_ref, count, which)[:, first : first + wide]
+    return stack_dot(parts_ref[...], one_hot(source, ROWS))
 
 
 def prepare(
@@ -117,38 +128,32 @@
     negatives_ref,
     first_ref,
     second_ref,
+    parts_ref,
     sem,
 ):
-    copies = fetch(
-        sem, (edges_hbm, edges_ref), (table_hbm, table_ref), (negatives_hbm, negatives_ref)
-    )
+    negatives_copy, edges_copy, table_copy = fetch(
+        sem, (negatives_hbm, negatives_ref), (edges_hbm, edges_ref), (table_hbm, table_ref)
+    )
+    negatives_copy.wait()
+    edges_copy.wait()
+    write_lists((first_ref, second_ref), edges_ref, negatives_ref, 0)
+    table_copy.wait()
+    stack(parts_ref, table_ref[...])
+    count = counts_ref[0, 0]
+    first_ref[0:DIM, :] = source_rows(parts_ref, edges_ref, count, 0, 0, EARLY)
+    copies = fetch(sem, (first_ref, first_out))
+    second_ref[0:DIM, :] = source_rows(parts_ref, edges_ref, count, 0, EARLY, EDGES - EARLY)
+    copies += fetch(sem.at[1:2], (second_ref, second_out))
     for copy in copies:
         copy.wait()
-    pieces = (first_ref, second_ref)
-    parts = halves(table_ref[...])
-    write_payload(pieces, parts, edges_ref, negatives_ref, counts_ref[0, 0], 0)
-    for copy in fetch(sem, (first_ref, first_out), (second_ref, second_out)):
-        copy.wait()
-
-
-def settle(
-    table_ref,
-    rel_ref,
-    state_ref,
-    store,
-    state_out,
-    rel_high,
-    rel_low,
-    table_high,
-    table_low,
-    rel,
-    sem,
-):
+
+
+def settle(table_ref, rel_ref, state_ref, store, state_out, rel_parts, table_parts, rel, sem):
     rel[:, 10 * 128 : RELP] = jnp.zeros((DIM, RELP - 10 * 128), F32)
     rel[:, 0:REL] = rel_ref[...]
     (copy,) = fetch(sem, (rel, store.at[RELATION]))
-    rel_high[...], rel_low[...] = halves(rel[...])
-    table_high[...], table_low[...] = halves(table_ref[...])
+    stack(rel_parts, rel[...])
+    stack(table_parts, table_ref[...])
     state_out[...] = jnp.ones((1, RELP), F32)
     state_out[:, 0:REL] = state_ref[...]
     copy.wait()
@@ -174,21 +179,25 @@
     return plus * times - jnp.where(lanes == target, minus, 0.0)
 
 
-def edge_terms(load_ref, table_parts, rel_parts, work, sg_out, rg_ref, first, put):
-    w_ref, q_ref, score_ref, high_ref, low_ref, back_ref = work
+def edge_terms(load_ref, table_ref, rel_ref, work, sg_out, rg_ref, first, put):
+    w_ref, q_ref, parts_ref, score_ref, high_ref, low_ref, back_ref = work
     wide = load_ref.shape[1]
     pick = one_hot(load_ref[ID_ROW : ID_ROW + 1, :].astype(jnp.int32), RELP)
-    w_ref[...] = dot(rel_parts[0], pick) + dot(rel_parts[1], pick)
+    w_ref[...] = stack_dot(rel_ref[...], pick)
     s_re, s_im = load_ref[0:HALF, :], load_ref[HALF:DIM, :]
     w_re, w_im = w_ref[0:HALF, :], w_ref[HALF:DIM, :]
     multiply(s_re, s_im, w_re, w_im, False, q_ref, slice(None))
     product = q_ref[...]
-    product_parts = halves(product)
+    stack(parts_ref, product)
     target = load_ref[ID_ROW : ID_ROW + 8, :].T[:, 1:2].astype(jnp.int32)
     turned = halves(product.T)
+    table_high, table_low = table_ref[0:DIM, :], table_ref[LOW : LOW + DIM, :]
     spans = [slice(start, min(start + STEP, wide)) for start in range(0, wide, STEP)]
     for edges in spans:
-        score_ref[edges, :] = dot3((turned[0][edges], turned[1][edges]), table_parts)
+        count = edges.stop - edges.start
+        high, low = turned[0][edges], turned[1][edges]
+        both = dot(jnp.concatenate([high, low], axis=0), table_high)
+        score_ref[edges, :] = both[0:count] + both[count:] + dot(high, table_low)
     table_grad = None
     for span in spans:
         for block in range(span.start, span.stop, BLOCK):
@@ -198,9 +207,9 @@
                 times = load_ref[HIST_ROW + tile : HIST_ROW + tile + 1, edges] * (1.0 / NEG)
                 value = weights(score_ref[edges, lanes], times, target[edges], tile * 128)
                 high_ref[edges, lanes], low_ref[edges, lanes] = halves(value)
-        weight_parts = high_ref[span, :], low_ref[span, :]
-        back_ref[:, span] = dot3(table_parts, weight_parts, NT)
-        part = dot3((product_parts[0][:, span], product_parts[1][:, span]), weight_parts)
+        high, low = high_ref[span, :], low_ref[span, :]
+        back_ref[:, span] = stack_dot(table_ref[...], high, low, NT)
+        part = stack_dot(parts_ref[:, span], high, low)
         table_grad = part if table_grad is None else table_grad + part
     copies = put(table_grad)
     up_re, up_im = back_ref[0:HALF, :], back_ref[HALF:DIM, :]
@@ -210,9 +219,9 @@
     return pick, copies
 
 
-def relation_grad(rg_ref, pick):
-    high, low = halves(rg_ref[...])
-    return dot(high, pick, NT) + dot(low, pick, NT)
+def relation_grad(rg_ref, parts_ref, pick):
+    stack(parts_ref, rg_ref[...])
+    return stack_dot(parts_ref[...], pick, None, NT)
 
 
 def split_flat(core, grad, flat, send_out, keep_out):
@@ -237,17 +246,14 @@
     return store.at[plane, :, 0:ROWS]
 
 
-def first_piece(
-    load_ref, high_ref, low_ref, rel_high, rel_low, _, sg_out, rg_out, store, *work
-):
+def first_piece(load_ref, table_ref, rel_ref, _, sg_out, rg_out, store, *work):
     work, grad_ref, sem = work[:-2], work[-2], work[-1]
 
     def put(value):
         grad_ref[...] = value
         return fetch(sem, (grad_ref, entities_of(store, GRAD)))
 
-    table_parts, rel_parts = (high_ref[...], low_ref[...]), (rel_high[...], rel_low[...])
-    _, copies = edge_terms(load_ref, table_parts, rel_parts, work, sg_out, rg_out, 0, put)
+    _, copies = edge_terms(load_ref, table_ref, rel_ref, work, sg_out, rg_out, 0, put)
     for copy in copies:
         copy.wait()
 
@@ -256,10 +262,8 @@
     core_ref,
     early_ref,
     load_ref,
-    high_ref,
-    low_ref,
-    rel_high,
-    rel_low,
+    table_ref,
+    rel_ref,
     sg_ref,
     rg_ref,
     _,
@@ -269,7 +273,7 @@
     store,
     *work,
 ):
-    work, rg, flat, grad_ref, g_ref, sem = work[:-5], *work[-5:]
+    work, rg, rg_parts, flat, grad_ref, g_ref, sem = work[:-6], *work[-6:]
     (g_copy,) = fetch(sem, (entities_of(store, GRAD), g_ref))
 
     def put(value):
@@ -277,19 +281,22 @@
         grad_ref[...] = value + g_ref[...]
         return fetch(sem, (grad_ref, entities_of(store, GRAD)))
 
-    table_parts, rel_parts = (high_ref[...], low_ref[...]), (rel_high[...], rel_low[...])
     sg_out[:, 0:EARLY] = sg_ref[...]
     rg[:, 0:EARLY] = rg_ref[...]
-    pick, copies = edge_terms(load_ref, table_parts, rel_parts, work, sg_out, rg, EARLY, put)
+    pick, copies = edge_terms(load_ref, table_ref, rel_ref, work, sg_out, rg, EARLY, put)
     early = one_hot(early_ref[ID_ROW : ID_ROW + 1, :].astype(jnp.int32), RELP)
     pick = jnp.concatenate([early, pick], axis=1)
-    split_flat(core_ref[0], relation_grad(rg, pick), flat, send, keep)
+    split_flat(core_ref[0], relation_grad(rg, rg_parts, pick), flat, send, keep)
     for copy in copies:
         copy.wait()
 
 
 def step_relations(core, mine_ref, other_ref, rel_ref, state_ref, flat, rel_out, state_out):
     join_flat(core, mine_ref, other_ref, flat)
+    step_tiles(rel_ref, state_ref, flat, rel_out, state_out)
+
+
+def step_tiles(rel_ref, state_ref, flat, rel_out, state_out):
     for tile in range(RELP // 128):
         lanes = slice(tile * 128, (tile + 1) * 128)
         rel_out[:, lanes], state_out[:, lanes] = adagrad(
@@ -311,7 +318,7 @@
     store,
     *work,
 ):
-    work, rg, flat, old_ref, rel_ref, grad_ref, sem = work[:-6], *work[-6:]
+    work, rg, rg_parts, flat, old_ref, rel_ref, grad_ref, tables, rels, sem = work[:-9], *work[-9:]
     rel_copy, table_copy = fetch(
         sem, (store.at[RELATION], old_ref), (entities_of(store, TABLE), grad_ref)
     )
@@ -320,23 +327,25 @@
     step_relations(core, mine_ref, other_ref, old_ref, state_ref, flat, rel_ref, state_out)
     (rel_copy,) = fetch(sem, (rel_ref, store.at[RELATION]))
     table_copy.wait()
-    table_parts = halves(grad_ref[...])
+    stack(tables, grad_ref[...])
 
     def put(value):
         grad_ref[...] = value
         return fetch(sem.at[1:2], (grad_ref, entities_of(store, GRAD)))
 
-    rel_parts = halves(rel_ref[...])
-    pick, copies = edge_terms(load_ref, table_parts, rel_parts, work, sg_out, rg, 0, put)
-    split_flat(core, relation_grad(rg, pick), flat, send, keep)
+    stack(rels, rel_ref[...])
+    pick, copies = edge_terms(load_ref, tables, rels, work, sg_out, rg, 0, put)
+    split_flat(core, relation_grad(rg, rg_parts, pick), flat, send, keep)
     for copy in [rel_copy, *copies]:
         copy.wait()
 
 
-def step_entities(table_ref, state_ref, grad_ref, back_ref, edges_ref, count, which):
+def step_entities(
+    table_ref, state_ref, grad_ref, back_ref, parts_ref, edges_ref, count, which
+):
     pick = one_hot(live_sources(edges_ref, count, which), ROWS)
-    high, low = halves(back_ref[...])
-    grad = grad_ref[...] + (dot(high, pick, NT) + dot(low, pick, NT))
+    stack(parts_ref, back_ref[...])
+    grad = grad_ref[...] + stack_dot(parts_ref[...], pick, None, NT)
     return adagrad(table_ref[...], state_ref[...], grad)
 
 
@@ -356,6 +365,8 @@
     back_ref,
     edges_ref,
     negatives_ref,
+    parts_ref,
+    tables_ref,
     sem,
 ):
     copies = fetch(
@@ -369,11 +380,13 @@
     for copy in copies:
         copy.wait()
     table, state_out[...] = step_entities(
-        table_ref, state_ref, grad_ref, back_ref, edges_ref, counts_ref[0, 0], 0
+        table_ref, state_ref, grad_ref, back_ref, parts_ref, edges_ref, counts_ref[0, 0], 0
     )
     table_ref[...] = table
     (copy,) = fetch(sem, (table_ref, entities_of(store, TABLE)))
-    write_payload((load,), halves(table), edges_ref, negatives_ref, counts_ref[0, 1], 1)
+    stack(tables_ref, table)
+    write_lists((load,), edges_ref, negatives_ref, 1)
+    load[0:DIM, :] = source_rows(tables_ref, edges_ref, counts_ref[0, 1], 1, 0, EDGES)
     copy.wait()
 
 
@@ -389,6 +402,7 @@
     grad_ref,
     back_ref,
     edges_ref,
+    parts_ref,
     sem,
 ):
     copies = fetch(
@@ -401,7 +415,7 @@
     for copy in copies:
         copy.wait()
     table, state_out[...] = step_entities(
-        table_ref, state_ref, grad_ref, back_ref, edges_ref, counts_ref[0, 1], 1
+        table_ref, state_ref, grad_ref, back_ref, parts_ref, edges_ref, counts_ref[0, 1], 1
     )
     table_ref[...] = table
     (copy,) = fetch(sem, (table_ref, table_out))
@@ -423,16 +437,18 @@
     sem,
 ):
     (copy,) = fetch(sem, (store.at[RELATION], old_ref))
+    join_flat(core_ref[0], mine_ref, other_ref, flat)
     copy.wait()
-    step_relations(core_ref[0], mine_ref, other_ref, old_ref, state_ref, flat, rel, state)
+    step_tiles(old_ref, state_ref, flat, rel, state)
     rel_out[...] = rel[:, 0:REL]
-    state_out[...] = state[:, 0:REL]
+    state_out[...] = state[0, 0:REL]
 
 
 def work_shapes(wide):
     return [
         pltpu.VMEM((DIM, wide), F32),
         pltpu.VMEM((DIM, wide), F32),
+        pltpu.VMEM((STACK, wide), BF16),
         pltpu.VMEM((wide, ROWS), F32),
         pltpu.VMEM((wide, ROWS), BF16),
         pltpu.VMEM((wide, ROWS), BF16),
@@ -463,11 +479,11 @@
 
 def total(send, keep):
     part = (keep + across(send, C, 1)).reshape(16, SIDE // 16, 128)
-    part = lax.all_to_all(part, (X, Y), 0, 0, tiled=True).sum(axis=0)
+    part = lax.all_to_all(part, (Y, X), 0, 0, tiled=True).sum(axis=0)
     part = jnp.broadcast_to(part[None], (8, *part.shape))
     part = lax.all_to_all(part, Z, 0, 0, tiled=True).sum(axis=0)
     part = jnp.broadcast_to(part[None], (16, *part.shape))
-    part = lax.all_to_all(part, (X, Y), 0, 0, tiled=True)
+    part = lax.all_to_all(part, (Y, X), 0, 0, tiled=True)
     mine = part.reshape(SIDE, 128)
     return mine, across(mine, C, 1)
 
@@ -479,10 +495,9 @@
     state = entity_state.reshape(1, ROWS)
     late = EDGES - EARLY
     grown = shape(DIM, ROWS)
-    narrow = shape(DIM, ROWS, dtype=BF16)
-    wide_rel = shape(DIM, RELP, dtype=BF16)
     vmem = pltpu.VMEM
-    table_mem = vmem((DIM, ROWS), F32)
+    table_mem, rg_mem = vmem((DIM, ROWS), F32), vmem((STACK, EDGES), BF16)
+    tables_mem, rels_mem = vmem((STACK, ROWS), BF16), vmem((STACK, RELP), BF16)
     flat_mem = vmem((FLAT, 128), F32)
     back_mem, rel_mem = vmem((DIM, EDGES), F32), vmem((DIM, RELP), F32)
     edge_mem, negative_mem = vmem((3, 2, EDGES), jnp.int32), vmem(negatives.shape, jnp.int32)
@@ -491,17 +506,19 @@
         "shhh",
         [("h", shape(LOAD, EARLY)), ("h", shape(LOAD, late))],
         (counts, table, edges, negatives),
-        [table_mem, edge_mem, negative_mem, vmem((LOAD, EARLY), F32), vmem((LOAD, late), F32)],
+        [table_mem, edge_mem, negative_mem, vmem((LOAD, EARLY), F32), vmem((LOAD, late), F32)]
+        + [tables_mem],
         3,
         63 << 20,
     )
     first = across(first, Z, 4)
     second = across(second, Z, 4)
     store_out = ("h", shape(STORE, DIM, RELP))
-    store, rel_state, rel_high, rel_low, high, low = call(
+    store, rel_state, rel_parts, table_parts = call(
         settle,
         "vvv",
-        [store_out, ("v", shape(1, RELP))] + [("v", wide_rel)] * 2 + [("v", narrow)] * 2,
+        [store_out, ("v", shape(1, RELP))]
+        + [("v", shape(STACK, RELP, dtype=BF16)), ("v", shape(STACK, ROWS, dtype=BF16))],
         (table, rel, relation_state.reshape(1, REL)),
         [rel_mem],
         1,
@@ -509,22 +526,22 @@
     piece = ("v", shape(DIM, EARLY))
     back, rel_terms, store = call(
         first_piece,
-        "vvvvvh",
+        "vvvh",
         [piece, piece, store_out],
-        (first, high, low, rel_high, rel_low, store),
+        (first, table_parts, rel_parts, store),
         work_shapes(EARLY) + [table_mem],
         1,
-        alias={5: 2},
+        alias={3: 2},
     )
     half = ("v", shape(SIDE, 128))
     back, send, keep, store = call(
         second_piece,
-        "svvvvvvvvh",
+        "svvvvvvh",
         [("v", shape(DIM, EDGES)), half, half, store_out],
-        (core, first, second, high, low, rel_high, rel_low, back, rel_terms, store),
-        work_shapes(late) + [back_mem, flat_mem, table_mem, table_mem],
+        (core, first, second, table_parts, rel_parts, back, rel_terms, store),
+        work_shapes(late) + [back_mem, rg_mem, flat_mem, table_mem, table_mem],
         1,
-        alias={9: 3},
+        alias={7: 3},
     )
     back = across(back, Z, 4)
     mine, other = total(send, keep)
@@ -533,7 +550,7 @@
         "shvhhhh",
         [("v", shape(1, ROWS)), store_out, ("v", shape(LOAD, EDGES))],
         (counts, table, state, store, back, edges, negatives),
-        [table_mem, table_mem, back_mem, edge_mem, negative_mem],
+        [table_mem, table_mem, back_mem, edge_mem, negative_mem, rg_mem, tables_mem],
         5,
         63 << 20,
         {3: 1},
@@ -545,7 +562,7 @@
         [("v", shape(DIM, EDGES)), half, half, ("v", shape(1, RELP)), store_out],
         (core, mine, other, rel_state, load, store),
         work_shapes(EDGES)
-        + [back_mem, flat_mem, rel_mem, rel_mem, table_mem],
+        + [back_mem, rg_mem, flat_mem, rel_mem, rel_mem, table_mem, tables_mem, rels_mem],
         2,
         alias={5: 4},
     )
@@ -556,19 +573,19 @@
         "svhhh",
         [("h", grown), ("v", shape(1, ROWS))],
         (counts, state, store, back, edges),
-        [table_mem, table_mem, back_mem, edge_mem],
+        [table_mem, table_mem, back_mem, edge_mem, rg_mem],
         4,
         63 << 20,
     )
     rel, rel_state = call(
         last_relations,
         "svvhv",
-        [("v", shape(DIM, REL)), ("v", shape(1, REL))],
+        [("v", shape(DIM, REL)), ("v", shape(REL))],
         (core, mine, other, store, rel_state),
         [flat_mem, rel_mem, rel_mem, vmem((1, RELP), F32)],
         1,
     )
-    return table.T, state.reshape(ROWS), rel.T, rel_state.reshape(REL)
+    return table.T, state.reshape(ROWS), rel.T, rel_state
 
 
 def solution(mesh):

time: 184 us -> 183 us (level)
  no operation moved by 1% of the time
where the time goes in v4:
time: 183 us; the launch traced here: 182 us
  blocking collectives  84.7 us (46%)
  Pallas kernels  36.1 us (20%)
  starting transfers between devices  32.6 us (18%)
  waiting for transfers between devices  21.9 us (12%)
  local copies, waits for them, and re-layouts  5.53 us (3%)
    pallas_call x8, Pallas kernels, call(): pl.pallas_call(body, out_shape=[out for _, out in outs], in_specs=[SPECS[...  36.1 us
    all_to_all x2, blocking collectives, total(): part = lax.all_to_all(part, (Y, X), 0, 0, tiled=True).sum(axis=0)  36 us
    all_to_all x2, blocking collectives, total(): part = lax.all_to_all(part, Z, 0, 0, tiled=True).sum(axis=0)  35.1 us
    ppermute x9, starting transfers between devices, across(): return lax.ppermute(value, axis, [(i, i ^ apart) for i in range(count)])  28.2 us
    ppermute x9, waiting for transfers between devices, across(): return lax.ppermute(value, axis, [(i, i ^ apart) for i in range(count)])  14.6 us
    all_to_all x1, blocking collectives, total(): part = lax.all_to_all(part, (Y, X), 0, 0, tiled=True)  13.6 us
    all_to_all x1, waiting for transfers between devices, total(): part = lax.all_to_all(part, (Y, X), 0, 0, tiled=True)  7.35 us
    all_to_all x1, starting transfers between devices, total(): part = lax.all_to_all(part, (Y, X), 0, 0, tiled=True)  4.45 us
  transfers between devices with their start and end apart: 10, of which 8 were waited for; matrix products, arithmetic and copies ran while one was open for 0% of the time, Pallas kernels for 8%

profile of v4, /device:TPU:1, one launch (start us, length us, event | category | flops | bytes accessed | tf_op | source)
XLA Modules:
  0.0 182.1 jit_solution(7942605929243093877)
XLA Ops:
  0.6 3.3 %shard_map.102 = (f32[216,256]{1,0:T(8,128)}, f32[216,256]{1,0:T(8,128)}) custom-call(s32[1,2]{1,0:T(1,128)} %bitcast.26, f32[200,1024]{1,0:T(8,128)} %bitcast.13, s32[3,2,512]{2,1,0:T(2,128)} %bitcast.23, s32[2,4,1000]{2,1,0:T(4,128)} %negatives_hbm.3), custom_call_target="tpu_custom_call" | custom-call | tf_op jit(solution)/shard_map/pallas_call | solution.py:464
  3.9 7.8 %collective-permute-start = (f32[216,256]{1,0:T(8,128)}, f32[216,256]{1,0:T(8,128)S(1)}, u32[]{:S(2)}, u32[]{:S(2)}) collective-permute-start(f32[216,256]{1,0:T(8,128)} %get-tuple-element.29), channel_id=1, source_target_pairs={{0,128},{32,160},{64,192},{96,224},{128,0},{160,32},{192,64},{224,... | collective-permute-start | bytes 663560 | tf_op jit(solution)/shard_map/ppermute | solution.py:477
  11.7 0.1 collective-permute-start.1
  11.8 0.7 reshape.38.state_ref
  12.5 0.0 copy-start
  12.5 1.1 copy-done
  13.6 0.0 copy-start.1
  13.7 1.2 copy-done.1
  14.9 1.1 shard_map.103
  16.0 0.6 collective-permute-done.load_ref.early_ref
  16.6 4.0 %shard_map.104 = (f32[200,256]{1,0:T(8,128)S(1)}, f32[200,256]{1,0:T(8,128)S(1)}, f32[18,200,1408]{2,1,0:T(8,128)}) custom-call(f32[216,256]{1,0:T(8,128)S(1)} %collective-permute-done.load_ref.early_ref, bf16[416,1024]{1,0:T(8,128)(2,1)S(1)} %get-tuple-element.31.table_ref, ...), custom_call_target="tpu_custom_call", output_to_operand_aliasing={{2}: (3, {})} | custom-call | tf_op jit(solution)/shard_map/pallas_call | solution.py:464
  20.6 2.1 %collective-permute-done.1.load_ref = f32[216,256]{1,0:T(8,128)S(1)} collective-permute-done((f32[216,256]{1,0:T(8,128)}, f32[216,256]{1,0:T(8,128)S(1)}, u32[]{:S(2)}, u32[]{:S(2)}) %collective-permute-start.1) | collective-permute-done | bytes 221216 | tf_op jit(solution)/shard_map/ppermute | solution.py:477
  22.6 6.0 %shard_map.105 = (f32[200,512]{1,0:T(8,128)S(1)}, f32[1152,128]{1,0:T(8,128)S(1)}, f32[1152,128]{1,0:T(8,128)S(1)}, f32[18,200,1408]{2,1,0:T(8,128)}) custom-call(s32[1]{0:T(128)} %bitcast.3.core_ref, f32[216,256]{1,0:T(8,128)S(1)} %collective-permute-done.load_ref.early_ref, ...), custom_call_target="tpu_custom_call", output_to_operand_aliasing={{3}: (7, {})} | custom-call | tf_op jit(solution)/shard_map/pallas_call | solution.py:464
  28.6 2.8 %collective-permute-start.3 = (f32[1152,128]{1,0:T(8,128)S(1)}, f32[1152,128]{1,0:T(8,128)S(1)}, u32[]{:S(2)}, u32[]{:S(2)}) collective-permute-start(f32[1152,128]{1,0:T(8,128)S(1)} %get-tuple-element.41), channel_id=1, source_target_pairs={{0,1},{1,0},{2,3},{3,2},{4,5},{5,4},{6,7},{7,6},{8,9},{9,8},{10,11... | collective-permute-start | bytes 1769480 | tf_op jit(solution)/shard_map/ppermute | solution.py:477
  31.4 1.6 collective-permute-done.3
  33.0 0.1 add.6
  33.1 18.0 %all_to_all.30 = f32[16,72,128]{2,1,0:T(8,128)S(1)} all-to-all(f32[16,72,128]{2,1,0:T(8,128)S(1)} %bitcast.21), channel_id=1, replica_groups=mesh['z'=8,'x'=4,'y'=4,'c'=2] {'y','x'}, dimensions={0} | all-to-all | bytes 1179648 | tf_op jit(solution)/shard_map/all_to_all | solution.py:482
  51.1 22.6 %all_to_all.31 = f32[8,72,128]{2,1,0:T(8,128)S(1)} all-to-all(f32[8,72,128]{2,1,0:T(8,128)S(1)} %broadcast_in_dim.8), channel_id=1, replica_groups=mesh['z'=8,'x'=4,'y'=4,'c'=2] {'z'}, dimensions={0} | all-to-all | bytes 589824 | tf_op jit(solution)/shard_map/all_to_all | solution.py:484
  73.8 0.9 broadcast_in_dim.9
  74.6 4.4 %all-to-all-start.2 = ((f32[16,72,128]{2,1,0:T(8,128)}), f32[16,72,128]{2,1,0:T(8,128)S(1)}, u32[]{:S(2)}, u32[]{:S(2)}) async-start(f32[16,72,128]{2,1,0:T(8,128)} %broadcast_in_dim.9), calls=%async_computation.2 | async-start | bytes 1179648 | tf_op jit(solution)/shard_map/all_to_all | solution.py:486
  79.1 2.0 %collective-permute-start.2 = (f32[200,512]{1,0:T(8,128)S(1)}, f32[200,512]{1,0:T(8,128)S(1)}, u32[]{:S(2)}, u32[]{:S(2)}) collective-permute-start(f32[200,512]{1,0:T(8,128)S(1)} %get-tuple-element.38), channel_id=1, source_target_pairs={{0,128},{32,160},{64,192},{96,224},{128,0},{160,32},{192,64},{224,... | collective-permute-start | bytes 1228808 | tf_op jit(solution)/shard_map/ppermute | solution.py:477
  81.1 7.4 %all-to-all-done.2 = f32[16,72,128]{2,1,0:T(8,128)S(1)} async-done(((f32[16,72,128]{2,1,0:T(8,128)}), f32[16,72,128]{2,1,0:T(8,128)S(1)}, u32[]{:S(2)}, u32[]{:S(2)}) %all-to-all-start.2) | async-done | bytes 589856 | tf_op jit(solution)/shard_map/all_to_all | solution.py:486
  88.4 4.5 %collective-permute-start.4 = (f32[1152,128]{1,0:T(8,128)S(1)}, f32[1152,128]{1,0:T(8,128)}, u32[]{:S(2)}, u32[]{:S(2)}) collective-permute-start(f32[1152,128]{1,0:T(8,128)S(1)} %bitcast.16), channel_id=1, source_target_pairs={{0,1},{1,0},{2,3},{3,2},{4,5},{5,4},{6,7},{7,6},{8,9},{9,8},{10,11... | collective-permute-start | bytes 1769480 | tf_op jit(solution)/shard_map/ppermute | solution.py:477
  93.0 4.8 %collective-permute-done.2.back_hbm = f32[200,512]{1,0:T(8,128)S(1)} collective-permute-done((f32[200,512]{1,0:T(8,128)S(1)}, f32[200,512]{1,0:T(8,128)S(1)}, u32[]{:S(2)}, u32[]{:S(2)}) %collective-permute-start.2) | collective-permute-done | bytes 409632 | tf_op jit(solution)/shard_map/ppermute | solution.py:477
  97.8 0.0 copy-start.2
  97.8 0.7 copy-done.2
  98.5 5.0 %shard_map.106 = (f32[1,1024]{1,0:T(1,128)}, f32[18,200,1408]{2,1,0:T(8,128)}, f32[216,512]{1,0:T(8,128)}) custom-call(s32[1,2]{1,0:T(1,128)} %bitcast.27, f32[200,1024]{1,0:T(8,128)} %bitcast.14, f32[1,1024]{1,0:T(1,128)} %bitcast.29, f32[18,200,1408]{2,1,0:T(8,128)} %get-tuple-element.37._, f32[200,512]{1,0:T(8,128)} %copy-done.2, ...), custom_call_target="tpu_custom_call", output_to_operand_aliasing={{1}: (3, {})} | custom-call | tf_op jit(solution)/shard_map/pallas_call | solution.py:464
  103.6 6.0 %collective-permute-start.5 = (f32[216,512]{1,0:T(8,128)}, f32[216,512]{1,0:T(8,128)S(1)}, u32[]{:S(2)}, u32[]{:S(2)}) collective-permute-start(f32[216,512]{1,0:T(8,128)} %get-tuple-element.43), channel_id=1, source_target_pairs={{0,1},{1,0},{2,3},{3,2},{4,5},{5,4},{6,7},{7,6},{8,9},{9,8},{10,11... | collective-permute-start | bytes 1327112 | tf_op jit(solution)/shard_map/ppermute | solution.py:477
  109.6 1.6 collective-permute-done.5.load_ref
  111.2 0.0 collective-permute-done.4.other_ref
  111.2 8.7 %shard_map.107 = (f32[200,512]{1,0:T(8,128)S(1)}, f32[1152,128]{1,0:T(8,128)S(1)}, f32[1152,128]{1,0:T(8,128)S(1)}, f32[1,1408]{1,0:T(1,128)S(1)}, f32[18,200,1408]{2,1,0:T(8,128)}) custom-call(s32[1]{0:T(128)} %bitcast.3.core_ref, f32[1152,128]{1,0:T(8,128)S(1)} %bitcast.17, ...), custom_call_target="tpu_custom_call", output_to_operand_aliasing={{4}: (5, {})} | custom-call | tf_op jit(solution)/shard_map/pallas_call | solution.py:464
  119.9 0.5 collective-permute-start.7
  120.3 1.6 collective-permute-done.7
  122.0 0.1 add.7
  122.0 18.0 %all_to_all.32 = f32[16,72,128]{2,1,0:T(8,128)S(1)} all-to-all(f32[16,72,128]{2,1,0:T(8,128)S(1)} %bitcast.22), channel_id=1, replica_groups=mesh['z'=8,'x'=4,'y'=4,'c'=2] {'y','x'}, dimensions={0} | all-to-all | bytes 1179648 | tf_op jit(solution)/shard_map/all_to_all | solution.py:482
  140.1 12.5 %all_to_all.33 = f32[8,72,128]{2,1,0:T(8,128)S(1)} all-to-all(f32[8,72,128]{2,1,0:T(8,128)S(1)} %broadcast_in_dim.10), channel_id=1, replica_groups=mesh['z'=8,'x'=4,'y'=4,'c'=2] {'z'}, dimensions={0} | all-to-all | bytes 589824 | tf_op jit(solution)/shard_map/all_to_all | solution.py:484
  152.6 13.6 %all_to_all.34 = f32[16,72,128]{2,1,0:T(8,128)S(1)} all-to-all(f32[16,72,128]{2,1,0:T(8,128)S(1)} %broadcast_in_dim.11), channel_id=1, replica_groups=mesh['z'=8,'x'=4,'y'=4,'c'=2] {'y','x'}, dimensions={0} | all-to-all | bytes 1179648 | tf_op jit(solution)/shard_map/all_to_all | solution.py:486
  166.3 4.5 %collective-permute-start.8 = (f32[1152,128]{1,0:T(8,128)S(1)}, f32[1152,128]{1,0:T(8,128)}, u32[]{:S(2)}, u32[]{:S(2)}) collective-permute-start(f32[1152,128]{1,0:T(8,128)S(1)} %bitcast.18), channel_id=1, source_target_pairs={{0,1},{1,0},{2,3},{3,2},{4,5},{5,4},{6,7},{7,6},{8,9},{9,8},{10,11... | collective-permute-start | bytes 1769480 | tf_op jit(solution)/shard_map/ppermute | solution.py:477
  170.8 0.0 collective-permute-start.6
  170.8 2.2 %collective-permute-done.6.back_hbm = f32[200,512]{1,0:T(8,128)S(1)} collective-permute-done((f32[200,512]{1,0:T(8,128)S(1)}, f32[200,512]{1,0:T(8,128)S(1)}, u32[]{:S(2)}, u32[]{:S(2)}) %collective-permute-start.6) | collective-permute-done | bytes 409632 | tf_op jit(solution)/shard_map/ppermute | solution.py:477
  173.0 0.0 copy-start.3
  173.0 0.7 copy-done.3
  173.8 4.6 %shard_map.108 = (f32[200,1024]{1,0:T(8,128)}, f32[1,1024]{1,0:T(1,128)}) custom-call(s32[1,2]{1,0:T(1,128)} %bitcast.28, f32[1,1024]{1,0:T(1,128)} %get-tuple-element.39.state_ref, f32[18,200,1408]{2,1,0:T(8,128)} %get-tuple-element.45.store, f32[200,512]{1,0:T(8,128)} %copy-done.3, s32[3,2,512]{2,1,0:T(2,128)} %bitcast.25), custom_call_target="tpu_custom_call" | custom-call | tf_op jit(solution)/shard_map/pallas_call | solution.py:464
  178.3 0.0 collective-permute-done.8.other_ref
  178.4 3.6 %shard_map.109 = (f32[200,1345]{1,0:T(8,128)}, f32[1345]{0:T(1024)}) custom-call(s32[1]{0:T(128)} %bitcast.3.core_ref, f32[1152,128]{1,0:T(8,128)S(1)} %bitcast.19, f32[1152,128]{1,0:T(8,128)} %collective-permute-done.8.other_ref, f32[18,200,1408]{2,1,0:T(8,128)} %get-tuple-element.45.store, f32[1,1408]{1,0:T(1,128)S(1)} %get-tuple-element.51.state_ref), custom_call_target="tpu_custom_call" | custom-call | tf_op jit(solution)/shard_map/pallas_call | solution.py:464
  (7 shorter events, 0.2 us)
Async XLA Ops:
  3.9 12.7 %collective-permute-start = (f32[216,256]{1,0:T(8,128)}, f32[216,256]{1,0:T(8,128)S(1)}, u32[]{:S(2)}, u32[]{:S(2)}) collective-permute-start(f32[216,256]{1,0:T(8,128)} %get-tuple-element.29), channel_id=1, source_target_pairs={{0,128},{32,160},{64,192},{96,224},{128,0},{160,32},{192,64},{224,... | collective-permute-start | bytes 663560 | tf_op jit(solution)/shard_map/ppermute | solution.py:477
  11.7 10.9 %collective-permute-start.1 = (f32[216,256]{1,0:T(8,128)}, f32[216,256]{1,0:T(8,128)S(1)}, u32[]{:S(2)}, u32[]{:S(2)}) collective-permute-start(f32[216,256]{1,0:T(8,128)} %get-tuple-element.30), channel_id=1, source_target_pairs={{0,128},{32,160},{64,192},{96,224},{128,0},{160,32},{192,64},{224,... | collective-permute-start | bytes 663560 | tf_op jit(solution)/shard_map/ppermute | solution.py:477
  12.5 1.1 copy-start
  13.6 1.3 copy-start.1
  28.6 4.4 %collective-permute-start.3 = (f32[1152,128]{1,0:T(8,128)S(1)}, f32[1152,128]{1,0:T(8,128)S(1)}, u32[]{:S(2)}, u32[]{:S(2)}) collective-permute-start(f32[1152,128]{1,0:T(8,128)S(1)} %get-tuple-element.41), channel_id=1, source_target_pairs={{0,1},{1,0},{2,3},{3,2},{4,5},{5,4},{6,7},{7,6},{8,9},{9,8},{10,11... | collective-permute-start | bytes 1769480 | tf_op jit(solution)/shard_map/ppermute | solution.py:477
  74.6 13.8 %all-to-all-start.2 = ((f32[16,72,128]{2,1,0:T(8,128)}), f32[16,72,128]{2,1,0:T(8,128)S(1)}, u32[]{:S(2)}, u32[]{:S(2)}) async-start(f32[16,72,128]{2,1,0:T(8,128)} %broadcast_in_dim.9), calls=%async_computation.2 | async-start | bytes 1179648 | tf_op jit(solution)/shard_map/all_to_all | solution.py:486
  79.1 18.7 %collective-permute-start.2 = (f32[200,512]{1,0:T(8,128)S(1)}, f32[200,512]{1,0:T(8,128)S(1)}, u32[]{:S(2)}, u32[]{:S(2)}) collective-permute-start(f32[200,512]{1,0:T(8,128)S(1)} %get-tuple-element.38), channel_id=1, source_target_pairs={{0,128},{32,160},{64,192},{96,224},{128,0},{160,32},{192,64},{224,... | collective-permute-start | bytes 1228808 | tf_op jit(solution)/shard_map/ppermute | solution.py:477
  88.4 22.8 %collective-permute-start.4 = (f32[1152,128]{1,0:T(8,128)S(1)}, f32[1152,128]{1,0:T(8,128)}, u32[]{:S(2)}, u32[]{:S(2)}) collective-permute-start(f32[1152,128]{1,0:T(8,128)S(1)} %bitcast.16), channel_id=1, source_target_pairs={{0,1},{1,0},{2,3},{3,2},{4,5},{5,4},{6,7},{7,6},{8,9},{9,8},{10,11... | collective-permute-start | bytes 1769480 | tf_op jit(solution)/shard_map/ppermute | solution.py:477
  97.8 0.8 copy-start.2
  103.6 7.6 %collective-permute-start.5 = (f32[216,512]{1,0:T(8,128)}, f32[216,512]{1,0:T(8,128)S(1)}, u32[]{:S(2)}, u32[]{:S(2)}) collective-permute-start(f32[216,512]{1,0:T(8,128)} %get-tuple-element.43), channel_id=1, source_target_pairs={{0,1},{1,0},{2,3},{3,2},{4,5},{5,4},{6,7},{7,6},{8,9},{9,8},{10,11... | collective-permute-start | bytes 1327112 | tf_op jit(solution)/shard_map/ppermute | solution.py:477
  119.9 2.1 %collective-permute-start.7 = (f32[1152,128]{1,0:T(8,128)S(1)}, f32[1152,128]{1,0:T(8,128)S(1)}, u32[]{:S(2)}, u32[]{:S(2)}) collective-permute-start(f32[1152,128]{1,0:T(8,128)S(1)} %get-tuple-element.50), channel_id=1, source_target_pairs={{0,1},{1,0},{2,3},{3,2},{4,5},{5,4},{6,7},{7,6},{8,9},{9,8},{10,11... | collective-permute-start | bytes 1769480 | tf_op jit(solution)/shard_map/ppermute | solution.py:477
  166.3 12.1 %collective-permute-start.8 = (f32[1152,128]{1,0:T(8,128)S(1)}, f32[1152,128]{1,0:T(8,128)}, u32[]{:S(2)}, u32[]{:S(2)}) collective-permute-start(f32[1152,128]{1,0:T(8,128)S(1)} %bitcast.18), channel_id=1, source_target_pairs={{0,1},{1,0},{2,3},{3,2},{4,5},{5,4},{6,7},{7,6},{8,9},{9,8},{10,11... | collective-permute-start | bytes 1769480 | tf_op jit(solution)/shard_map/ppermute | solution.py:477
  170.8 2.2 %collective-permute-start.6 = (f32[200,512]{1,0:T(8,128)S(1)}, f32[200,512]{1,0:T(8,128)S(1)}, u32[]{:S(2)}, u32[]{:S(2)}) collective-permute-start(f32[200,512]{1,0:T(8,128)S(1)} %get-tuple-element.46), channel_id=1, source_target_pairs={{0,1},{1,0},{2,3},{3,2},{4,5},{5,4},{6,7},{7,6},{8,9},{9,8},{10,11... | collective-permute-start | bytes 1228808 | tf_op jit(solution)/shard_map/ppermute | solution.py:477
  173.0 0.8 copy-start.3

commit v5 on v3

--- a/solution.py
+++ b/solution.py
@@ -15,6 +15,8 @@
 ROWS = 1024
 DIM = 200
 HALF = DIM // 2
+LOW = 208
+STACK = 2 * LOW
 REL = 1345
 RELP = 1408
 NEG = 1000
@@ -59,6 +61,19 @@
     return dot(a[0], b[0], dims) + (dot(a[1], b[0], dims) + dot(a[0], b[1], dims))
 
 
+def stack(ref, value):
+    high, low = halves(value)
+    gap = jnp.zeros((LOW - DIM, value.shape[1]), BF16)
+    ref[0:DIM, :], ref[DIM:LOW, :] = high, gap
+    ref[LOW : LOW + DIM, :], ref[LOW + DIM : STACK, :] = low, gap
+
+
+def stack_dot(parts, high, low=None, dims=((1,), (0,))):
+    both = dot(parts, high, dims)
+    total = both[0:DIM] + both[LOW : LOW + DIM]
+    return total if low is None else total + dot(parts[0:DIM], low, dims)
+
+
 def one_hot(ids, count):
     places = lax.broadcasted_iota(jnp.int32, (count, ids.shape[1]), 0)
     return jnp.where(places == ids, 1.0, 0.0).astype(BF16)
@@ -84,16 +99,11 @@
     return copies
 
 
-def write_payload(out_refs, parts, edges_ref, negatives_ref, count, which):
-    source = live_sources(edges_ref, count, which)
-    pick = one_hot(source, ROWS)
-    high, low = parts
-    rows = dot(high, pick) + dot(low, pick)
+def write_lists(refs, edges_ref, negatives_ref, which):
     first = 0
-    for ref in out_refs:
+    for ref in refs:
         wide = ref.shape[1]
         span = slice(first, first + wide)
-        ref[0:DIM, :] = rows[:, span]
         ref[ID_ROW : ID_ROW + 1, :] = edges_ref[1, which : which + 1, span].astype(F32)
         ref[ID_ROW + 1 : ID_ROW + 2, :] = edges_ref[2, which : which + 1, span].astype(F32)
         ref[ID_ROW + 2 : HIST_ROW, :] = jnp.zeros((HIST_ROW - ID_ROW - 2, wide), F32)
@@ -103,6 +113,11 @@
                 negatives_ref[which, k : k + 1, :]
             )
         first += wide
+
+
+def source_rows(parts_ref, edges_ref, count, which, first, wide):
+    source = live_sources(edges_ref, count, which)[:, first : first + wide]
+    return stack_dot(parts_ref[...], one_hot(source, ROWS))
 
 
 def prepare(
@@ -117,17 +132,23 @@
     negatives_ref,
     first_ref,
     second_ref,
+    parts_ref,
     sem,
 ):
-    copies = fetch(
-        sem, (edges_hbm, edges_ref), (table_hbm, table_ref), (negatives_hbm, negatives_ref)
-    )
+    negatives_copy, edges_copy, table_copy = fetch(
+        sem, (negatives_hbm, negatives_ref), (edges_hbm, edges_ref), (table_hbm, table_ref)
+    )
+    negatives_copy.wait()
+    edges_copy.wait()
+    write_lists((first_ref, second_ref), edges_ref, negatives_ref, 0)
+    table_copy.wait()
+    stack(parts_ref, table_ref[...])
+    count = counts_ref[0, 0]
+    first_ref[0:DIM, :] = source_rows(parts_ref, edges_ref, count, 0, 0, EARLY)
+    copies = fetch(sem, (first_ref, first_out))
+    second_ref[0:DIM, :] = source_rows(parts_ref, edges_ref, count, 0, EARLY, EDGES - EARLY)
+    copies += fetch(sem.at[1:2], (second_ref, second_out))
     for copy in copies:
-        copy.wait()
-    pieces = (first_ref, second_ref)
-    parts = halves(table_ref[...])
-    write_payload(pieces, parts, edges_ref, negatives_ref, counts_ref[0, 0], 0)
-    for copy in fetch(sem, (first_ref, first_out), (second_ref, second_out)):
         copy.wait()
 
 
@@ -288,8 +309,7 @@
         copy.wait()
 
 
-def step_relations(core, mine_ref, other_ref, rel_ref, state_ref, flat, rel_out, state_out):
-    join_flat(core, mine_ref, other_ref, flat)
+def step_tiles(rel_ref, state_ref, flat, rel_out, state_out):
     for tile in range(RELP // 128):
         lanes = slice(tile * 128, (tile + 1) * 128)
         rel_out[:, lanes], state_out[:, lanes] = adagrad(
@@ -316,11 +336,12 @@
         sem, (store.at[RELATION], old_ref), (entities_of(store, TABLE), grad_ref)
     )
     core = core_ref[0]
+    join_flat(core, mine_ref, other_ref, flat)
     rel_copy.wait()
-    step_relations(core, mine_ref, other_ref, old_ref, state_ref, flat, rel_ref, state_out)
-    (rel_copy,) = fetch(sem, (rel_ref, store.at[RELATION]))
+    step_tiles(old_ref, state_ref, flat, rel_ref, state_out)
     table_copy.wait()
     table_parts = halves(grad_ref[...])
+    (rel_copy,) = fetch(sem, (rel_ref, store.at[RELATION]))
 
     def put(value):
         grad_ref[...] = value
@@ -333,10 +354,12 @@
         copy.wait()
 
 
-def step_entities(table_ref, state_ref, grad_ref, back_ref, edges_ref, count, which):
+def step_entities(
+    table_ref, state_ref, grad_ref, back_ref, parts_ref, edges_ref, count, which
+):
     pick = one_hot(live_sources(edges_ref, count, which), ROWS)
-    high, low = halves(back_ref[...])
-    grad = grad_ref[...] + (dot(high, pick, NT) + dot(low, pick, NT))
+    stack(parts_ref, back_ref[...])
+    grad = grad_ref[...] + stack_dot(parts_ref[...], pick, None, NT)
     return adagrad(table_ref[...], state_ref[...], grad)
 
 
@@ -356,6 +379,8 @@
     back_ref,
     edges_ref,
     negatives_ref,
+    parts_ref,
+    tables_ref,
     sem,
 ):
     copies = fetch(
@@ -369,11 +394,13 @@
     for copy in copies:
         copy.wait()
     table, state_out[...] = step_entities(
-        table_ref, state_ref, grad_ref, back_ref, edges_ref, counts_ref[0, 0], 0
+        table_ref, state_ref, grad_ref, back_ref, parts_ref, edges_ref, counts_ref[0, 0], 0
     )
     table_ref[...] = table
     (copy,) = fetch(sem, (table_ref, entities_of(store, TABLE)))
-    write_payload((load,), halves(table), edges_ref, negatives_ref, counts_ref[0, 1], 1)
+    stack(tables_ref, table)
+    write_lists((load,), edges_ref, negatives_ref, 1)
+    load[0:DIM, :] = source_rows(tables_ref, edges_ref, counts_ref[0, 1], 1, 0, EDGES)
     copy.wait()
 
 
@@ -389,6 +416,7 @@
     grad_ref,
     back_ref,
     edges_ref,
+    parts_ref,
     sem,
 ):
     copies = fetch(
@@ -401,7 +429,7 @@
     for copy in copies:
         copy.wait()
     table, state_out[...] = step_entities(
-        table_ref, state_ref, grad_ref, back_ref, edges_ref, counts_ref[0, 1], 1
+        table_ref, state_ref, grad_ref, back_ref, parts_ref, edges_ref, counts_ref[0, 1], 1
     )
     table_ref[...] = table
     (copy,) = fetch(sem, (table_ref, table_out))
@@ -423,10 +451,11 @@
     sem,
 ):
     (copy,) = fetch(sem, (store.at[RELATION], old_ref))
+    join_flat(core_ref[0], mine_ref, other_ref, flat)
     copy.wait()
-    step_relations(core_ref[0], mine_ref, other_ref, old_ref, state_ref, flat, rel, state)
+    step_tiles(old_ref, state_ref, flat, rel, state)
     rel_out[...] = rel[:, 0:REL]
-    state_out[...] = state[:, 0:REL]
+    state_out[...] = state[0, 0:REL]
 
 
 def work_shapes(wide):
@@ -463,11 +492,11 @@
 
 def total(send, keep):
     part = (keep + across(send, C, 1)).reshape(16, SIDE // 16, 128)
-    part = lax.all_to_all(part, (X, Y), 0, 0, tiled=True).sum(axis=0)
+    part = lax.all_to_all(part, (Y, X), 0, 0, tiled=True).sum(axis=0)
     part = jnp.broadcast_to(part[None], (8, *part.shape))
     part = lax.all_to_all(part, Z, 0, 0, tiled=True).sum(axis=0)
     part = jnp.broadcast_to(part[None], (16, *part.shape))
-    part = lax.all_to_all(part, (X, Y), 0, 0, tiled=True)
+    part = lax.all_to_all(part, (Y, X), 0, 0, tiled=True)
     mine = part.reshape(SIDE, 128)
     return mine, across(mine, C, 1)
 
@@ -482,7 +511,8 @@
     narrow = shape(DIM, ROWS, dtype=BF16)
     wide_rel = shape(DIM, RELP, dtype=BF16)
     vmem = pltpu.VMEM
-    table_mem = vmem((DIM, ROWS), F32)
+    table_mem, back_parts_mem = vmem((DIM, ROWS), F32), vmem((STACK, EDGES), BF16)
+    parts_mem = vmem((STACK, ROWS), BF16)
     flat_mem = vmem((FLAT, 128), F32)
     back_mem, rel_mem = vmem((DIM, EDGES), F32), vmem((DIM, RELP), F32)
     edge_mem, negative_mem = vmem((3, 2, EDGES), jnp.int32), vmem(negatives.shape, jnp.int32)
@@ -491,7 +521,8 @@
         "shhh",
         [("h", shape(LOAD, EARLY)), ("h", shape(LOAD, late))],
         (counts, table, edges, negatives),
-        [table_mem, edge_mem, negative_mem, vmem((LOAD, EARLY), F32), vmem((LOAD, late), F32)],
+        [table_mem, edge_mem, negative_mem, vmem((LOAD, EARLY), F32), vmem((LOAD, late), F32)]
+        + [parts_mem],
         3,
         63 << 20,
     )
@@ -533,7 +564,7 @@
         "shvhhhh",
         [("v", shape(1, ROWS)), store_out, ("v", shape(LOAD, EDGES))],
         (counts, table, state, store, back, edges, negatives),
-        [table_mem, table_mem, back_mem, edge_mem, negative_mem],
+        [table_mem, table_mem, back_mem, edge_mem, negative_mem, back_parts_mem, parts_mem],
         5,
         63 << 20,
         {3: 1},
@@ -556,19 +587,19 @@
         "svhhh",
         [("h", grown), ("v", shape(1, ROWS))],
         (counts, state, store, back, edges),
-        [table_mem, table_mem, back_mem, edge_mem],
+        [table_mem, table_mem, back_mem, edge_mem, back_parts_mem],
         4,
         63 << 20,
     )
     rel, rel_state = call(
         last_relations,
         "svvhv",
-        [("v", shape(DIM, REL)), ("v", shape(1, REL))],
+        [("v", shape(DIM, REL)), ("v", shape(REL))],
         (core, mine, other, store, rel_state),
         [flat_mem, rel_mem, rel_mem, vmem((1, RELP), F32)],
         1,
     )
-    return table.T, state.reshape(ROWS), rel.T, rel_state.reshape(REL)
+    return table.T, state.reshape(ROWS), rel.T, rel_state
 
 
 def solution(mesh):

time: 184 us -> 182 us (0.989)
  no operation moved by 1% of the time
where the time goes in v5:
time: 182 us
  blocking collectives  84.7 us (47%)
  Pallas kernels  35.6 us (20%)
  starting transfers between devices  32.6 us (18%)
  waiting for transfers between devices  22 us (12%)
  local copies, waits for them, and re-layouts  5.53 us (3%)
    all_to_all x2, blocking collectives, total(): part = lax.all_to_all(part, (Y, X), 0, 0, tiled=True).sum(axis=0)  36 us
    pallas_call x8, Pallas kernels, call(): pl.pallas_call(body, out_shape=[out for _, out in outs], in_specs=[SPECS[...  35.6 us
    all_to_all x2, blocking collectives, total(): part = lax.all_to_all(part, Z, 0, 0, tiled=True).sum(axis=0)  35.1 us
    ppermute x9, starting transfers between devices, across(): return lax.ppermute(value, axis, [(i, i ^ apart) for i in range(count)])  28.1 us
    ppermute x9, waiting for transfers between devices, across(): return lax.ppermute(value, axis, [(i, i ^ apart) for i in range(count)])  14.6 us
    all_to_all x1, blocking collectives, total(): part = lax.all_to_all(part, (Y, X), 0, 0, tiled=True)  13.6 us
    all_to_all x1, waiting for transfers between devices, total(): part = lax.all_to_all(part, (Y, X), 0, 0, tiled=True)  7.35 us
    all_to_all x1, starting transfers between devices, total(): part = lax.all_to_all(part, (Y, X), 0, 0, tiled=True)  4.45 us
  transfers between devices with their start and end apart: 10, of which 8 were waited for; matrix products, arithmetic and copies ran while one was open for 0% of the time, Pallas kernels for 8%

profile of v5, /device:TPU:1, one launch (start us, length us, event | category | flops | bytes accessed | tf_op | source)
XLA Modules:
  0.0 181.6 jit_solution(5562660061851347487)
XLA Ops:
  0.6 3.3 %shard_map.102 = (f32[216,256]{1,0:T(8,128)}, f32[216,256]{1,0:T(8,128)}) custom-call(s32[1,2]{1,0:T(1,128)} %bitcast.26, f32[200,1024]{1,0:T(8,128)} %bitcast.13, s32[3,2,512]{2,1,0:T(2,128)} %bitcast.23, s32[2,4,1000]{2,1,0:T(4,128)} %negatives_hbm.3), custom_call_target="tpu_custom_call" | custom-call | tf_op jit(solution)/shard_map/pallas_call | solution.py:477
  3.9 7.8 %collective-permute-start = (f32[216,256]{1,0:T(8,128)}, f32[216,256]{1,0:T(8,128)S(1)}, u32[]{:S(2)}, u32[]{:S(2)}) collective-permute-start(f32[216,256]{1,0:T(8,128)} %get-tuple-element.31), channel_id=1, source_target_pairs={{0,128},{32,160},{64,192},{96,224},{128,0},{160,32},{192,64},{224,... | collective-permute-start | bytes 663560 | tf_op jit(solution)/shard_map/ppermute | solution.py:490
  11.7 0.1 collective-permute-start.1
  11.8 0.7 reshape.38.state_ref
  12.5 0.0 copy-start
  12.5 1.1 copy-done
  13.6 0.0 copy-start.1
  13.7 1.2 copy-done.1
  14.9 1.1 shard_map.103
  16.0 0.6 collective-permute-done.load_ref.early_ref
  16.6 3.9 %shard_map.104 = (f32[200,256]{1,0:T(8,128)S(1)}, f32[200,256]{1,0:T(8,128)S(1)}, f32[18,200,1408]{2,1,0:T(8,128)}) custom-call(f32[216,256]{1,0:T(8,128)S(1)} %collective-permute-done.load_ref.early_ref, bf16[200,1024]{1,0:T(8,128)(2,1)S(1)} %get-tuple-element.33.high_ref, ...), custom_call_target="tpu_custom_call", output_to_operand_aliasing={{2}: (5, {})} | custom-call | tf_op jit(solution)/shard_map/pallas_call | solution.py:477
  20.5 2.1 %collective-permute-done.1.load_ref = f32[216,256]{1,0:T(8,128)S(1)} collective-permute-done((f32[216,256]{1,0:T(8,128)}, f32[216,256]{1,0:T(8,128)S(1)}, u32[]{:S(2)}, u32[]{:S(2)}) %collective-permute-start.1) | collective-permute-done | bytes 221216 | tf_op jit(solution)/shard_map/ppermute | solution.py:490
  22.6 5.6 %shard_map.105 = (f32[200,512]{1,0:T(8,128)S(1)}, f32[1152,128]{1,0:T(8,128)S(1)}, f32[1152,128]{1,0:T(8,128)S(1)}, f32[18,200,1408]{2,1,0:T(8,128)}) custom-call(s32[1]{0:T(128)} %bitcast.3.core_ref, f32[216,256]{1,0:T(8,128)S(1)} %collective-permute-done.load_ref.early_ref, ...), custom_call_target="tpu_custom_call", output_to_operand_aliasing={{3}: (9, {})} | custom-call | tf_op jit(solution)/shard_map/pallas_call | solution.py:477
  28.2 2.8 %collective-permute-start.3 = (f32[1152,128]{1,0:T(8,128)S(1)}, f32[1152,128]{1,0:T(8,128)S(1)}, u32[]{:S(2)}, u32[]{:S(2)}) collective-permute-start(f32[1152,128]{1,0:T(8,128)S(1)} %get-tuple-element.45), channel_id=1, source_target_pairs={{0,1},{1,0},{2,3},{3,2},{4,5},{5,4},{6,7},{7,6},{8,9},{9,8},{10,11... | collective-permute-start | bytes 1769480 | tf_op jit(solution)/shard_map/ppermute | solution.py:490
  31.0 1.6 collective-permute-done.3
  32.6 0.1 add.6
  32.7 18.0 %all_to_all.30 = f32[16,72,128]{2,1,0:T(8,128)S(1)} all-to-all(f32[16,72,128]{2,1,0:T(8,128)S(1)} %bitcast.21), channel_id=1, replica_groups=mesh['z'=8,'x'=4,'y'=4,'c'=2] {'y','x'}, dimensions={0} | all-to-all | bytes 1179648 | tf_op jit(solution)/shard_map/all_to_all | solution.py:495
  50.7 22.6 %all_to_all.31 = f32[8,72,128]{2,1,0:T(8,128)S(1)} all-to-all(f32[8,72,128]{2,1,0:T(8,128)S(1)} %broadcast_in_dim.8), channel_id=1, replica_groups=mesh['z'=8,'x'=4,'y'=4,'c'=2] {'z'}, dimensions={0} | all-to-all | bytes 589824 | tf_op jit(solution)/shard_map/all_to_all | solution.py:497
  73.4 0.9 broadcast_in_dim.9
  74.3 4.4 %all-to-all-start.2 = ((f32[16,72,128]{2,1,0:T(8,128)}), f32[16,72,128]{2,1,0:T(8,128)S(1)}, u32[]{:S(2)}, u32[]{:S(2)}) async-start(f32[16,72,128]{2,1,0:T(8,128)} %broadcast_in_dim.9), calls=%async_computation.2 | async-start | bytes 1179648 | tf_op jit(solution)/shard_map/all_to_all | solution.py:499
  78.7 2.0 %collective-permute-start.2 = (f32[200,512]{1,0:T(8,128)S(1)}, f32[200,512]{1,0:T(8,128)S(1)}, u32[]{:S(2)}, u32[]{:S(2)}) collective-permute-start(f32[200,512]{1,0:T(8,128)S(1)} %get-tuple-element.42), channel_id=1, source_target_pairs={{0,128},{32,160},{64,192},{96,224},{128,0},{160,32},{192,64},{224,... | collective-permute-start | bytes 1228808 | tf_op jit(solution)/shard_map/ppermute | solution.py:490
  80.7 7.4 %all-to-all-done.2 = f32[16,72,128]{2,1,0:T(8,128)S(1)} async-done(((f32[16,72,128]{2,1,0:T(8,128)}), f32[16,72,128]{2,1,0:T(8,128)S(1)}, u32[]{:S(2)}, u32[]{:S(2)}) %all-to-all-start.2) | async-done | bytes 589856 | tf_op jit(solution)/shard_map/all_to_all | solution.py:499
  88.1 4.5 %collective-permute-start.4 = (f32[1152,128]{1,0:T(8,128)S(1)}, f32[1152,128]{1,0:T(8,128)}, u32[]{:S(2)}, u32[]{:S(2)}) collective-permute-start(f32[1152,128]{1,0:T(8,128)S(1)} %bitcast.16), channel_id=1, source_target_pairs={{0,1},{1,0},{2,3},{3,2},{4,5},{5,4},{6,7},{7,6},{8,9},{9,8},{10,11... | collective-permute-start | bytes 1769480 | tf_op jit(solution)/shard_map/ppermute | solution.py:490
  92.6 4.8 %collective-permute-done.2.back_hbm = f32[200,512]{1,0:T(8,128)S(1)} collective-permute-done((f32[200,512]{1,0:T(8,128)S(1)}, f32[200,512]{1,0:T(8,128)S(1)}, u32[]{:S(2)}, u32[]{:S(2)}) %collective-permute-start.2) | collective-permute-done | bytes 409632 | tf_op jit(solution)/shard_map/ppermute | solution.py:490
  97.4 0.0 copy-start.2
  97.4 0.7 copy-done.2
  98.2 5.0 %shard_map.106 = (f32[1,1024]{1,0:T(1,128)}, f32[18,200,1408]{2,1,0:T(8,128)}, f32[216,512]{1,0:T(8,128)}) custom-call(s32[1,2]{1,0:T(1,128)} %bitcast.27, f32[200,1024]{1,0:T(8,128)} %bitcast.14, f32[1,1024]{1,0:T(1,128)} %bitcast.29, f32[18,200,1408]{2,1,0:T(8,128)} %get-tuple-element.41._, f32[200,512]{1,0:T(8,128)} %copy-done.2, ...), custom_call_target="tpu_custom_call", output_to_operand_aliasing={{1}: (3, {})} | custom-call | tf_op jit(solution)/shard_map/pallas_call | solution.py:477
  103.2 6.0 %collective-permute-start.5 = (f32[216,512]{1,0:T(8,128)}, f32[216,512]{1,0:T(8,128)S(1)}, u32[]{:S(2)}, u32[]{:S(2)}) collective-permute-start(f32[216,512]{1,0:T(8,128)} %get-tuple-element.47), channel_id=1, source_target_pairs={{0,1},{1,0},{2,3},{3,2},{4,5},{5,4},{6,7},{7,6},{8,9},{9,8},{10,11... | collective-permute-start | bytes 1327112 | tf_op jit(solution)/shard_map/ppermute | solution.py:490
  109.2 1.6 collective-permute-done.5.load_ref
  110.8 0.0 collective-permute-done.4.other_ref
  110.8 8.6 %shard_map.107 = (f32[200,512]{1,0:T(8,128)S(1)}, f32[1152,128]{1,0:T(8,128)S(1)}, f32[1152,128]{1,0:T(8,128)S(1)}, f32[1,1408]{1,0:T(1,128)S(1)}, f32[18,200,1408]{2,1,0:T(8,128)}) custom-call(s32[1]{0:T(128)} %bitcast.3.core_ref, f32[1152,128]{1,0:T(8,128)S(1)} %bitcast.17, ...), custom_call_target="tpu_custom_call", output_to_operand_aliasing={{4}: (5, {})} | custom-call | tf_op jit(solution)/shard_map/pallas_call | solution.py:477
  119.4 0.5 collective-permute-start.7
  119.9 1.6 collective-permute-done.7
  121.5 0.1 add.7
  121.6 18.0 %all_to_all.32 = f32[16,72,128]{2,1,0:T(8,128)S(1)} all-to-all(f32[16,72,128]{2,1,0:T(8,128)S(1)} %bitcast.22), channel_id=1, replica_groups=mesh['z'=8,'x'=4,'y'=4,'c'=2] {'y','x'}, dimensions={0} | all-to-all | bytes 1179648 | tf_op jit(solution)/shard_map/all_to_all | solution.py:495
  139.6 12.5 %all_to_all.33 = f32[8,72,128]{2,1,0:T(8,128)S(1)} all-to-all(f32[8,72,128]{2,1,0:T(8,128)S(1)} %broadcast_in_dim.10), channel_id=1, replica_groups=mesh['z'=8,'x'=4,'y'=4,'c'=2] {'z'}, dimensions={0} | all-to-all | bytes 589824 | tf_op jit(solution)/shard_map/all_to_all | solution.py:497
  152.2 13.6 %all_to_all.34 = f32[16,72,128]{2,1,0:T(8,128)S(1)} all-to-all(f32[16,72,128]{2,1,0:T(8,128)S(1)} %broadcast_in_dim.11), channel_id=1, replica_groups=mesh['z'=8,'x'=4,'y'=4,'c'=2] {'y','x'}, dimensions={0} | all-to-all | bytes 1179648 | tf_op jit(solution)/shard_map/all_to_all | solution.py:499
  165.8 4.5 %collective-permute-start.8 = (f32[1152,128]{1,0:T(8,128)S(1)}, f32[1152,128]{1,0:T(8,128)}, u32[]{:S(2)}, u32[]{:S(2)}) collective-permute-start(f32[1152,128]{1,0:T(8,128)S(1)} %bitcast.18), channel_id=1, source_target_pairs={{0,1},{1,0},{2,3},{3,2},{4,5},{5,4},{6,7},{7,6},{8,9},{9,8},{10,11... | collective-permute-start | bytes 1769480 | tf_op jit(solution)/shard_map/ppermute | solution.py:490
  170.3 0.0 collective-permute-start.6
  170.3 2.2 %collective-permute-done.6.back_hbm = f32[200,512]{1,0:T(8,128)S(1)} collective-permute-done((f32[200,512]{1,0:T(8,128)S(1)}, f32[200,512]{1,0:T(8,128)S(1)}, u32[]{:S(2)}, u32[]{:S(2)}) %collective-permute-start.6) | collective-permute-done | bytes 409632 | tf_op jit(solution)/shard_map/ppermute | solution.py:490
  172.6 0.0 copy-start.3
  172.6 0.7 copy-done.3
  173.3 4.6 %shard_map.108 = (f32[200,1024]{1,0:T(8,128)}, f32[1,1024]{1,0:T(1,128)}) custom-call(s32[1,2]{1,0:T(1,128)} %bitcast.28, f32[1,1024]{1,0:T(1,128)} %get-tuple-element.43.state_ref, f32[18,200,1408]{2,1,0:T(8,128)} %get-tuple-element.49.store, f32[200,512]{1,0:T(8,128)} %copy-done.3, s32[3,2,512]{2,1,0:T(2,128)} %bitcast.25), custom_call_target="tpu_custom_call" | custom-call | tf_op jit(solution)/shard_map/pallas_call | solution.py:477
  177.9 0.0 collective-permute-done.8.other_ref
  177.9 3.6 %shard_map.109 = (f32[200,1345]{1,0:T(8,128)}, f32[1345]{0:T(1024)}) custom-call(s32[1]{0:T(128)} %bitcast.3.core_ref, f32[1152,128]{1,0:T(8,128)S(1)} %bitcast.19, f32[1152,128]{1,0:T(8,128)} %collective-permute-done.8.other_ref, f32[18,200,1408]{2,1,0:T(8,128)} %get-tuple-element.49.store, f32[1,1408]{1,0:T(1,128)S(1)} %get-tuple-element.55.state_ref), custom_call_target="tpu_custom_call" | custom-call | tf_op jit(solution)/shard_map/pallas_call | solution.py:477
  (7 shorter events, 0.2 us)
Async XLA Ops:
  3.9 12.7 %collective-permute-start = (f32[216,256]{1,0:T(8,128)}, f32[216,256]{1,0:T(8,128)S(1)}, u32[]{:S(2)}, u32[]{:S(2)}) collective-permute-start(f32[216,256]{1,0:T(8,128)} %get-tuple-element.31), channel_id=1, source_target_pairs={{0,128},{32,160},{64,192},{96,224},{128,0},{160,32},{192,64},{224,... | collective-permute-start | bytes 663560 | tf_op jit(solution)/shard_map/ppermute | solution.py:490
  11.7 10.9 %collective-permute-start.1 = (f32[216,256]{1,0:T(8,128)}, f32[216,256]{1,0:T(8,128)S(1)}, u32[]{:S(2)}, u32[]{:S(2)}) collective-permute-start(f32[216,256]{1,0:T(8,128)} %get-tuple-element.32), channel_id=1, source_target_pairs={{0,128},{32,160},{64,192},{96,224},{128,0},{160,32},{192,64},{224,... | collective-permute-start | bytes 663560 | tf_op jit(solution)/shard_map/ppermute | solution.py:490
  12.5 1.1 copy-start
  13.6 1.3 copy-start.1
  28.2 4.4 %collective-permute-start.3 = (f32[1152,128]{1,0:T(8,128)S(1)}, f32[1152,128]{1,0:T(8,128)S(1)}, u32[]{:S(2)}, u32[]{:S(2)}) collective-permute-start(f32[1152,128]{1,0:T(8,128)S(1)} %get-tuple-element.45), channel_id=1, source_target_pairs={{0,1},{1,0},{2,3},{3,2},{4,5},{5,4},{6,7},{7,6},{8,9},{9,8},{10,11... | collective-permute-start | bytes 1769480 | tf_op jit(solution)/shard_map/ppermute | solution.py:490
  74.3 13.8 %all-to-all-start.2 = ((f32[16,72,128]{2,1,0:T(8,128)}), f32[16,72,128]{2,1,0:T(8,128)S(1)}, u32[]{:S(2)}, u32[]{:S(2)}) async-start(f32[16,72,128]{2,1,0:T(8,128)} %broadcast_in_dim.9), calls=%async_computation.2 | async-start | bytes 1179648 | tf_op jit(solution)/shard_map/all_to_all | solution.py:499
  78.7 18.7 %collective-permute-start.2 = (f32[200,512]{1,0:T(8,128)S(1)}, f32[200,512]{1,0:T(8,128)S(1)}, u32[]{:S(2)}, u32[]{:S(2)}) collective-permute-start(f32[200,512]{1,0:T(8,128)S(1)} %get-tuple-element.42), channel_id=1, source_target_pairs={{0,128},{32,160},{64,192},{96,224},{128,0},{160,32},{192,64},{224,... | collective-permute-start | bytes 1228808 | tf_op jit(solution)/shard_map/ppermute | solution.py:490
  88.1 22.8 %collective-permute-start.4 = (f32[1152,128]{1,0:T(8,128)S(1)}, f32[1152,128]{1,0:T(8,128)}, u32[]{:S(2)}, u32[]{:S(2)}) collective-permute-start(f32[1152,128]{1,0:T(8,128)S(1)} %bitcast.16), channel_id=1, source_target_pairs={{0,1},{1,0},{2,3},{3,2},{4,5},{5,4},{6,7},{7,6},{8,9},{9,8},{10,11... | collective-permute-start | bytes 1769480 | tf_op jit(solution)/shard_map/ppermute | solution.py:490
  97.4 0.8 copy-start.2
  103.2 7.6 %collective-permute-start.5 = (f32[216,512]{1,0:T(8,128)}, f32[216,512]{1,0:T(8,128)S(1)}, u32[]{:S(2)}, u32[]{:S(2)}) collective-permute-start(f32[216,512]{1,0:T(8,128)} %get-tuple-element.47), channel_id=1, source_target_pairs={{0,1},{1,0},{2,3},{3,2},{4,5},{5,4},{6,7},{7,6},{8,9},{9,8},{10,11... | collective-permute-start | bytes 1327112 | tf_op jit(solution)/shard_map/ppermute | solution.py:490
  119.4 2.1 %collective-permute-start.7 = (f32[1152,128]{1,0:T(8,128)S(1)}, f32[1152,128]{1,0:T(8,128)S(1)}, u32[]{:S(2)}, u32[]{:S(2)}) collective-permute-start(f32[1152,128]{1,0:T(8,128)S(1)} %get-tuple-element.54), channel_id=1, source_target_pairs={{0,1},{1,0},{2,3},{3,2},{4,5},{5,4},{6,7},{7,6},{8,9},{9,8},{10,11... | collective-permute-start | bytes 1769480 | tf_op jit(solution)/shard_map/ppermute | solution.py:490
  165.8 12.1 %collective-permute-start.8 = (f32[1152,128]{1,0:T(8,128)S(1)}, f32[1152,128]{1,0:T(8,128)}, u32[]{:S(2)}, u32[]{:S(2)}) collective-permute-start(f32[1152,128]{1,0:T(8,128)S(1)} %bitcast.18), channel_id=1, source_target_pairs={{0,1},{1,0},{2,3},{3,2},{4,5},{5,4},{6,7},{7,6},{8,9},{9,8},{10,11... | collective-permute-start | bytes 1769480 | tf_op jit(solution)/shard_map/ppermute | solution.py:490
  170.3 2.2 %collective-permute-start.6 = (f32[200,512]{1,0:T(8,128)S(1)}, f32[200,512]{1,0:T(8,128)S(1)}, u32[]{:S(2)}, u32[]{:S(2)}) collective-permute-start(f32[200,512]{1,0:T(8,128)S(1)} %get-tuple-element.50), channel_id=1, source_target_pairs={{0,1},{1,0},{2,3},{3,2},{4,5},{5,4},{6,7},{7,6},{8,9},{9,8},{10,11... | collective-permute-start | bytes 1228808 | tf_op jit(solution)/shard_map/ppermute | solution.py:490
  172.6 0.8 copy-start.3
